TPU v7x, 256 devices: a whole 4x4x8 slice. The times are simulated.
256 devices in a mesh: gz: 64 (over x, z, core), gy: 4 (over y).
Axes of the slice: x: 4, y: 4, z: 8, core: 2. Of those that a mesh axis runs over, the one named last changes fastest.
Arguments:
- source_first: float32 [512, 32, 16, 128], P('gz', 'gy'), may hold values from -6 to 6
- source_second: float32 [256, 16, 16, 128], P('gz', 'gy'), may hold values from -6 to 6
- source_third: float32 [128, 8, 16, 128], P('gz', 'gy'), may hold values from -6 to 6
- source_fourth: float32 [64, 4, 16, 128], P('gz', 'gy'), may hold values from -6 to 6
- guess_first: float32 [512, 32, 16, 128], P('gz', 'gy'), may hold values from -6 to 6
- guess_second: float32 [256, 16, 16, 128], P('gz', 'gy'), may hold values from -6 to 6
- guess_third: float32 [128, 8, 16, 128], P('gz', 'gy'), may hold values from -6 to 6
- guess_fourth: float32 [64, 4, 16, 128], P('gz', 'gy'), may hold values from -6 to 6
- shift_first: float32 [512, 32, 128], P('gz', 'gy'), may hold values from 0.2 to 2
- shift_second: float32 [256, 16, 128], P('gz', 'gy'), may hold values from 0.2 to 2
- shift_third: float32 [128, 8, 128], P('gz', 'gy'), may hold values from 0.2 to 2
- shift_fourth: float32 [64, 4, 128], P('gz', 'gy'), may hold values from 0.2 to 2
- blocks_first: bfloat16 [512, 32, 2, 128, 128], P('gz', 'gy'), may hold values from -0.375 to 0.375
- blocks_second: bfloat16 [256, 16, 2, 128, 128], P('gz', 'gy'), may hold values from -0.375 to 0.375
- blocks_third: bfloat16 [128, 8, 2, 128, 128], P('gz', 'gy'), may hold values from -0.375 to 0.375
- links_first: int32 [512, 32, 2], P('gz', 'gy'), may hold values from 0 to 4095, as said below
- links_second: int32 [256, 16, 2], P('gz', 'gy'), may hold values from 0 to 1023, as said below
- links_third: int32 [128, 8, 2], P('gz', 'gy'), may hold values from 0 to 255, as said below
Outputs:
- smooth_first: float32 [512, 32, 16, 128], P('gz', 'gy')
- smooth_second: float32 [256, 16, 16, 128], P('gz', 'gy')
- smooth_third: float32 [128, 8, 16, 128], P('gz', 'gy')
- smooth_fourth: float32 [64, 4, 16, 128], P('gz', 'gy')
Inputs may be any that keep to these rules, and one draw needn't show every extreme that they name: `links_first`: entry k of fine cell (i, j) names coarse column x * 16 + y with x within one of i // 2 and y within one of j // 2, both periodic on the coarse grid. `links_second`: entry k of cell (i, j) names coarse column x * 8 + y with x within one of i // 2 and y within one of j // 2, both periodic on the coarse grid. `links_third`: entry k of cell (i, j) names coarse column x * 4 + y with x within one of i // 2 and y within one of j // 2, both periodic on the coarse grid.
All inputs are finite; a program needn't handle non-finite values.
Results may differ from a plain program's by a relative error of at most 0.0005.
Values may be sent and summed in bfloat16 or wider, within the bound.
No kernel may reach another device: no remote copies, remote signals or barrier semaphores. Data moves between devices by JAX's collectives and lax.ppermute only.
A program may use at most 256 MiB of HBM per device.

v0:
```python
import jax
import jax.numpy as jnp
from jax import lax
from jax.experimental import pallas as pl
from jax.experimental.pallas import tpu as pltpu
from jax.sharding import PartitionSpec as P

UPPER = 14.0
LOWER = UPPER / 8.0
CENTRE = (UPPER + LOWER) / 2.0
HALF = (UPPER - LOWER) / 2.0
RATIO = CENTRE / HALF
FACTOR0 = 1.0 / RATIO
FACTOR1 = 1.0 / (2.0 * RATIO - FACTOR0)
FACTOR2 = 1.0 / (2.0 * RATIO - FACTOR1)

F32 = jnp.float32
BF16 = jnp.bfloat16
R = 16
L = 128

NZ, NY = 64, 4


def swap(x, axis, partner):
    return lax.ppermute(x, axis, [(i, partner(i)) for i in range(lax.axis_size(axis))])


def z_on(x):
    return swap(x, "gz", lambda i: i ^ 1)


def z_off(x):
    return swap(x, "gz", lambda i: (((i + 1) ^ 1) - 1) % NZ)


def z_off3(x):
    return swap(x, "gz", lambda i: (i - 3 if i % 2 == 0 else i + 3) % NZ)


def y_by(x, k):
    return swap(x, "gy", lambda j: j ^ k)


def y_even(x):
    return y_by(x, 1)


def y_odd(x):
    return y_by(x, 3)


def neighbours(v, i, j, width, wrap):
    jl = (j - 1) % width if wrap else j - 1
    jr = (j + 1) % width if wrap else j + 1
    mid = v[i, j]
    beside = v[i - 1, j] + v[i + 1, j] + v[i, jl] + v[i, jr]
    beside = beside + pltpu.roll(mid, 1, 1) + pltpu.roll(mid, L - 1, 1)
    return mid, beside


def smooth(u, f, s, res, d0, d1, emit, low, rows, width, wrap):
    def columns(k):
        return range(width) if wrap else range(k, width - k)

    def first(i, carry):
        for j in columns(1):
            mid, beside = neighbours(u, i, j, width, wrap)
            r = f[i, j] - ((6.0 + s[i, j]) * mid - beside)
            res[i, j] = r
            d0[i, j] = r * (1.0 / CENTRE)
        return carry

    def second(i, carry):
        for j in columns(2):
            mid, beside = neighbours(d0, i, j, width, wrap)
            r = res[i, j] - ((6.0 + s[i, j]) * mid - beside)
            res[i, j] = r
            d1[i, j] = (FACTOR1 * FACTOR0) * mid + (2.0 * FACTOR1 / HALF) * r
        return carry

    def third(i, carry):
        for j in columns(3):
            mid, beside = neighbours(d1, i, j, width, wrap)
            r = res[i, j] - ((6.0 + s[i, j]) * mid - beside)
            d2 = (FACTOR2 * FACTOR1) * mid + (2.0 * FACTOR2 / HALF) * r
            emit(i, j, u[i, j] + d0[i, j] + mid + d2)
        return carry

    lax.fori_loop(low + 1, low + 5 + rows, first, 0)
    lax.fori_loop(low + 2, low + 4 + rows, second, 0)
    lax.fori_loop(low + 3, low + 3 + rows, third, 0)


def prolong_cell(lines, index, blocks, guess, a, b):
    total = guess[a, b]
    for k in range(2):
        ri, ci = index(a, b, k)
        total = total + lax.dot_general(
            lines[ri, ci], blocks[a, b, k], (((1,), (1,)), ((), ())), preferred_element_type=F32
        )
    return total


VMEM = pl.BlockSpec(memory_space=pltpu.VMEM)
SMEM = pl.BlockSpec(memory_space=pltpu.SMEM)


def call(kernel, inputs, specs, outs, scratch, name, flops):
    nbytes = sum(x.size * x.dtype.itemsize for x in inputs)
    return pl.pallas_call(
        kernel,
        out_shape=outs,
        in_specs=specs,
        out_specs=jax.tree.map(lambda _: VMEM, outs),
        scratch_shapes=scratch,
        name=name,
        cost_estimate=pl.CostEstimate(flops=flops, bytes_accessed=nbytes, transcendentals=0),
    )(*inputs)


def cells(rows, cols, dtype=F32):
    return pltpu.VMEM((rows, cols, R, L), dtype)


def shifts(rows, cols):
    return pltpu.VMEM((rows, cols, 1, L), F32)


def fourth_kernel(pair, a, a3, b, b3, links, blocks, guess, out, start, u, f, s, res, d0, d1, lines):
    gz, gy = lax.axis_index("gz"), lax.axis_index("gy")
    core = lax.rem(gz, 2)

    def place(ref, chip, first_bit):
        for slot in range(2):
            bit = first_bit if slot == 0 else 1 - first_bit
            row = chip * 2 + bit
            for k in range(4):
                col = lax.bitwise_xor(gy, k)
                f[row, col] = ref[slot, k, 0:16, :]
                u[row, col] = ref[slot, k, 16:32, :]
                s[row, col] = ref[slot, k, 32:33, :]

    place(pair, 2, core)
    place(a, 1 + 2 * core, 1 - core)
    place(b, 3 - 2 * core, core)
    place(a3, 4 * core, 1 - core)
    place(b3, 4 - 4 * core, core)

    def emit(i, j, value):
        lines[i - 3 - core, j] = value.astype(BF16)
        res[i, j] = value

    smooth(u, f, s, res, d0, d1, emit, core, 3, 4, True)
    out[0, 0] = res[4 + core, gy]

    def index(i, j, k):
        q = links[(i * 2 + j) * 2 + k]
        return lax.rem(q // 4 - gz + 1 + NZ, NZ), lax.rem(q, 4)

    for i in range(2):
        for j in range(2):
            start[i, j] = prolong_cell(lines, index, blocks, guess, i, j)


def third_kernel(pair, a, b, fpair, fa, fb, links, blocks, guess, out, start, u, f, s, res, d0, d1, lines):
    gz, gy = lax.axis_index("gz"), lax.axis_index("gy")
    core = lax.rem(gz, 2)

    def place(ref, fref, chip, first_bit):
        for slot in range(2):
            bit = first_bit if slot == 0 else 1 - first_bit
            for k in range(4):
                col = lax.bitwise_xor(gy, k) * 2
                for i in range(2):
                    row = chip * 4 + bit * 2 + i
                    for j in range(2):
                        at = (i * 2 + j) * R
                        u[row, col + j] = ref[slot, k, at : at + R, :]
                        f[row, col + j] = fref[slot, k, 40 + at : 40 + at + R, :]
                        s[row, col + j] = fref[slot, k, 33 + i * 2 + j : 34 + i * 2 + j, :]

    place(pair, fpair, 1, core)
    place(a, fa, 2 * core, 1 - core)
    place(b, fb, 2 - 2 * core, core)

    def emit(i, j, value):
        lines[i - 3 - 2 * core, j] = value.astype(BF16)
        res[i, j] = value

    smooth(u, f, s, res, d0, d1, emit, 2 * core, 4, 8, True)
    for i in range(2):
        for j in range(2):
            out[i, j] = res[4 + 2 * core + i, 2 * gy + j]

    def index(i, j, k):
        q = links[(i * 4 + j) * 2 + k]
        return lax.rem(q // 8 - 2 * gz + 1 + 2 * NZ, 2 * NZ), lax.rem(q, 8)

    for i in range(4):
        for j in range(4):
            start[i, j] = prolong_cell(lines, index, blocks, guess, i, j)


def second_kernel(own, on, off, fown, fon, foff, links, blocks, guess, out, start, even, odd, u, f, s, res, d0, d1, lines):
    gz, gy = lax.axis_index("gz"), lax.axis_index("gy")
    core, side = lax.rem(gz, 2), lax.rem(gy, 2)
    starts = (4, 8 - 8 * side, 8 * side)

    def place(ref, fref, row0):
        for k in range(3):
            for i in range(4):
                for j in range(4):
                    c = i * 4 + j
                    row, col = row0 + i, starts[k] + j
                    u[row, col] = ref[k, c * R : (c + 1) * R, :]
                    f[row, col] = fref[k, c * R : (c + 1) * R, :].astype(F32)
                    s[row, col] = fref[k, 256 + c : 257 + c, :].astype(F32)

    place(own, fown, 4)
    place(on, fon, 8 - 8 * core)
    place(off, foff, 8 * core)

    def emit(i, j, value):
        lines[i - 3, j - 3] = value.astype(BF16)
        res[i, j] = value

    smooth(u, f, s, res, d0, d1, emit, 0, 6, 12, False)
    for i in range(4):
        for j in range(4):
            out[i, j] = res[4 + i, 4 + j]

    def index(i, j, k):
        q = links[(i * 8 + j) * 2 + k]
        row = lax.rem(q // 16 - 4 * gz + 1 + 4 * NZ, 4 * NZ)
        return row, lax.rem(lax.rem(q, 16) - 4 * gy + 1 + 4 * NY, 4 * NY)

    def row_of_cells(i, carry):
        for j in range(8):
            start[i, j] = prolong_cell(lines, index, blocks, guess, i, j)
        return carry

    lax.fori_loop(0, 8, row_of_cells, 0)
    for i in range(8):
        for j in range(3):
            even[i, j] = start[i, 5 - 5 * side + j]
            odd[i, j] = start[i, 5 * side + j]


def first_kernel(own, even, odd, on, off, fown, feven, fodd, fon, foff, sown, seven, sodd, son, soff, out, u, f, s, res, d0, d1):
    gz, gy = lax.axis_index("gz"), lax.axis_index("gy")
    core, side = lax.rem(gz, 2), lax.rem(gy, 2)
    even_u, odd_u = 11 - 11 * side, 11 * side
    even_f, odd_f = 11 - 10 * side, 1 + 10 * side

    def own_rows(i, carry):
        for j in range(8):
            u[3 + i, 3 + j] = own[i, j]
            f[3 + i, 3 + j] = fown[i, j]
            s[3 + i, 3 + j] = sown[i, j : j + 1, :]
        for j in range(3):
            u[3 + i, even_u + j] = even[i, j]
            u[3 + i, odd_u + j] = odd[i, j]
        for j in range(2):
            f[3 + i, even_f + j] = feven[i, j].astype(F32)
            f[3 + i, odd_f + j] = fodd[i, j].astype(F32)
            s[3 + i, even_f + j] = seven[i, j : j + 1, :].astype(F32)
            s[3 + i, odd_f + j] = sodd[i, j : j + 1, :].astype(F32)
        return carry

    lax.fori_loop(0, 8, own_rows, 0)

    def place(ref, fref, sref, row_u, row_f):
        for i in range(3):
            for j in range(8):
                u[row_u + i, 3 + j] = ref[i, j]
            for j in range(3):
                u[row_u + i, even_u + j] = ref[i, 8 + j]
                u[row_u + i, odd_u + j] = ref[i, 11 + j]
        for i in range(2):
            for j in range(8):
                f[row_f + i, 3 + j] = fref[i, j].astype(F32)
                s[row_f + i, 3 + j] = sref[i, j : j + 1, :].astype(F32)
            for j in range(2):
                f[row_f + i, even_f + j] = fref[i, 8 + j].astype(F32)
                f[row_f + i, odd_f + j] = fref[i, 10 + j].astype(F32)
                s[row_f + i, even_f + j] = sref[i, 8 + j : 9 + j, :].astype(F32)
                s[row_f + i, odd_f + j] = sref[i, 10 + j : 11 + j, :].astype(F32)

    place(on, fon, son, 11 - 11 * core, 11 - 10 * core)
    place(off, foff, soff, 11 * core, 1 + 10 * core)

    def emit(i, j, value):
        out[i - 3, j - 3] = value

    smooth(u, f, s, res, d0, d1, emit, 0, 8, 14, False)


def strip(x, dim, at, width):
    return lax.dynamic_slice_in_dim(x, at, width, dim)


def sds(*shape, dtype=F32):
    return jax.ShapeDtypeStruct(shape, dtype)


def flat(x):
    return x.reshape(-1, L)


def shards(
    source_first, source_second, source_third, source_fourth,
    guess_first, guess_second, guess_third, guess_fourth,
    shift_first, shift_second, shift_third, shift_fourth,
    blocks_first, blocks_second, blocks_third,
    links_first, links_second, links_third,
):
    core = lax.axis_index("gz") % 2
    side = lax.axis_index("gy") % 2

    pack = jnp.concatenate(
        [flat(source_fourth), flat(guess_fourth), flat(shift_fourth), flat(shift_third), jnp.zeros((3, L), F32), flat(source_third)]
    )
    line = jnp.stack([pack, y_by(pack, 1), y_by(pack, 2), y_by(pack, 3)])
    pair = jnp.stack([line, z_on(line)])
    far = z_off3(pair[:, :, :40])
    near = z_off(pair)
    near_b, far_b = z_on(near), z_on(far)

    second = jnp.concatenate([flat(source_second), flat(shift_second)])
    f_even = strip(source_first, 1, 6 - 6 * side, 2)
    f_odd = strip(source_first, 1, 6 * side, 2)
    s_even = strip(shift_first, 1, 6 - 6 * side, 2)
    s_odd = strip(shift_first, 1, 6 * side, 2)
    ahead_even = y_even(jnp.concatenate([second, flat(f_even), flat(s_even)]))
    ahead_odd = y_odd(jnp.concatenate([second, flat(f_odd), flat(s_odd)]))
    second_even, second_odd = ahead_even[:272], ahead_odd[:272]
    f_even, f_odd = (x[272:528].reshape(8, 2, R, L) for x in (ahead_even, ahead_odd))
    s_even, s_odd = (x[528:544].reshape(8, 2, L) for x in (ahead_even, ahead_odd))
    second3 = jnp.stack([second, second_even, second_odd])

    def across(at):
        f = jnp.concatenate([strip(x, 0, at, 2) for x in (source_first, f_even, f_odd)], axis=1)
        s = jnp.concatenate([strip(x, 0, at, 2) for x in (shift_first, s_even, s_odd)], axis=1)
        return jnp.concatenate([flat(second3), flat(f), flat(s)])

    ahead_on = z_on(across(6 - 6 * core))
    ahead_off = z_off(across(6 * core))
    second_on, second_off = (x[:816].reshape(3, 272, L) for x in (ahead_on, ahead_off))
    f_on, f_off = (x[816:1200].reshape(2, 12, R, L) for x in (ahead_on, ahead_off))
    s_on, s_off = (x[1200:1224].reshape(2, 12, L) for x in (ahead_on, ahead_off))

    def smoothing_scratch(rows, cols):
        return [cells(rows, cols), cells(rows, cols), shifts(rows, cols)] + [cells(rows, cols)] * 3

    out_fourth, start_third = call(
        fourth_kernel,
        (pair, near, far, near_b, far_b, links_third.reshape(-1), blocks_third, guess_third),
        [VMEM] * 5 + [SMEM] + [VMEM] * 2,
        (sds(1, 1, R, L), sds(2, 2, R, L)),
        smoothing_scratch(10, 4) + [cells(3, 4, BF16)],
        "fourth", 4_000_000,
    )

    mine = flat(start_third)
    line3 = jnp.stack([mine, y_by(mine, 1), y_by(mine, 2), y_by(mine, 3)])
    pair3 = jnp.stack([line3, z_on(line3)])
    near3 = z_off(pair3)
    near3_b = z_on(near3)
    out_third, start_second = call(
        third_kernel,
        (pair3, near3, near3_b, pair, near, near_b, links_second.reshape(-1), blocks_second, guess_second),
        [VMEM] * 6 + [SMEM] + [VMEM] * 2,
        (sds(2, 2, R, L), sds(4, 4, R, L)),
        smoothing_scratch(12, 8) + [cells(4, 8, BF16)],
        "third", 8_000_000,
    )

    mine = flat(start_second)
    own2 = jnp.stack([mine, y_even(mine), y_odd(mine)])
    out_second, start_first, strip_even, strip_odd = call(
        second_kernel,
        (own2, z_on(own2), z_off(own2), second3, second_on, second_off, links_first.reshape(-1), blocks_first, guess_first),
        [VMEM] * 6 + [SMEM] + [VMEM] * 2,
        (sds(4, 4, R, L), sds(8, 8, R, L), sds(8, 3, R, L), sds(8, 3, R, L)),
        smoothing_scratch(12, 12) + [cells(6, 6, BF16)],
        "second", 16_000_000,
    )

    u_even, u_odd = y_even(strip_even), y_odd(strip_odd)

    def rows_of(at):
        return jnp.concatenate([strip(x, 0, at, 3) for x in (start_first, u_even, u_odd)], axis=1)

    u_on = z_on(rows_of(5 - 5 * core))
    u_off = z_off(rows_of(5 * core))
    (out_first,) = call(
        first_kernel,
        (start_first, u_even, u_odd, u_on, u_off, source_first, f_even, f_odd, f_on, f_off, shift_first, s_even, s_odd, s_on, s_off),
        [VMEM] * 15,
        (sds(8, 8, R, L),),
        smoothing_scratch(14, 14),
        "first", 16_000_000,
    )
    return out_first, out_second, out_third, out_fourth


def solution(mesh):
    field = P("gz", "gy", None, None)
    line = P("gz", "gy", None)
    block = P("gz", "gy", None, None, None)
    return jax.shard_map(
        shards,
        mesh=mesh,
        in_specs=(field,) * 8 + (line,) * 4 + (block,) * 3 + (line,) * 3,
        out_specs=(field,) * 4,
        check_vma=False,
    )
```

profile of v0, /device:TPU:1, one launch (start us, length us, event | category | flops | bytes accessed | tf_op | source)
XLA Modules:
  0.0 124.6 jit_solution(11446803892315123089)
XLA Ops:
  0.7 2.9 %concatenate.38 = f32[104,128]{1,0:T(8,128)S(1)} concatenate(f32[16,128]{1,0:T(8,128)} %bitcast.90, f32[16,128]{1,0:T(8,128)} %bitcast.91, f32[1,128]{1,0:T(1,128)} %bitcast.93, f32[4,128]{1,0:T(4,128)} %bitcast.92, f32[3,128]{1,0:T(4,128)S(1)} %broadcast_in_dim.3, f32[64,128]{1,0:T(8,128)} %bitcast.89), dimensions={0} | concatenate | bytes 106496 | tf_op jit(solution)/shard_map/concatenate | solution.py:321
  3.6 3.6 %collective-permute-start.2 = (f32[104,128]{1,0:T(8,128)S(1)}, f32[104,128]{1,0:T(8,128)S(1)}, u32[]{:S(2)}, u32[]{:S(2)}) collective-permute-start(f32[104,128]{1,0:T(8,128)S(1)} %concatenate.38), channel_id=1, source_target_pairs={{0,3},{1,2},{2,1},{3,0},{4,7},{5,6},{6,5},{7,4},{8,11},{9,10},{10,... | collective-permute-start | bytes 159752 | tf_op jit(solution)/shard_map/ppermute | solution.py:26
  7.7 0.9 collective-permute-done.2
  8.7 3.1 %collective-permute-done.1 = f32[104,128]{1,0:T(8,128)S(1)} collective-permute-done((f32[104,128]{1,0:T(8,128)S(1)}, f32[104,128]{1,0:T(8,128)S(1)}, u32[]{:S(2)}, u32[]{:S(2)}) %collective-permute-start.1) | collective-permute-done | bytes 53280 | tf_op jit(solution)/shard_map/ppermute | solution.py:26
  11.8 2.1 %collective-permute-start.3 = (f32[4,104,128]{2,1,0:T(8,128)S(1)}, f32[4,104,128]{2,1,0:T(8,128)S(1)}, u32[]{:S(2)}, u32[]{:S(2)}) collective-permute-start(f32[4,104,128]{2,1,0:T(8,128)S(1)} %get-tuple-element.29), channel_id=1, source_target_pairs={{0,4},{4,0},{8,12},{12,8},{16,20},{20,16},{24,28},{28,24},{32,36},... | collective-permute-start | bytes 638984 | tf_op jit(solution)/shard_map/ppermute | solution.py:26
  13.9 1.0 constant_dynamic-slice_fusion.21
  15.0 2.0 %collective-permute-start.4 = (f32[2,4,104,128]{3,2,1,0:T(8,128)S(1)}, f32[2,4,104,128]{3,2,1,0:T(8,128)S(1)}, u32[]{:S(2)}, u32[]{:S(2)}) collective-permute-start(f32[2,4,104,128]{3,2,1,0:T(8,128)S(1)} %pad_maximum_fusion.2.pair.fpair), channel_id=1, source_target_pairs={{0,252},{4,8},{8,4},{12,16},{16,12},{20,24},{24,20},{28,32},{32,28... | collective-permute-start | bytes 1277960 | tf_op jit(solution)/shard_map/ppermute | solution.py:26
  17.0 0.8 constant_dynamic-slice_fusion.20
  17.8 1.7 %pad_maximum_fusion.7 = (f32[544,128]{1,0:T(8,128)}, f32[544,128]{1,0:T(8,128)S(1)}) fusion(f32[16,128]{1,0:T(8,128)S(1)} %bitcast.80, f32[256,128]{1,0:T(8,128)S(1)} %bitcast.62, f32[16,128]{1,0:T(8,128)} %bitcast.78, f32[256,128]{1,0:T(8,128)} %bitcast.60, f32[16,128]{1,0:T(8,128)S(1)} %bitcast.81, f32[256,128]{1,0:T(8,128)S(1)} %bitcast.63), kind=kLoop, calls=%fused_computation.11 | loop fusion | flops 348160 | bytes 974848 | tf_op jit(solution)/shard_map/concatenate | solution.py:335
  19.5 2.0 %collective-permute-start.19 = (f32[544,128]{1,0:T(8,128)S(1)}, f32[544,128]{1,0:T(8,128)S(1)}, u32[]{:S(2)}, u32[]{:S(2)}) collective-permute-start(f32[544,128]{1,0:T(8,128)S(1)} %get-tuple-element.35), channel_id=1, source_target_pairs={{0,3},{1,2},{2,1},{3,0},{4,7},{5,6},{6,5},{7,4},{8,11},{9,10},{10,... | collective-permute-start | bytes 835592 | tf_op jit(solution)/shard_map/ppermute | solution.py:26
  21.5 0.9 maximum_bitcast_fusion
  22.5 2.0 %collective-permute-start.5 = (f32[2,4,40,128]{3,2,1,0:T(8,128)S(1)}, f32[2,4,40,128]{3,2,1,0:T(8,128)}, u32[]{:S(2)}, u32[]{:S(2)}) collective-permute-start(f32[2,4,40,128]{3,2,1,0:T(8,128)S(1)} %fusion.4), channel_id=1, source_target_pairs={{0,244},{4,16},{8,252},{12,24},{16,4},{20,32},{24,12},{28,40},{32,... | collective-permute-start | bytes 491528 | tf_op jit(solution)/shard_map/ppermute | solution.py:26
  24.5 5.8 %collective-permute-start.6 = (f32[2,4,104,128]{3,2,1,0:T(8,128)S(1)}, f32[2,4,104,128]{3,2,1,0:T(8,128)S(1)}, u32[]{:S(2)}, u32[]{:S(2)}) collective-permute-start(f32[2,4,104,128]{3,2,1,0:T(8,128)S(1)} %collective-permute-done.4.a.fa), channel_id=1, source_target_pairs={{0,4},{4,0},{8,12},{12,8},{16,20},{20,16},{24,28},{28,24},{32,36},... | collective-permute-start | bytes 1277960 | tf_op jit(solution)/shard_map/ppermute | solution.py:26
  30.3 1.3 %constant_dynamic-slice_fusion.8 = (f32[2,8,128]{2,1,0:T(8,128)}, f32[2,8,128]{2,1,0:T(8,128)}) fusion(f32[8,8,128]{2,1,0:T(8,128)} %sown.1, s32[]{:T(128)S(6)} %select_n.50, s32[]{:T(128)S(6)} %select_n.49), kind=kLoop, calls=%fused_computation.34 | loop fusion | bytes 32776 | tf_op jit(solution)/shard_map/dynamic_slice | solution.py:300
  31.6 1.3 %reshape.107.links = s32[8]{0:T(128)} reshape(s32[2,2,2]{2,1,0:T(2,128)} %param.35) | data formatting | bytes 64 | tf_op jit(solution)/shard_map/reshape | solution.py:358
  32.9 0.8 copy.24
  34.4 4.6 %collective-permute-start.7 = (f32[2,4,40,128]{3,2,1,0:T(8,128)}, f32[2,4,40,128]{3,2,1,0:T(8,128)S(1)}, u32[]{:S(2)}, u32[]{:S(2)}) collective-permute-start(f32[2,4,40,128]{3,2,1,0:T(8,128)} %collective-permute-done.5.a3), channel_id=1, source_target_pairs={{0,4},{4,0},{8,12},{12,8},{16,20},{20,16},{24,28},{28,24},{32,36},... | collective-permute-start | bytes 491528 | tf_op jit(solution)/shard_map/ppermute | solution.py:26
  39.1 1.2 collective-permute-done.7.b3
  41.0 0.8 copy-done.4
  41.7 3.7 %fourth.1 = (f32[1,1,16,128]{3,2,1,0:T(8,128)}, f32[2,2,16,128]{3,2,1,0:T(8,128)}) custom-call(f32[2,4,104,128]{3,2,1,0:T(8,128)} %copy-done, f32[2,4,104,128]{3,2,1,0:T(8,128)} %copy-done.3, f32[2,4,40,128]{3,2,1,0:T(8,128)} %collective-permute-done.5.a3, f32[2,4,104,128]{3,2,1,0:T(8,128)} %copy-done.4, f32[2,4,40,128]{3,2,1,0:T(8,128)} %copy-done.15, ...), custom_call_target="tpu_custom_call" | custom-call | flops 4000000 | bytes 1900576 | tf_op jit(solution)/shard_map/fourth/pallas_call | solution.py:111
  46.1 1.0 collective-permute-start.9
  47.1 1.6 %collective-permute-start.8 = (f32[64,128]{1,0:T(8,128)}, f32[64,128]{1,0:T(8,128)S(1)}, u32[]{:S(2)}, u32[]{:S(2)}) collective-permute-start(f32[64,128]{1,0:T(8,128)} %bitcast.84), channel_id=1, source_target_pairs={{0,1},{1,0},{2,3},{3,2},{4,5},{5,4},{6,7},{7,6},{8,9},{9,8},{10,11... | collective-permute-start | bytes 98312 | tf_op jit(solution)/shard_map/ppermute | solution.py:26
  48.8 0.9 collective-permute-done.10
  49.6 1.1 collective-permute-done.9
  50.9 0.8 fusion.5
  51.6 1.7 %collective-permute-start.11 = (f32[4,64,128]{2,1,0:T(8,128)S(1)}, f32[4,64,128]{2,1,0:T(8,128)S(1)}, u32[]{:S(2)}, u32[]{:S(2)}) collective-permute-start(f32[4,64,128]{2,1,0:T(8,128)S(1)} %get-tuple-element.41), channel_id=1, source_target_pairs={{0,4},{4,0},{8,12},{12,8},{16,20},{20,16},{24,28},{28,24},{32,36},... | collective-permute-start | bytes 393224 | tf_op jit(solution)/shard_map/ppermute | solution.py:26
  53.4 1.0 collective-permute-done.11
  55.2 5.1 %collective-permute-done.12.a = f32[2,4,64,128]{3,2,1,0:T(8,128)S(1)} collective-permute-done((f32[2,4,64,128]{3,2,1,0:T(8,128)S(1)}, f32[2,4,64,128]{3,2,1,0:T(8,128)S(1)}, u32[]{:S(2)}, u32[]{:S(2)}) %collective-permute-start.12) | collective-permute-done | bytes 262176 | tf_op jit(solution)/shard_map/ppermute | solution.py:26
  60.3 3.7 %collective-permute-start.13 = (f32[2,4,64,128]{3,2,1,0:T(8,128)S(1)}, f32[2,4,64,128]{3,2,1,0:T(8,128)S(1)}, u32[]{:S(2)}, u32[]{:S(2)}) collective-permute-start(f32[2,4,64,128]{3,2,1,0:T(8,128)S(1)} %collective-permute-done.12.a), channel_id=1, source_target_pairs={{0,4},{4,0},{8,12},{12,8},{16,20},{20,16},{24,28},{28,24},{32,36},... | collective-permute-start | bytes 786440 | tf_op jit(solution)/shard_map/ppermute | solution.py:26
  64.0 1.1 collective-permute-done.13.b
  65.8 5.3 %third.1 = (f32[2,2,16,128]{3,2,1,0:T(8,128)}, f32[4,4,16,128]{3,2,1,0:T(8,128)}) custom-call(f32[2,4,64,128]{3,2,1,0:T(8,128)} %copy-done.6, f32[2,4,64,128]{3,2,1,0:T(8,128)} %copy-done.13, f32[2,4,64,128]{3,2,1,0:T(8,128)} %copy-done.14, f32[2,4,104,128]{3,2,1,0:T(8,128)} %copy-done, f32[2,4,104,128]{3,2,1,0:T(8,128)} %copy-done.3, ...), custom_call_target="tpu_custom_call" | custom-call | flops 8000000 | bytes 3244160 | tf_op jit(solution)/shard_map/third/pallas_call | solution.py:111
  71.1 2.0 %collective-permute-start.15 = (f32[256,128]{1,0:T(8,128)}, f32[256,128]{1,0:T(8,128)S(1)}, u32[]{:S(2)}, u32[]{:S(2)}) collective-permute-start(f32[256,128]{1,0:T(8,128)} %bitcast.65), channel_id=1, source_target_pairs={{0,3},{1,2},{2,1},{3,0},{4,7},{5,6},{6,5},{7,4},{8,11},{9,10},{10,... | collective-permute-start | bytes 393224 | tf_op jit(solution)/shard_map/ppermute | solution.py:26
  74.2 3.1 %collective-permute-done.15 = f32[256,128]{1,0:T(8,128)S(1)} collective-permute-done((f32[256,128]{1,0:T(8,128)}, f32[256,128]{1,0:T(8,128)S(1)}, u32[]{:S(2)}, u32[]{:S(2)}) %collective-permute-start.15) | collective-permute-done | bytes 131104 | tf_op jit(solution)/shard_map/ppermute | solution.py:26
  77.7 0.9 pad_maximum_fusion.4.own
  78.7 1.6 %collective-permute-start.16 = (f32[3,256,128]{2,1,0:T(8,128)S(1)}, f32[3,256,128]{2,1,0:T(8,128)}, u32[]{:S(2)}, u32[]{:S(2)}) collective-permute-start(f32[3,256,128]{2,1,0:T(8,128)S(1)} %pad_maximum_fusion.4.own), channel_id=1, source_target_pairs={{0,4},{4,0},{8,12},{12,8},{16,20},{20,16},{24,28},{28,24},{32,36},... | collective-permute-start | bytes 1179656 | tf_op jit(solution)/shard_map/ppermute | solution.py:26
  81.1 2.3 %collective-permute-done.21 = f32[1224,128]{1,0:T(8,128)S(1)} collective-permute-done((f32[1224,128]{1,0:T(8,128)S(1)}, f32[1224,128]{1,0:T(8,128)S(1)}, u32[]{:S(2)}, u32[]{:S(2)}) %collective-permute-start.21) | collective-permute-done | bytes 626720 | tf_op jit(solution)/shard_map/ppermute | solution.py:26
  83.4 0.8 slice.61
  84.2 0.8 slice.60
  85.0 2.7 %collective-permute-done.17.off = f32[3,256,128]{2,1,0:T(8,128)} collective-permute-done((f32[3,256,128]{2,1,0:T(8,128)S(1)}, f32[3,256,128]{2,1,0:T(8,128)}, u32[]{:S(2)}, u32[]{:S(2)}) %collective-permute-start.17) | collective-permute-done | bytes 393248 | tf_op jit(solution)/shard_map/ppermute | solution.py:26
  87.8 9.8 %second.1 = (f32[4,4,16,128]{3,2,1,0:T(8,128)}, f32[8,8,16,128]{3,2,1,0:T(8,128)}, f32[8,3,16,128]{3,2,1,0:T(8,128)}, f32[8,3,16,128]{3,2,1,0:T(8,128)}) custom-call(f32[3,256,128]{2,1,0:T(8,128)} %copy-done.5, f32[3,256,128]{2,1,0:T(8,128)} %collective-permute-done.16.on, f32[3,256,128]{2,1,0:T(8,128)} %collective-permute-done.17.off, ...), custom_call_target="tpu_custom_call" | custom-call | flops 16000000 | bytes 7152128 | tf_op jit(solution)/shard_map/second/pallas_call | solution.py:111
  97.6 1.5 %collective-permute-start.22 = (f32[8,3,16,128]{3,2,1,0:T(8,128)}, f32[8,3,16,128]{3,2,1,0:T(8,128)S(1)}, u32[]{:S(2)}, u32[]{:S(2)}) collective-permute-start(f32[8,3,16,128]{3,2,1,0:T(8,128)} %get-tuple-element.15), channel_id=1, source_target_pairs={{0,1},{1,0},{2,3},{3,2},{4,5},{5,4},{6,7},{7,6},{8,9},{9,8},{10,11... | collective-permute-start | bytes 589832 | tf_op jit(solution)/shard_map/ppermute | solution.py:26
  99.0 0.8 collective-permute-start.23
  99.8 1.0 constant_dynamic-slice_fusion.2
  100.8 1.5 %collective-permute-done.22.even = f32[8,3,16,128]{3,2,1,0:T(8,128)S(1)} collective-permute-done((f32[8,3,16,128]{3,2,1,0:T(8,128)}, f32[8,3,16,128]{3,2,1,0:T(8,128)S(1)}, u32[]{:S(2)}, u32[]{:S(2)}) %collective-permute-start.22) | collective-permute-done | bytes 196640 | tf_op jit(solution)/shard_map/ppermute | solution.py:26
  102.3 2.7 %collective-permute-done.23.odd = f32[8,3,16,128]{3,2,1,0:T(8,128)S(1)} collective-permute-done((f32[8,3,16,128]{3,2,1,0:T(8,128)}, f32[8,3,16,128]{3,2,1,0:T(8,128)S(1)}, u32[]{:S(2)}, u32[]{:S(2)}) %collective-permute-start.23) | collective-permute-done | bytes 196640 | tf_op jit(solution)/shard_map/ppermute | solution.py:26
  105.0 5.5 %collective-permute-start.24 = (f32[3,14,16,128]{3,2,1,0:T(8,128)S(1)}, f32[3,14,16,128]{3,2,1,0:T(8,128)S(1)}, u32[]{:S(2)}, u32[]{:S(2)}) collective-permute-start(f32[3,14,16,128]{3,2,1,0:T(8,128)S(1)} %pad_maximum_fusion.5), channel_id=1, source_target_pairs={{0,4},{4,0},{8,12},{12,8},{16,20},{20,16},{24,28},{28,24},{32,36},... | collective-permute-start | bytes 1032200 | tf_op jit(solution)/shard_map/ppermute | solution.py:26
  113.2 4.3 %collective-permute-done.25.off = f32[3,14,16,128]{3,2,1,0:T(8,128)S(1)} collective-permute-done((f32[3,14,16,128]{3,2,1,0:T(8,128)S(1)}, f32[3,14,16,128]{3,2,1,0:T(8,128)S(1)}, u32[]{:S(2)}, u32[]{:S(2)}) %collective-permute-start.25) | collective-permute-done | bytes 344096 | tf_op jit(solution)/shard_map/ppermute | solution.py:26
  118.3 6.3 %first.1 = f32[8,8,16,128]{3,2,1,0:T(8,128)} custom-call(f32[8,8,16,128]{3,2,1,0:T(8,128)} %get-tuple-element.14.own, f32[8,3,16,128]{3,2,1,0:T(8,128)} %copy-done.9, f32[8,3,16,128]{3,2,1,0:T(8,128)} %copy-done.10, f32[3,14,16,128]{3,2,1,0:T(8,128)} %copy-done.11, f32[3,14,16,128]{3,2,1,0:T(8,128)} %copy-done.12, f32[8,8,16,128]{3,2,1,0:T(8,128)} %fown.1, ...), custom_call_target="tpu_custom_call" | custom-call | flops 16000000 | bytes 2859008 | tf_op jit(solution)/shard_map/first/pallas_call | solution.py:111
  (96 shorter events, 10.6 us)
Async XLA Ops:
  0.6 33.7 %copy-start.2 = (f32[8,8,16,128]{3,2,1,0:T(8,128)S(1)}, f32[8,8,16,128]{3,2,1,0:T(8,128)}, u32[]{:S(2)}) copy-start(f32[8,8,16,128]{3,2,1,0:T(8,128)} %fown.1) | copy-start | bytes 1572868
  3.6 5.1 %collective-permute-start.2 = (f32[104,128]{1,0:T(8,128)S(1)}, f32[104,128]{1,0:T(8,128)S(1)}, u32[]{:S(2)}, u32[]{:S(2)}) collective-permute-start(f32[104,128]{1,0:T(8,128)S(1)} %concatenate.38), channel_id=1, source_target_pairs={{0,3},{1,2},{2,1},{3,0},{4,7},{5,6},{6,5},{7,4},{8,11},{9,10},{10,... | collective-permute-start | bytes 159752 | tf_op jit(solution)/shard_map/ppermute | solution.py:26
  7.1 4.6 %collective-permute-start.1 = (f32[104,128]{1,0:T(8,128)S(1)}, f32[104,128]{1,0:T(8,128)S(1)}, u32[]{:S(2)}, u32[]{:S(2)}) collective-permute-start(f32[104,128]{1,0:T(8,128)S(1)} %concatenate.38), channel_id=1, source_target_pairs={{0,2},{1,3},{2,0},{3,1},{4,6},{5,7},{6,4},{7,5},{8,10},{9,11},{10,... | collective-permute-start | bytes 159752 | tf_op jit(solution)/shard_map/ppermute | solution.py:26
  7.5 4.2 %collective-permute-start = (f32[104,128]{1,0:T(8,128)S(1)}, f32[104,128]{1,0:T(8,128)S(1)}, u32[]{:S(2)}, u32[]{:S(2)}) collective-permute-start(f32[104,128]{1,0:T(8,128)S(1)} %concatenate.38), channel_id=1, source_target_pairs={{0,1},{1,0},{2,3},{3,2},{4,5},{5,4},{6,7},{7,6},{8,9},{9,8},{10,11... | collective-permute-start | bytes 159752 | tf_op jit(solution)/shard_map/ppermute | solution.py:26
  11.8 3.2 %collective-permute-start.3 = (f32[4,104,128]{2,1,0:T(8,128)S(1)}, f32[4,104,128]{2,1,0:T(8,128)S(1)}, u32[]{:S(2)}, u32[]{:S(2)}) collective-permute-start(f32[4,104,128]{2,1,0:T(8,128)S(1)} %get-tuple-element.29), channel_id=1, source_target_pairs={{0,4},{4,0},{8,12},{12,8},{16,20},{20,16},{24,28},{28,24},{32,36},... | collective-permute-start | bytes 638984 | tf_op jit(solution)/shard_map/ppermute | solution.py:26
  15.0 25.3 %copy-start = (f32[2,4,104,128]{3,2,1,0:T(8,128)}, f32[2,4,104,128]{3,2,1,0:T(8,128)S(1)}, u32[]{:S(2)}) copy-start(f32[2,4,104,128]{3,2,1,0:T(8,128)S(1)} %pad_maximum_fusion.2.pair.fpair) | copy-start | bytes 1277956
  15.0 9.5 %collective-permute-start.4 = (f32[2,4,104,128]{3,2,1,0:T(8,128)S(1)}, f32[2,4,104,128]{3,2,1,0:T(8,128)S(1)}, u32[]{:S(2)}, u32[]{:S(2)}) collective-permute-start(f32[2,4,104,128]{3,2,1,0:T(8,128)S(1)} %pad_maximum_fusion.2.pair.fpair), channel_id=1, source_target_pairs={{0,252},{4,8},{8,4},{12,16},{16,12},{20,24},{24,20},{28,32},{32,28... | collective-permute-start | bytes 1277960 | tf_op jit(solution)/shard_map/ppermute | solution.py:26
  19.5 14.9 %collective-permute-start.18 = (f32[544,128]{1,0:T(8,128)}, f32[544,128]{1,0:T(8,128)S(1)}, u32[]{:S(2)}, u32[]{:S(2)}) collective-permute-start(f32[544,128]{1,0:T(8,128)} %get-tuple-element.34), channel_id=1, source_target_pairs={{0,1},{1,0},{2,3},{3,2},{4,5},{5,4},{6,7},{7,6},{8,9},{9,8},{10,11... | collective-permute-start | bytes 835592 | tf_op jit(solution)/shard_map/ppermute | solution.py:26
  19.5 14.9 %collective-permute-start.19 = (f32[544,128]{1,0:T(8,128)S(1)}, f32[544,128]{1,0:T(8,128)S(1)}, u32[]{:S(2)}, u32[]{:S(2)}) collective-permute-start(f32[544,128]{1,0:T(8,128)S(1)} %get-tuple-element.35), channel_id=1, source_target_pairs={{0,3},{1,2},{2,1},{3,0},{4,7},{5,6},{6,5},{7,4},{8,11},{9,10},{10,... | collective-permute-start | bytes 835592 | tf_op jit(solution)/shard_map/ppermute | solution.py:26
  22.5 12.0 %collective-permute-start.5 = (f32[2,4,40,128]{3,2,1,0:T(8,128)S(1)}, f32[2,4,40,128]{3,2,1,0:T(8,128)}, u32[]{:S(2)}, u32[]{:S(2)}) collective-permute-start(f32[2,4,40,128]{3,2,1,0:T(8,128)S(1)} %fusion.4), channel_id=1, source_target_pairs={{0,244},{4,16},{8,252},{12,24},{16,4},{20,32},{24,12},{28,40},{32,... | collective-permute-start | bytes 491528 | tf_op jit(solution)/shard_map/ppermute | solution.py:26
  24.5 15.8 %copy-start.3 = (f32[2,4,104,128]{3,2,1,0:T(8,128)}, f32[2,4,104,128]{3,2,1,0:T(8,128)S(1)}, u32[]{:S(2)}) copy-start(f32[2,4,104,128]{3,2,1,0:T(8,128)S(1)} %collective-permute-done.4.a.fa) | copy-start | bytes 1277956
  24.5 15.8 %collective-permute-start.6 = (f32[2,4,104,128]{3,2,1,0:T(8,128)S(1)}, f32[2,4,104,128]{3,2,1,0:T(8,128)S(1)}, u32[]{:S(2)}, u32[]{:S(2)}) collective-permute-start(f32[2,4,104,128]{3,2,1,0:T(8,128)S(1)} %collective-permute-done.4.a.fa), channel_id=1, source_target_pairs={{0,4},{4,0},{8,12},{12,8},{16,20},{20,16},{24,28},{28,24},{32,36},... | collective-permute-start | bytes 1277960 | tf_op jit(solution)/shard_map/ppermute | solution.py:26
  34.4 36.7 %copy-start.7 = (f32[256,128]{1,0:T(8,128)}, f32[256,128]{1,0:T(8,128)S(1)}, u32[]{:S(2)}) copy-start(f32[256,128]{1,0:T(8,128)S(1)} %slice.56) | copy-start | bytes 393220
  34.4 29.6 %copy-start.18 = (f32[2,8,128]{2,1,0:T(8,128)S(1)}, f32[2,8,128]{2,1,0:T(8,128)}, u32[]{:S(2)}) copy-start(f32[2,8,128]{2,1,0:T(8,128)} %get-tuple-element.43) | copy-start | bytes 24580
  34.4 36.6 %copy-start.8 = (f32[256,128]{1,0:T(8,128)}, f32[256,128]{1,0:T(8,128)S(1)}, u32[]{:S(2)}) copy-start(f32[256,128]{1,0:T(8,128)S(1)} %slice.57) | copy-start | bytes 393220
  34.4 5.8 %collective-permute-start.7 = (f32[2,4,40,128]{3,2,1,0:T(8,128)}, f32[2,4,40,128]{3,2,1,0:T(8,128)S(1)}, u32[]{:S(2)}, u32[]{:S(2)}) collective-permute-start(f32[2,4,40,128]{3,2,1,0:T(8,128)} %collective-permute-done.5.a3), channel_id=1, source_target_pairs={{0,4},{4,0},{8,12},{12,8},{16,20},{20,16},{24,28},{28,24},{32,36},... | collective-permute-start | bytes 491528 | tf_op jit(solution)/shard_map/ppermute | solution.py:26
  40.3 0.7 copy-start.15
  41.0 0.8 copy-start.4
  45.5 4.2 %collective-permute-start.10 = (f32[64,128]{1,0:T(8,128)}, f32[64,128]{1,0:T(8,128)S(1)}, u32[]{:S(2)}, u32[]{:S(2)}) collective-permute-start(f32[64,128]{1,0:T(8,128)} %bitcast.82), channel_id=1, source_target_pairs={{0,3},{1,2},{2,1},{3,0},{4,7},{5,6},{6,5},{7,4},{8,11},{9,10},{10,... | collective-permute-start | bytes 98312 | tf_op jit(solution)/shard_map/ppermute | solution.py:26
  46.1 4.6 %collective-permute-start.9 = (f32[64,128]{1,0:T(8,128)}, f32[64,128]{1,0:T(8,128)S(1)}, u32[]{:S(2)}, u32[]{:S(2)}) collective-permute-start(f32[64,128]{1,0:T(8,128)} %bitcast.83), channel_id=1, source_target_pairs={{0,2},{1,3},{2,0},{3,1},{4,6},{5,7},{6,4},{7,5},{8,10},{9,11},{10,... | collective-permute-start | bytes 98312 | tf_op jit(solution)/shard_map/ppermute | solution.py:26
  47.1 3.8 %collective-permute-start.8 = (f32[64,128]{1,0:T(8,128)}, f32[64,128]{1,0:T(8,128)S(1)}, u32[]{:S(2)}, u32[]{:S(2)}) collective-permute-start(f32[64,128]{1,0:T(8,128)} %bitcast.84), channel_id=1, source_target_pairs={{0,1},{1,0},{2,3},{3,2},{4,5},{5,4},{6,7},{7,6},{8,9},{9,8},{10,11... | collective-permute-start | bytes 98312 | tf_op jit(solution)/shard_map/ppermute | solution.py:26
  48.7 29.9 %copy-start.16 = (f32[16,128]{1,0:T(8,128)}, f32[16,128]{1,0:T(8,128)S(1)}, u32[]{:S(2)}) copy-start(f32[16,128]{1,0:T(8,128)S(1)} %slice.58) | copy-start | bytes 24580
  48.8 29.9 %copy-start.17 = (f32[16,128]{1,0:T(8,128)}, f32[16,128]{1,0:T(8,128)S(1)}, u32[]{:S(2)}) copy-start(f32[16,128]{1,0:T(8,128)S(1)} %slice.59) | copy-start | bytes 24580
  51.6 2.7 %collective-permute-start.11 = (f32[4,64,128]{2,1,0:T(8,128)S(1)}, f32[4,64,128]{2,1,0:T(8,128)S(1)}, u32[]{:S(2)}, u32[]{:S(2)}) collective-permute-start(f32[4,64,128]{2,1,0:T(8,128)S(1)} %get-tuple-element.41), channel_id=1, source_target_pairs={{0,4},{4,0},{8,12},{12,8},{16,20},{20,16},{24,28},{28,24},{32,36},... | collective-permute-start | bytes 393224 | tf_op jit(solution)/shard_map/ppermute | solution.py:26
  53.4 27.0 %copy-start.19 = (s32[8,8,2]{1,2,0:T(2,128)S(1)}, s32[8,8,2]{1,2,0:T(2,128)}, u32[]{:S(2)}) copy-start(s32[8,8,2]{1,2,0:T(2,128)} %param.33) | copy-start | bytes 1540
  54.4 10.7 %copy-start.6 = (f32[2,4,64,128]{3,2,1,0:T(8,128)}, f32[2,4,64,128]{3,2,1,0:T(8,128)S(1)}, u32[]{:S(2)}) copy-start(f32[2,4,64,128]{3,2,1,0:T(8,128)S(1)} %pad_maximum_fusion.9.pair) | copy-start | bytes 786436
  54.4 5.9 %collective-permute-start.12 = (f32[2,4,64,128]{3,2,1,0:T(8,128)S(1)}, f32[2,4,64,128]{3,2,1,0:T(8,128)S(1)}, u32[]{:S(2)}, u32[]{:S(2)}) collective-permute-start(f32[2,4,64,128]{3,2,1,0:T(8,128)S(1)} %pad_maximum_fusion.9.pair), channel_id=1, source_target_pairs={{0,252},{4,8},{8,4},{12,16},{16,12},{20,24},{24,20},{28,32},{32,28... | collective-permute-start | bytes 786440 | tf_op jit(solution)/shard_map/ppermute | solution.py:26
  60.3 4.9 %copy-start.13 = (f32[2,4,64,128]{3,2,1,0:T(8,128)}, f32[2,4,64,128]{3,2,1,0:T(8,128)S(1)}, u32[]{:S(2)}) copy-start(f32[2,4,64,128]{3,2,1,0:T(8,128)S(1)} %collective-permute-done.12.a) | copy-start | bytes 786436
  60.3 4.8 %collective-permute-start.13 = (f32[2,4,64,128]{3,2,1,0:T(8,128)S(1)}, f32[2,4,64,128]{3,2,1,0:T(8,128)S(1)}, u32[]{:S(2)}, u32[]{:S(2)}) collective-permute-start(f32[2,4,64,128]{3,2,1,0:T(8,128)S(1)} %collective-permute-done.12.a), channel_id=1, source_target_pairs={{0,4},{4,0},{8,12},{12,8},{16,20},{20,16},{24,28},{28,24},{32,36},... | collective-permute-start | bytes 786440 | tf_op jit(solution)/shard_map/ppermute | solution.py:26
  64.0 23.7 %copy-start.1 = (f32[3,272,128]{2,1,0:T(8,128)}, f32[3,272,128]{2,1,0:T(8,128)S(1)}, u32[]{:S(2)}) copy-start(f32[3,272,128]{2,1,0:T(8,128)S(1)} %pad_maximum_fusion.3.fown) | copy-start | bytes 1253380
  65.1 0.7 copy-start.14
  71.1 6.2 %collective-permute-start.15 = (f32[256,128]{1,0:T(8,128)}, f32[256,128]{1,0:T(8,128)S(1)}, u32[]{:S(2)}, u32[]{:S(2)}) collective-permute-start(f32[256,128]{1,0:T(8,128)} %bitcast.65), channel_id=1, source_target_pairs={{0,3},{1,2},{2,1},{3,0},{4,7},{5,6},{6,5},{7,4},{8,11},{9,10},{10,... | collective-permute-start | bytes 393224 | tf_op jit(solution)/shard_map/ppermute | solution.py:26
  73.1 4.6 %collective-permute-start.14 = (f32[256,128]{1,0:T(8,128)}, f32[256,128]{1,0:T(8,128)S(1)}, u32[]{:S(2)}, u32[]{:S(2)}) collective-permute-start(f32[256,128]{1,0:T(8,128)} %bitcast.66), channel_id=1, source_target_pairs={{0,1},{1,0},{2,3},{3,2},{4,5},{5,4},{6,7},{7,6},{8,9},{9,8},{10,11... | collective-permute-start | bytes 393224 | tf_op jit(solution)/shard_map/ppermute | solution.py:26
  73.2 10.3 %collective-permute-start.21 = (f32[1224,128]{1,0:T(8,128)S(1)}, f32[1224,128]{1,0:T(8,128)S(1)}, u32[]{:S(2)}, u32[]{:S(2)}) collective-permute-start(f32[1224,128]{1,0:T(8,128)S(1)} %get-tuple-element.26), channel_id=1, source_target_pairs={{0,252},{4,8},{8,4},{12,16},{16,12},{20,24},{24,20},{28,32},{32,28... | collective-permute-start | bytes 1880072 | tf_op jit(solution)/shard_map/ppermute | solution.py:26
  73.4 10.8 %collective-permute-start.20 = (f32[1224,128]{1,0:T(8,128)S(1)}, f32[1224,128]{1,0:T(8,128)S(1)}, u32[]{:S(2)}, u32[]{:S(2)}) collective-permute-start(f32[1224,128]{1,0:T(8,128)S(1)} %get-tuple-element.27), channel_id=1, source_target_pairs={{0,4},{4,0},{8,12},{12,8},{16,20},{20,16},{24,28},{28,24},{32,36},... | collective-permute-start | bytes 1880072 | tf_op jit(solution)/shard_map/ppermute | solution.py:26
  78.6 9.1 %copy-start.5 = (f32[3,256,128]{2,1,0:T(8,128)}, f32[3,256,128]{2,1,0:T(8,128)S(1)}, u32[]{:S(2)}) copy-start(f32[3,256,128]{2,1,0:T(8,128)S(1)} %pad_maximum_fusion.4.own) | copy-start | bytes 1179652
  78.6 9.1 %collective-permute-start.17 = (f32[3,256,128]{2,1,0:T(8,128)S(1)}, f32[3,256,128]{2,1,0:T(8,128)}, u32[]{:S(2)}, u32[]{:S(2)}) collective-permute-start(f32[3,256,128]{2,1,0:T(8,128)S(1)} %pad_maximum_fusion.4.own), channel_id=1, source_target_pairs={{0,252},{4,8},{8,4},{12,16},{16,12},{20,24},{24,20},{28,32},{32,28... | collective-permute-start | bytes 1179656 | tf_op jit(solution)/shard_map/ppermute | solution.py:26
  78.7 9.0 %collective-permute-start.16 = (f32[3,256,128]{2,1,0:T(8,128)S(1)}, f32[3,256,128]{2,1,0:T(8,128)}, u32[]{:S(2)}, u32[]{:S(2)}) collective-permute-start(f32[3,256,128]{2,1,0:T(8,128)S(1)} %pad_maximum_fusion.4.own), channel_id=1, source_target_pairs={{0,4},{4,0},{8,12},{12,8},{16,20},{20,16},{24,28},{28,24},{32,36},... | collective-permute-start | bytes 1179656 | tf_op jit(solution)/shard_map/ppermute | solution.py:26
  97.6 4.7 %collective-permute-start.22 = (f32[8,3,16,128]{3,2,1,0:T(8,128)}, f32[8,3,16,128]{3,2,1,0:T(8,128)S(1)}, u32[]{:S(2)}, u32[]{:S(2)}) collective-permute-start(f32[8,3,16,128]{3,2,1,0:T(8,128)} %get-tuple-element.15), channel_id=1, source_target_pairs={{0,1},{1,0},{2,3},{3,2},{4,5},{5,4},{6,7},{7,6},{8,9},{9,8},{10,11... | collective-permute-start | bytes 589832 | tf_op jit(solution)/shard_map/ppermute | solution.py:26
  99.0 5.9 %collective-permute-start.23 = (f32[8,3,16,128]{3,2,1,0:T(8,128)}, f32[8,3,16,128]{3,2,1,0:T(8,128)S(1)}, u32[]{:S(2)}, u32[]{:S(2)}) collective-permute-start(f32[8,3,16,128]{3,2,1,0:T(8,128)} %get-tuple-element.16), channel_id=1, source_target_pairs={{0,3},{1,2},{2,1},{3,0},{4,7},{5,6},{6,5},{7,4},{8,11},{9,10},{10,... | collective-permute-start | bytes 589832 | tf_op jit(solution)/shard_map/ppermute | solution.py:26
  102.3 15.3 %copy-start.9 = (f32[8,3,16,128]{3,2,1,0:T(8,128)}, f32[8,3,16,128]{3,2,1,0:T(8,128)S(1)}, u32[]{:S(2)}) copy-start(f32[8,3,16,128]{3,2,1,0:T(8,128)S(1)} %collective-permute-done.22.even) | copy-start | bytes 589828
  105.0 12.6 %copy-start.10 = (f32[8,3,16,128]{3,2,1,0:T(8,128)}, f32[8,3,16,128]{3,2,1,0:T(8,128)S(1)}, u32[]{:S(2)}) copy-start(f32[8,3,16,128]{3,2,1,0:T(8,128)S(1)} %collective-permute-done.23.odd) | copy-start | bytes 589828
  105.0 8.2 %collective-permute-start.24 = (f32[3,14,16,128]{3,2,1,0:T(8,128)S(1)}, f32[3,14,16,128]{3,2,1,0:T(8,128)S(1)}, u32[]{:S(2)}, u32[]{:S(2)}) collective-permute-start(f32[3,14,16,128]{3,2,1,0:T(8,128)S(1)} %pad_maximum_fusion.5), channel_id=1, source_target_pairs={{0,4},{4,0},{8,12},{12,8},{16,20},{20,16},{24,28},{28,24},{32,36},... | collective-permute-start | bytes 1032200 | tf_op jit(solution)/shard_map/ppermute | solution.py:26
  110.5 7.1 %collective-permute-start.25 = (f32[3,14,16,128]{3,2,1,0:T(8,128)S(1)}, f32[3,14,16,128]{3,2,1,0:T(8,128)S(1)}, u32[]{:S(2)}, u32[]{:S(2)}) collective-permute-start(f32[3,14,16,128]{3,2,1,0:T(8,128)S(1)} %pad_maximum_fusion.6), channel_id=1, source_target_pairs={{0,252},{4,8},{8,4},{12,16},{16,12},{20,24},{24,20},{28,32},{32,28... | collective-permute-start | bytes 1032200 | tf_op jit(solution)/shard_map/ppermute | solution.py:26
  113.2 4.3 %copy-start.11 = (f32[3,14,16,128]{3,2,1,0:T(8,128)}, f32[3,14,16,128]{3,2,1,0:T(8,128)S(1)}, u32[]{:S(2)}) copy-start(f32[3,14,16,128]{3,2,1,0:T(8,128)S(1)} %collective-permute-done.24.on) | copy-start | bytes 1032196
  117.6 0.7 copy-start.12
where the time goes:
time: 125 us
  starting transfers between devices  43.9 us (35%)
  waiting for transfers between devices  31.5 us (25%)
  Pallas kernels  25.1 us (20%)
  local copies, waits for them, and re-layouts  17.8 us (14%)
  other arithmetic  5.3 us (4%)
    ppermute x26, starting transfers between devices, swap(): lax.ppermute(x, axis, [(i, partner(i)) for i in range(lax.axis_size(axis))])  43.9 us
    ppermute x26, waiting for transfers between devices, swap(): lax.ppermute(x, axis, [(i, partner(i)) for i in range(lax.axis_size(axis))])  31.5 us
    pallas_call x4, Pallas kernels, call(): pl.pallas_call(kernel, out_shape=outs, in_specs=specs, out_specs=jax.tree...  25.1 us
    dynamic_slice x9, local copies, waits for them, and re-layouts, strip(): return lax.dynamic_slice_in_dim(x, at, width, dim)  4.25 us
    unnamed x42, local copies, waits for them, and re-layouts  3.81 us
    concatenate x1, local copies, waits for them, and re-layouts, shards(): jnp.concatenate([flat(source_fourth), flat(guess_fourth), flat(shift_four...  2.93 us
  transfers between devices with their start and end apart: 26, of which 17 were waited for; matrix products, arithmetic and copies ran while one was open for 13% of the time, Pallas kernels for 0%

commit v1 on v0

v1 whole, which is shorter than its diff:
```python
import jax
import jax.numpy as jnp
from jax import lax
from jax.experimental import pallas as pl
from jax.experimental.pallas import tpu as pltpu
from jax.sharding import PartitionSpec as P


UPPER = 14.0
LOWER = UPPER / 8.0
CENTRE = (UPPER + LOWER) / 2.0
HALF = (UPPER - LOWER) / 2.0
RATIO = CENTRE / HALF
FACTOR0 = 1.0 / RATIO
FACTOR1 = 1.0 / (2.0 * RATIO - FACTOR0)
FACTOR2 = 1.0 / (2.0 * RATIO - FACTOR1)

F32 = jnp.float32
BF16 = jnp.bfloat16
R = 16
L = 128

NZ, NY = 64, 4


def swap(x, axis, partner):
    return lax.ppermute(x, axis, [(i, partner(i)) for i in range(lax.axis_size(axis))])


def z_on(x):
    return swap(x, "gz", lambda i: i ^ 1)


def z_off(x):
    return swap(x, "gz", lambda i: (((i + 1) ^ 1) - 1) % NZ)


def z_off3(x):
    return swap(x, "gz", lambda i: (i - 3 if i % 2 == 0 else i + 3) % NZ)


def y_by(x, k):
    return swap(x, "gy", lambda j: j ^ k)


def y_even(x):
    return y_by(x, 1)


def y_odd(x):
    return y_by(x, 3)


def neighbours(v, i, j, width, wrap):
    jl = (j - 1) % width if wrap else j - 1
    jr = (j + 1) % width if wrap else j + 1
    mid = v[i, j]
    beside = v[i - 1, j] + v[i + 1, j] + v[i, jl] + v[i, jr]
    beside = beside + pltpu.roll(mid, 1, 1) + pltpu.roll(mid, L - 1, 1)
    return mid, beside


def smooth(u, f, s, res, d0, d1, emit, low, rows, width, wrap):
    def columns(k):
        return range(width) if wrap else range(k, width - k)

    def first(i, carry):
        for j in columns(1):
            mid, beside = neighbours(u, i, j, width, wrap)
            r = f[i, j] - ((6.0 + s[i, j]) * mid - beside)
            res[i, j] = r
            d0[i, j] = r * (1.0 / CENTRE)
        return carry

    def second(i, carry):
        for j in columns(2):
            mid, beside = neighbours(d0, i, j, width, wrap)
            r = res[i, j] - ((6.0 + s[i, j]) * mid - beside)
            res[i, j] = r
            d1[i, j] = (FACTOR1 * FACTOR0) * mid + (2.0 * FACTOR1 / HALF) * r
        return carry

    def third(i, carry):
        for j in columns(3):
            mid, beside = neighbours(d1, i, j, width, wrap)
            r = res[i, j] - ((6.0 + s[i, j]) * mid - beside)
            d2 = (FACTOR2 * FACTOR1) * mid + (2.0 * FACTOR2 / HALF) * r
            emit(i, j, u[i, j] + d0[i, j] + mid + d2)
        return carry

    lax.fori_loop(low + 1, low + 5 + rows, first, 0)
    lax.fori_loop(low + 2, low + 4 + rows, second, 0)
    lax.fori_loop(low + 3, low + 3 + rows, third, 0)


def prolong_cell(lines, index, blocks, guess, a, b):
    total = guess[a, b]
    for k in range(2):
        ri, ci = index(a, b, k)
        total = total + lax.dot_general(
            lines[ri, ci], blocks[a, b, k], (((1,), (1,)), ((), ())), preferred_element_type=F32
        )
    return total


VMEM = pl.BlockSpec(memory_space=pltpu.VMEM)
HBM = pl.BlockSpec(memory_space=pltpu.HBM)


def fetch(sems, *pairs):
    copies = [pltpu.make_async_copy(a, b, sems.at[n]) for n, (a, b) in enumerate(pairs)]
    for copy in copies:
        copy.start()
    return copies


def fetched(*arrays):
    return [pltpu.VMEM(x.shape, x.dtype) for x in arrays] + [pltpu.SemaphoreType.DMA((len(arrays) + 1,))]


def smem_last(*arrays):
    *first, sems = fetched(*arrays)
    return [*first[:-1], pltpu.SMEM(arrays[-1].shape, arrays[-1].dtype), sems]


def call(kernel, inputs, outs, scratch, flops, vmem=16, hbm=()):
    nbytes = sum(x.size * x.dtype.itemsize for x in inputs)
    specs = [HBM if n in hbm else VMEM for n in range(len(inputs))]
    return pl.pallas_call(
        kernel,
        out_shape=outs,
        in_specs=specs,
        out_specs=jax.tree.map(lambda _: VMEM, outs),
        scratch_shapes=scratch,
        compiler_params=pltpu.CompilerParams(vmem_limit_bytes=vmem << 20),
        cost_estimate=pl.CostEstimate(flops=flops, bytes_accessed=nbytes, transcendentals=0),
    )(*inputs)


def cells(rows, cols, dtype=F32):
    return pltpu.VMEM((rows, cols, R, L), dtype)


def shifts(rows, cols):
    return pltpu.VMEM((rows, cols, 1, L), F32)


def pack_kernel(source_fourth, guess_fourth, shift_fourth, shift_third, source_third, out, s4, s3, sems):
    pairs = [(shift_fourth, s4), (shift_third, s3), (source_fourth.at[0, 0], out.at[0:16]), (guess_fourth.at[0, 0], out.at[16:32])]
    for i in range(2):
        for j in range(2):
            at = 40 + (i * 2 + j) * R
            pairs.append((source_third.at[i, j], out.at[at : at + R]))
    copies = fetch(sems, *pairs)
    copies[0].wait()
    copies[1].wait()
    out[32:33, :] = s4[0]
    for i in range(2):
        out[33 + 2 * i : 35 + 2 * i, :] = s3[i]
    out[37:40, :] = jnp.zeros((3, L), F32)
    for copy in copies[2:]:
        copy.wait()


def fourth_kernel(pair, a, a3, b, b3, links_h, blocks_h, guess_h, out, start, u, f, s, res, d0, d1, lines, blocks, guess, links, sems):
    copies = fetch(sems, (blocks_h, blocks), (guess_h, guess), (links_h, links))
    gz, gy = lax.axis_index("gz"), lax.axis_index("gy")
    core = lax.rem(gz, 2)

    def place(ref, chip, first_bit):
        for slot in range(2):
            bit = first_bit if slot == 0 else 1 - first_bit
            row = chip * 2 + bit
            for k in range(4):
                col = lax.bitwise_xor(gy, k)
                f[row, col] = ref[slot, k, 0:16, :]
                u[row, col] = ref[slot, k, 16:32, :]
                s[row, col] = ref[slot, k, 32:33, :]

    place(pair, 2, core)
    place(a, 1 + 2 * core, 1 - core)
    place(b, 3 - 2 * core, core)
    place(a3, 4 * core, 1 - core)
    place(b3, 4 - 4 * core, core)

    def emit(i, j, value):
        lines[i - 3 - core, j] = value.astype(BF16)
        res[i, j] = value

    smooth(u, f, s, res, d0, d1, emit, core, 3, 4, True)
    out[0, 0] = res[4 + core, gy]

    for copy in copies:
        copy.wait()

    def index(i, j, k):
        q = links[i, k, j]
        return lax.rem(q // 4 - gz + 1 + NZ, NZ), lax.rem(q, 4)

    for i in range(2):
        for j in range(2):
            start[i, j] = prolong_cell(lines, index, blocks, guess, i, j)


def third_kernel(pair, a, b, fpair, fa, fb, spair, sa, sb, links_h, blocks, guess_h, out, start, u, f, s, res, d0, d1, lines, guess, links, sems):
    copies = fetch(sems, (guess_h, guess), (links_h, links))
    gz, gy = lax.axis_index("gz"), lax.axis_index("gy")
    core = lax.rem(gz, 2)

    def place(ref, fref, sref, chip, first_bit):
        for slot in range(2):
            bit = first_bit if slot == 0 else 1 - first_bit
            for k in range(4):
                col = lax.bitwise_xor(gy, k) * 2
                for i in range(2):
                    row = chip * 4 + bit * 2 + i
                    for j in range(2):
                        at = (i * 2 + j) * R
                        u[row, col + j] = ref[slot, k, at : at + R, :]
                        f[row, col + j] = fref[slot, k, at : at + R, :]
                        s[row, col + j] = sref[slot, k, 33 + i * 2 + j : 34 + i * 2 + j, :]

    place(pair, fpair, spair, 1, core)
    place(a, fa, sa, 2 * core, 1 - core)
    place(b, fb, sb, 2 - 2 * core, core)

    def emit(i, j, value):
        lines[i - 3 - 2 * core, j] = value.astype(BF16)
        res[i, j] = value

    smooth(u, f, s, res, d0, d1, emit, 2 * core, 4, 8, True)
    for i in range(2):
        for j in range(2):
            out[i, j] = res[4 + 2 * core + i, 2 * gy + j]

    for copy in copies:
        copy.wait()

    def index(i, j, k):
        q = links[i, k, j]
        return lax.rem(q // 8 - 2 * gz + 1 + 2 * NZ, 2 * NZ), lax.rem(q, 8)

    for i in range(4):
        for j in range(4):
            start[i, j] = prolong_cell(lines, index, blocks, guess, i, j)


ALONG_Y, ALONG_Z = 544, 1224


def along_y_kernel(source_first, shift_first, source_second_h, shift_second_h, own, even, odd, source_second, shift_second, sems):
    copies = fetch(sems, (source_second_h, source_second), (shift_second_h, shift_second))
    side = lax.rem(lax.axis_index("gy"), 2)
    for copy in copies:
        copy.wait()
    for i in range(4):
        for j in range(4):
            at = (i * 4 + j) * R
            own[at : at + R, :] = source_second[i, j]
        own[256 + i * 4 : 260 + i * 4, :] = shift_second[i]
    for ref, first in ((even, 6 - 6 * side), (odd, 6 * side)):
        ref[0:272, :] = own[...]
        for i in range(8):
            for j in range(2):
                at = 272 + (i * 2 + j) * R
                ref[at : at + R, :] = source_first[i, first + j]
            ref[528 + i * 2 : 530 + i * 2, :] = jnp.where(first == 0, shift_first[i, 0:2, :], shift_first[i, 6:8, :])


def along_z_kernel(source_first, shift_first, own, even, odd, on, off):
    core = lax.rem(lax.axis_index("gz"), 2)
    for ref, first in ((on, 6 - 6 * core), (off, 6 * core)):
        ref[0:272, :] = own[...]
        ref[272:544, :] = even[0:272, :]
        ref[544:816, :] = odd[0:272, :]
        for i in range(2):
            row = first + i
            for j in range(8):
                at = 816 + (i * 12 + j) * R
                ref[at : at + R, :] = source_first[row, j]
            ref[1200 + i * 12 : 1208 + i * 12, :] = shift_first[row]
            for n, side_ref in enumerate((even, odd)):
                at = 816 + (i * 12 + 8 + 2 * n) * R
                ref[at : at + 2 * R, :] = side_ref[pl.ds(pl.multiple_of(272 + row * 2 * R, 8), 2 * R), :]
                low = side_ref[528 + 2 * i : 530 + 2 * i, :]
                high = side_ref[540 + 2 * i : 542 + 2 * i, :]
                ref[1208 + i * 12 + 2 * n : 1210 + i * 12 + 2 * n, :] = jnp.where(first == 0, low, high)


def second_kernel(own, own_even, own_odd, on, off, fown, feven, fodd, fon, foff, links_h, blocks, guess, out, start, even, odd, u, f, s, res, d0, d1, lines, links, sems):
    copies = fetch(sems, (links_h, links))
    gz, gy = lax.axis_index("gz"), lax.axis_index("gy")
    core, side = lax.rem(gz, 2), lax.rem(gy, 2)
    starts = (4, 8 - 8 * side, 8 * side)

    def place(refs, frefs, row0):
        for k in range(3):
            ref, base = refs[k]
            fref, fbase = frefs[k]
            for i in range(4):
                for j in range(4):
                    c = i * 4 + j
                    row, col = row0 + i, starts[k] + j
                    u[row, col] = ref[base + c * R : base + (c + 1) * R, :]
                    f[row, col] = fref[fbase + c * R : fbase + (c + 1) * R, :]
                    s[row, col] = fref[fbase + 256 + c : fbase + 257 + c, :]

    place(((own, 0), (own_even, 0), (own_odd, 0)), ((fown, 0), (feven, 0), (fodd, 0)), 4)
    for ref, fref, row0 in ((on, fon, 8 - 8 * core), (off, foff, 8 * core)):
        place([(ref, 256 * k) for k in range(3)], [(fref, 272 * k) for k in range(3)], row0)

    def emit(i, j, value):
        lines[i - 3, j - 3] = value.astype(BF16)
        res[i, j] = value

    smooth(u, f, s, res, d0, d1, emit, 0, 6, 12, False)
    for i in range(4):
        for j in range(4):
            out[i, j] = res[4 + i, 4 + j]

    for copy in copies:
        copy.wait()

    def index(i, j, k):
        q = links[i, k, j]
        row = lax.rem(q // 16 - 4 * gz + 1 + 4 * NZ, 4 * NZ)
        return row, lax.rem(lax.rem(q, 16) - 4 * gy + 1 + 4 * NY, 4 * NY)

    def row_of_cells(i, carry):
        for j in range(8):
            start[i, j] = prolong_cell(lines, index, blocks, guess, i, j)
        return carry

    lax.fori_loop(0, 8, row_of_cells, 0)
    for i in range(8):
        for j in range(3):
            at = (i * 3 + j) * R
            even[at : at + R, :] = start[i, 5 - 5 * side + j]
            odd[at : at + R, :] = start[i, 5 * side + j]


def rows_kernel(start, even, odd, on, off):
    core = lax.rem(lax.axis_index("gz"), 2)
    for ref, first in ((on, 5 - 5 * core), (off, 5 * core)):
        for i in range(3):
            for j in range(8):
                at = (i * 14 + j) * R
                ref[at : at + R, :] = start[first + i, j]
            for n, side_ref in enumerate((even, odd)):
                at = (i * 14 + 8 + 3 * n) * R
                ref[at : at + 3 * R, :] = side_ref[pl.ds(pl.multiple_of((first + i) * 3 * R, 8), 3 * R), :]


def first_kernel(own, even, odd, on, off, fown, sown, feven, fodd, fon, foff, out, u, f, s, res, d0, d1):
    gz, gy = lax.axis_index("gz"), lax.axis_index("gy")
    core, side = lax.rem(gz, 2), lax.rem(gy, 2)
    even_u, odd_u = 11 - 11 * side, 11 * side
    even_f, odd_f = 11 - 10 * side, 1 + 10 * side

    for i in range(8):
        for j in range(8):
            u[3 + i, 3 + j] = own[i, j]
            f[3 + i, 3 + j] = fown[i, j]
            s[3 + i, 3 + j] = sown[i, j : j + 1, :]
        for j in range(3):
            at = (i * 3 + j) * R
            u[3 + i, even_u + j] = even[at : at + R, :]
            u[3 + i, odd_u + j] = odd[at : at + R, :]
        for j in range(2):
            c = i * 2 + j
            at = 272 + c * R
            f[3 + i, even_f + j] = feven[at : at + R, :]
            f[3 + i, odd_f + j] = fodd[at : at + R, :]
            s[3 + i, even_f + j] = feven[528 + c : 529 + c, :]
            s[3 + i, odd_f + j] = fodd[528 + c : 529 + c, :]

    def place(ref, fref, row_u, row_f):
        for i in range(3):
            for j in range(14):
                col = 3 + j if j < 8 else even_u + j - 8 if j < 11 else odd_u + j - 11
                at = (i * 14 + j) * R
                u[row_u + i, col] = ref[at : at + R, :]
        for i in range(2):
            for j in range(12):
                col = 3 + j if j < 8 else even_f + j - 8 if j < 10 else odd_f + j - 10
                c = i * 12 + j
                at = 816 + c * R
                f[row_f + i, col] = fref[at : at + R, :]
                s[row_f + i, col] = fref[1200 + c : 1201 + c, :]

    place(on, fon, 11 - 11 * core, 11 - 10 * core)
    place(off, foff, 11 * core, 1 + 10 * core)

    def emit(i, j, value):
        out[i - 3, j - 3] = value

    smooth(u, f, s, res, d0, d1, emit, 0, 8, 14, False)


def sds(*shape, dtype=F32):
    return jax.ShapeDtypeStruct(shape, dtype)


def after(x, *done):
    return lax.optimization_barrier((x, *done))[0]


def flat(x):
    return x.reshape(-1, L)


def shards(
    source_first, source_second, source_third, source_fourth,
    guess_first, guess_second, guess_third, guess_fourth,
    shift_first, shift_second, shift_third, shift_fourth,
    blocks_first, blocks_second, blocks_third,
    links_first, links_second, links_third,
):
    links_first, links_second, links_third = (x.transpose(0, 2, 1) for x in (links_first, links_second, links_third))

    (pack,) = call(pack_kernel, (source_fourth, guess_fourth, shift_fourth, shift_third, source_third), (sds(104, L),), [pltpu.VMEM((1, 1, L), F32), pltpu.VMEM((2, 2, L), F32), pltpu.SemaphoreType.DMA((8,))], 1000, 2, range(5))
    y1, y2, y3 = y_by(pack, 1), y_by(pack, 2), y_by(pack, 3)
    line = jnp.stack([pack, y1, y2, y3])
    line_on = z_on(line)
    pair = jnp.stack([line[:, :40], line_on[:, :40]])
    pair_f = jnp.stack([line[:, 40:], line_on[:, 40:]])
    near = z_off(pair)
    far = z_off3(pair)

    mine, ahead_even, ahead_odd = call(
        along_y_kernel,
        (source_first, shift_first, source_second, shift_second),
        (sds(272, L), sds(ALONG_Y, L), sds(ALONG_Y, L)),
        fetched(source_second, shift_second), 10000, 4, (2, 3),
    )
    ahead_even, ahead_odd = y_even(after(ahead_even, y1, y2, y3)), y_odd(after(ahead_odd, y1, y2, y3))
    ahead_on, ahead_off = call(
        along_z_kernel,
        (source_first, shift_first, mine, ahead_even, ahead_odd),
        (sds(ALONG_Z, L), sds(ALONG_Z, L)),
        [], 10000, 6,
    )

    near_b, far_b = z_on(near), z_on(far)
    near_f = z_off(after(pair_f, near, far))
    near_fb = z_on(near_f)
    ahead_on = z_on(after(ahead_on, near_b, far_b))
    ahead_off = z_off(after(ahead_off, near_b, far_b))

    def smoothing_scratch(rows, cols):
        return [cells(rows, cols), cells(rows, cols), shifts(rows, cols)] + [cells(rows, cols)] * 3

    out_fourth, start_third = call(
        fourth_kernel,
        (pair, near, far, near_b, far_b, links_third, blocks_third, guess_third),
        (sds(1, 1, R, L), sds(2, 2, R, L)),
        smoothing_scratch(10, 4) + [cells(3, 4, BF16)] + smem_last(blocks_third, guess_third, links_third),
        4_000_000, 6, (5, 6, 7),
    )

    own = flat(start_third)
    line3 = jnp.stack([own, y_by(own, 1), y_by(own, 2), y_by(own, 3)])
    pair3 = jnp.stack([line3, z_on(line3)])
    near3 = z_off(pair3)
    near3_b = z_on(near3)
    out_third, start_second = call(
        third_kernel,
        (pair3, near3, near3_b, pair_f, near_f, near_fb, pair, near, near_b, links_second, blocks_second, guess_second),
        (sds(2, 2, R, L), sds(4, 4, R, L)),
        smoothing_scratch(12, 8) + [cells(4, 8, BF16)] + smem_last(guess_second, links_second),
        8_000_000, 12, (9, 11),
    )

    own = flat(start_second)
    own_even, own_odd = y_even(own), y_odd(own)
    block = jnp.concatenate([own, own_even, own_odd])
    out_second, start_first, strip_even, strip_odd = call(
        second_kernel,
        (own, own_even, own_odd, z_on(block), z_off(block), mine, ahead_even, ahead_odd, ahead_on, ahead_off, links_first, blocks_first, guess_first),
        (sds(4, 4, R, L), sds(8, 8, R, L), sds(24 * R, L), sds(24 * R, L)),
        smoothing_scratch(12, 12) + [cells(6, 6, BF16)] + smem_last(links_first),
        16_000_000, 20, (10,),
    )

    u_even, u_odd = y_even(strip_even), y_odd(strip_odd)
    u_on, u_off = call(rows_kernel, (start_first, u_even, u_odd), (sds(42 * R, L), sds(42 * R, L)), [], 10000, 4)
    (out_first,) = call(
        first_kernel,
        (start_first, u_even, u_odd, z_on(u_on), z_off(u_off), source_first, shift_first, ahead_even, ahead_odd, ahead_on, ahead_off),
        (sds(8, 8, R, L),),
        smoothing_scratch(14, 14),
        16_000_000, 20,
    )
    return out_first, out_second, out_third, out_fourth


def solution(mesh):
    field = P("gz", "gy", None, None)
    line = P("gz", "gy", None)
    block = P("gz", "gy", None, None, None)

    return jax.shard_map(
        shards,
        mesh=mesh,
        in_specs=(field,) * 8 + (line,) * 4 + (block,) * 3 + (line,) * 3,
        out_specs=(field,) * 4,
        check_vma=False,
    )
```

time: 125 us -> 114 us (0.912)
  local copies, waits for them, and re-layouts: 17.8 us -> 9.32 us
  starting transfers between devices: 43.9 us -> 52.3 us
  Pallas kernels: 25.1 us -> 16.8 us
  other arithmetic: 5.3 us -> 0.11 us
  waiting for transfers between devices: 31.5 us -> 33.9 us
    ppermute x26 -> x28, starting transfers between devices: 43.9 us -> 52.3 us  [swap(): lax.ppermute(x, axis, [(i, partner(i)) for i in range(lax.axis_size(axis))])]
    pallas_call x4 -> x8, Pallas kernels: 25.1 us -> 16.8 us  [call(): pl.pallas_call(kernel, out_shape=outs, in_specs=specs, out_specs=jax.tree...]
    unnamed x42 -> x35, local copies, waits for them, and re-layouts: 3.81 us -> 9.29 us
    dynamic_slice x9 -> x0, local copies, waits for them, and re-layouts: 4.25 us -> none  [strip(): return lax.dynamic_slice_in_dim(x, at, width, dim)]
    reshape x7 -> x0, local copies, waits for them, and re-layouts: 3.79 us -> none  [the longest x1 1.27 us: shards(): links_third.reshape(-1)]
    slice x10 -> x0, local copies, waits for them, and re-layouts: 3 us -> none  [the longest x2 1.57 us: shards(): x[:816].reshape(3, 272, L)]
    concatenate x1 -> x0, local copies, waits for them, and re-layouts: 2.93 us -> none  [shards(): jnp.concatenate([flat(source_fourth), flat(guess_fourth), flat(shift_four...]
    concatenate x8 -> x1, other arithmetic: 2.54 us -> 0.03 us  [shards(): block = jnp.concatenate([own, own_even, own_odd])]
  transfers between devices with their start and end apart: 26 -> 28, of which waited for: 17 -> 17; matrix products, arithmetic and copies ran while one was open for 13% -> 1% of each run, Pallas kernels for 0% -> 3%
where the time goes in v1:
time: 114 us; the launch traced here: 113 us
  starting transfers between devices  52.3 us (46%)
  waiting for transfers between devices  33.9 us (30%)
  Pallas kernels  16.8 us (15%)
  local copies, waits for them, and re-layouts  9.32 us (8%)
    ppermute x28, starting transfers between devices, swap(): lax.ppermute(x, axis, [(i, partner(i)) for i in range(lax.axis_size(axis))])  52.3 us
    ppermute x28, waiting for transfers between devices, swap(): lax.ppermute(x, axis, [(i, partner(i)) for i in range(lax.axis_size(axis))])  33.9 us
    pallas_call x8, Pallas kernels, call(): pl.pallas_call(kernel, out_shape=outs, in_specs=specs, out_specs=jax.tree...  16.8 us
    unnamed x35, local copies, waits for them, and re-layouts  9.29 us
  transfers between devices with their start and end apart: 28, of which 17 were waited for; matrix products, arithmetic and copies ran while one was open for 1% of the time, Pallas kernels for 3%

profile of v1, /device:TPU:1, one launch (start us, length us, event | category | flops | bytes accessed | tf_op | source)
XLA Modules:
  0.0 113.3 jit_solution(2705716144039411385)
XLA Ops:
  0.7 0.9 copy-done.8
  1.5 0.7 copy-done.12
  2.2 0.7 copy-done.13
  4.4 3.6 %collective-permute-start.2 = (f32[104,128]{1,0:T(8,128)S(1)}, f32[104,128]{1,0:T(8,128)S(1)}, u32[]{:S(2)}, u32[]{:S(2)}) collective-permute-start(f32[104,128]{1,0:T(8,128)S(1)} %shard_map.201), channel_id=1, source_target_pairs={{0,3},{1,2},{2,1},{3,0},{4,7},{5,6},{6,5},{7,4},{8,11},{9,10},{10,... | collective-permute-start | bytes 159752 | tf_op jit(solution)/shard_map/ppermute | solution.py:27
  8.7 0.8 collective-permute-done.2
  9.6 3.1 %collective-permute-done.1 = f32[104,128]{1,0:T(8,128)S(1)} collective-permute-done((f32[104,128]{1,0:T(8,128)S(1)}, f32[104,128]{1,0:T(8,128)S(1)}, u32[]{:S(2)}, u32[]{:S(2)}) %collective-permute-start.1) | collective-permute-done | bytes 53280 | tf_op jit(solution)/shard_map/ppermute | solution.py:27
  12.7 2.1 %collective-permute-start.3 = (f32[4,104,128]{2,1,0:T(8,128)S(1)}, f32[4,104,128]{2,1,0:T(8,128)S(1)}, u32[]{:S(2)}, u32[]{:S(2)}) collective-permute-start(f32[4,104,128]{2,1,0:T(8,128)S(1)} %pad_maximum_fusion.3), channel_id=1, source_target_pairs={{0,4},{4,0},{8,12},{12,8},{16,20},{20,16},{24,28},{28,24},{32,36},... | collective-permute-start | bytes 638984 | tf_op jit(solution)/shard_map/ppermute | solution.py:27
  14.8 1.1 collective-permute-done.3
  15.9 3.3 %collective-permute-start.5 = (f32[2,4,40,128]{3,2,1,0:T(8,128)S(1)}, f32[2,4,40,128]{3,2,1,0:T(8,128)S(1)}, u32[]{:S(2)}, u32[]{:S(2)}) collective-permute-start(f32[2,4,40,128]{3,2,1,0:T(8,128)S(1)} %pad_maximum_fusion.4.pair.spair), channel_id=1, source_target_pairs={{0,244},{4,16},{8,252},{12,24},{16,4},{20,32},{24,12},{28,40},{32,... | collective-permute-start | bytes 491528 | tf_op jit(solution)/shard_map/ppermute | solution.py:27
  19.2 6.0 %collective-permute-start.4 = (f32[2,4,40,128]{3,2,1,0:T(8,128)S(1)}, f32[2,4,40,128]{3,2,1,0:T(8,128)S(1)}, u32[]{:S(2)}, u32[]{:S(2)}) collective-permute-start(f32[2,4,40,128]{3,2,1,0:T(8,128)S(1)} %pad_maximum_fusion.4.pair.spair), channel_id=1, source_target_pairs={{0,252},{4,8},{8,4},{12,16},{16,12},{20,24},{24,20},{28,32},{32,28... | collective-permute-start | bytes 491528 | tf_op jit(solution)/shard_map/ppermute | solution.py:27
  25.2 4.0 %collective-permute-start.7 = (f32[2,4,40,128]{3,2,1,0:T(8,128)S(1)}, f32[2,4,40,128]{3,2,1,0:T(8,128)S(1)}, u32[]{:S(2)}, u32[]{:S(2)}) collective-permute-start(f32[2,4,40,128]{3,2,1,0:T(8,128)S(1)} %collective-permute-done.5.a3), channel_id=1, source_target_pairs={{0,4},{4,0},{8,12},{12,8},{16,20},{20,16},{24,28},{28,24},{32,36},... | collective-permute-start | bytes 491528 | tf_op jit(solution)/shard_map/ppermute | solution.py:27
  29.2 0.8 collective-permute-done.4.a.sa
  30.0 2.6 %collective-permute-start.6 = (f32[2,4,40,128]{3,2,1,0:T(8,128)S(1)}, f32[2,4,40,128]{3,2,1,0:T(8,128)S(1)}, u32[]{:S(2)}, u32[]{:S(2)}) collective-permute-start(f32[2,4,40,128]{3,2,1,0:T(8,128)S(1)} %collective-permute-done.4.a.sa), channel_id=1, source_target_pairs={{0,4},{4,0},{8,12},{12,8},{16,20},{20,16},{24,28},{28,24},{32,36},... | collective-permute-start | bytes 491528 | tf_op jit(solution)/shard_map/ppermute | solution.py:27
  32.6 0.8 copy.22
  33.7 0.9 copy-done.5
  34.6 0.8 copy-done.9
  35.4 2.2 %shard_map.202 = (f32[1,1,16,128]{3,2,1,0:T(8,128)}, f32[2,2,16,128]{3,2,1,0:T(8,128)S(1)}) custom-call(f32[2,4,40,128]{3,2,1,0:T(8,128)S(1)} %pad_maximum_fusion.4.pair.spair, f32[2,4,40,128]{3,2,1,0:T(8,128)S(1)} %collective-permute-done.4.a.sa, f32[2,4,40,128]{3,2,1,0:T(8,128)S(1)} %collective-permute-done.5.a3, ...), custom_call_target="tpu_custom_call" | custom-call | flops 4000000 | bytes 1114144 | tf_op jit(solution)/shard_map/pallas_call | solution.py:129
  37.6 1.1 collective-permute-start.10
  38.7 0.8 collective-permute-start.9
  39.5 1.4 %collective-permute-start.8 = (f32[64,128]{1,0:T(8,128)S(1)}, f32[64,128]{1,0:T(8,128)S(1)}, u32[]{:S(2)}, u32[]{:S(2)}) collective-permute-start(f32[64,128]{1,0:T(8,128)S(1)} %bitcast.31), channel_id=1, source_target_pairs={{0,1},{1,0},{2,3},{3,2},{4,5},{5,4},{6,7},{7,6},{8,9},{9,8},{10,11... | collective-permute-start | bytes 98312 | tf_op jit(solution)/shard_map/ppermute | solution.py:27
  41.0 0.7 collective-permute-done.10
  41.7 1.3 %collective-permute-done.9 = f32[64,128]{1,0:T(8,128)S(1)} collective-permute-done((f32[64,128]{1,0:T(8,128)S(1)}, f32[64,128]{1,0:T(8,128)S(1)}, u32[]{:S(2)}, u32[]{:S(2)}) %collective-permute-start.9) | collective-permute-done | bytes 32800 | tf_op jit(solution)/shard_map/ppermute | solution.py:27
  43.0 2.1 %collective-permute-start.11 = (f32[4,64,128]{2,1,0:T(8,128)S(1)}, f32[4,64,128]{2,1,0:T(8,128)S(1)}, u32[]{:S(2)}, u32[]{:S(2)}) collective-permute-start(f32[4,64,128]{2,1,0:T(8,128)S(1)} %get-tuple-element.45), channel_id=1, source_target_pairs={{0,4},{4,0},{8,12},{12,8},{16,20},{20,16},{24,28},{28,24},{32,36},... | collective-permute-start | bytes 393224 | tf_op jit(solution)/shard_map/ppermute | solution.py:27
  45.3 0.8 collective-permute-done.11
  46.2 1.0 collective-permute-start.12
  47.1 4.2 %collective-permute-done.14.fa = f32[2,4,64,128]{3,2,1,0:T(8,128)S(1)} collective-permute-done((f32[2,4,64,128]{3,2,1,0:T(8,128)S(1)}, f32[2,4,64,128]{3,2,1,0:T(8,128)S(1)}, u32[]{:S(2)}, u32[]{:S(2)}) %collective-permute-start.14) | collective-permute-done | bytes 262176 | tf_op jit(solution)/shard_map/ppermute | solution.py:27
  51.4 3.0 %collective-permute-start.15 = (f32[2,4,64,128]{3,2,1,0:T(8,128)S(1)}, f32[2,4,64,128]{3,2,1,0:T(8,128)S(1)}, u32[]{:S(2)}, u32[]{:S(2)}) collective-permute-start(f32[2,4,64,128]{3,2,1,0:T(8,128)S(1)} %collective-permute-done.14.fa), channel_id=1, source_target_pairs={{0,4},{4,0},{8,12},{12,8},{16,20},{20,16},{24,28},{28,24},{32,36},... | collective-permute-start | bytes 786440 | tf_op jit(solution)/shard_map/ppermute | solution.py:27
  54.4 3.7 %collective-permute-start.13 = (f32[2,4,64,128]{3,2,1,0:T(8,128)S(1)}, f32[2,4,64,128]{3,2,1,0:T(8,128)S(1)}, u32[]{:S(2)}, u32[]{:S(2)}) collective-permute-start(f32[2,4,64,128]{3,2,1,0:T(8,128)S(1)} %collective-permute-done.12.a), channel_id=1, source_target_pairs={{0,4},{4,0},{8,12},{12,8},{16,20},{20,16},{24,28},{28,24},{32,36},... | collective-permute-start | bytes 786440 | tf_op jit(solution)/shard_map/ppermute | solution.py:27
  58.2 0.9 copy-done.7
  59.1 0.7 copy-done.10
  60.0 1.5 %collective-permute-start.21 = (f32[544,128]{1,0:T(8,128)S(1)}, f32[544,128]{1,0:T(8,128)S(1)}, u32[]{:S(2)}, u32[]{:S(2)}) collective-permute-start(f32[544,128]{1,0:T(8,128)S(1)} %get-tuple-element.31), channel_id=1, source_target_pairs={{0,3},{1,2},{2,1},{3,0},{4,7},{5,6},{6,5},{7,4},{8,11},{9,10},{10,... | collective-permute-start | bytes 835592 | tf_op jit(solution)/shard_map/ppermute | solution.py:27
  61.5 0.9 copy-done.6
  63.1 3.2 %shard_map.203 = (f32[2,2,16,128]{3,2,1,0:T(8,128)}, f32[4,4,16,128]{3,2,1,0:T(8,128)S(1)}) custom-call(f32[2,4,64,128]{3,2,1,0:T(8,128)S(1)} %pad_maximum_fusion.1.pair, f32[2,4,64,128]{3,2,1,0:T(8,128)S(1)} %collective-permute-done.12.a, f32[2,4,64,128]{3,2,1,0:T(8,128)S(1)} %collective-permute-done.13.b, f32[2,4,64,128]{3,2,1,0:T(8,128)S(1)} %pad_maximum_fusion.2.fpair, ...), custom_call_target="tpu_custom_call" | custom-call | flops 8000000 | bytes 3244160 | tf_op jit(solution)/shard_map/pallas_call | solution.py:129
  66.4 1.7 %collective-permute-start.17 = (f32[256,128]{1,0:T(8,128)S(1)}, f32[256,128]{1,0:T(8,128)S(1)}, u32[]{:S(2)}, u32[]{:S(2)}) collective-permute-start(f32[256,128]{1,0:T(8,128)S(1)} %bitcast.24), channel_id=1, source_target_pairs={{0,3},{1,2},{2,1},{3,0},{4,7},{5,6},{6,5},{7,4},{8,11},{9,10},{10,... | collective-permute-start | bytes 393224 | tf_op jit(solution)/shard_map/ppermute | solution.py:27
  68.8 0.7 collective-permute-done.21.odd.fodd
  69.7 2.2 %collective-permute-start.22 = (f32[1224,128]{1,0:T(8,128)S(1)}, f32[1224,128]{1,0:T(8,128)S(1)}, u32[]{:S(2)}, u32[]{:S(2)}) collective-permute-start(f32[1224,128]{1,0:T(8,128)S(1)} %get-tuple-element.33), channel_id=1, source_target_pairs={{0,4},{4,0},{8,12},{12,8},{16,20},{20,16},{24,28},{28,24},{32,36},... | collective-permute-start | bytes 1880072 | tf_op jit(solution)/shard_map/ppermute | solution.py:27
  71.9 0.7 collective-permute-done.17.own_odd
  72.7 3.2 %collective-permute-start.18 = (f32[768,128]{1,0:T(8,128)S(1)}, f32[768,128]{1,0:T(8,128)S(1)}, u32[]{:S(2)}, u32[]{:S(2)}) collective-permute-start(f32[768,128]{1,0:T(8,128)S(1)} %pad_maximum_fusion), channel_id=1, source_target_pairs={{0,4},{4,0},{8,12},{12,8},{16,20},{20,16},{24,28},{28,24},{32,36},... | collective-permute-start | bytes 1179656 | tf_op jit(solution)/shard_map/ppermute | solution.py:27
  76.0 3.7 %collective-permute-done.23.foff = f32[1224,128]{1,0:T(8,128)S(1)} collective-permute-done((f32[1224,128]{1,0:T(8,128)S(1)}, f32[1224,128]{1,0:T(8,128)S(1)}, u32[]{:S(2)}, u32[]{:S(2)}) %collective-permute-start.23) | collective-permute-done | bytes 626720 | tf_op jit(solution)/shard_map/ppermute | solution.py:27
  79.7 4.2 %collective-permute-done.19.off = f32[768,128]{1,0:T(8,128)S(1)} collective-permute-done((f32[768,128]{1,0:T(8,128)S(1)}, f32[768,128]{1,0:T(8,128)S(1)}, u32[]{:S(2)}, u32[]{:S(2)}) %collective-permute-start.19) | collective-permute-done | bytes 393248 | tf_op jit(solution)/shard_map/ppermute | solution.py:27
  83.9 6.4 %shard_map.206 = (f32[4,4,16,128]{3,2,1,0:T(8,128)}, f32[8,8,16,128]{3,2,1,0:T(8,128)S(1)}, f32[384,128]{1,0:T(8,128)S(1)}, f32[384,128]{1,0:T(8,128)S(1)}) custom-call(f32[256,128]{1,0:T(8,128)S(1)} %bitcast.27, f32[256,128]{1,0:T(8,128)S(1)} %collective-permute-done.16.own_even, f32[256,128]{1,0:T(8,128)S(1)} %collective-permute-done.17.own_odd, ...), custom_call_target="tpu_custom_call" | custom-call | flops 16000000 | bytes 7848448 | tf_op jit(solution)/shard_map/pallas_call | solution.py:129
  90.6 1.4 %collective-permute-start.25 = (f32[384,128]{1,0:T(8,128)S(1)}, f32[384,128]{1,0:T(8,128)S(1)}, u32[]{:S(2)}, u32[]{:S(2)}) collective-permute-start(f32[384,128]{1,0:T(8,128)S(1)} %get-tuple-element.38), channel_id=1, source_target_pairs={{0,3},{1,2},{2,1},{3,0},{4,7},{5,6},{6,5},{7,4},{8,11},{9,10},{10,... | collective-permute-start | bytes 589832 | tf_op jit(solution)/shard_map/ppermute | solution.py:27
  91.9 3.0 %collective-permute-done.24.even = f32[384,128]{1,0:T(8,128)S(1)} collective-permute-done((f32[384,128]{1,0:T(8,128)S(1)}, f32[384,128]{1,0:T(8,128)S(1)}, u32[]{:S(2)}, u32[]{:S(2)}) %collective-permute-start.24) | collective-permute-done | bytes 196640 | tf_op jit(solution)/shard_map/ppermute | solution.py:27
  94.9 1.4 %collective-permute-done.25.odd = f32[384,128]{1,0:T(8,128)S(1)} collective-permute-done((f32[384,128]{1,0:T(8,128)S(1)}, f32[384,128]{1,0:T(8,128)S(1)}, u32[]{:S(2)}, u32[]{:S(2)}) %collective-permute-start.25) | collective-permute-done | bytes 196640 | tf_op jit(solution)/shard_map/ppermute | solution.py:27
  96.3 5.5 %collective-permute-start.26 = (f32[672,128]{1,0:T(8,128)S(1)}, f32[672,128]{1,0:T(8,128)S(1)}, u32[]{:S(2)}, u32[]{:S(2)}) collective-permute-start(f32[672,128]{1,0:T(8,128)S(1)} %get-tuple-element.39), channel_id=1, source_target_pairs={{0,4},{4,0},{8,12},{12,8},{16,20},{20,16},{24,28},{28,24},{32,36},... | collective-permute-start | bytes 1032200 | tf_op jit(solution)/shard_map/ppermute | solution.py:27
  101.9 1.3 %collective-permute-done.26.on = f32[672,128]{1,0:T(8,128)S(1)} collective-permute-done((f32[672,128]{1,0:T(8,128)S(1)}, f32[672,128]{1,0:T(8,128)S(1)}, u32[]{:S(2)}, u32[]{:S(2)}) %collective-permute-start.26) | collective-permute-done | bytes 344096 | tf_op jit(solution)/shard_map/ppermute | solution.py:27
  103.2 5.7 %collective-permute-done.27.off = f32[672,128]{1,0:T(8,128)S(1)} collective-permute-done((f32[672,128]{1,0:T(8,128)S(1)}, f32[672,128]{1,0:T(8,128)S(1)}, u32[]{:S(2)}, u32[]{:S(2)}) %collective-permute-start.27) | collective-permute-done | bytes 344096 | tf_op jit(solution)/shard_map/ppermute | solution.py:27
  108.8 4.5 %shard_map.208 = f32[8,8,16,128]{3,2,1,0:T(8,128)} custom-call(f32[8,8,16,128]{3,2,1,0:T(8,128)S(1)} %get-tuple-element.36.start.own, f32[384,128]{1,0:T(8,128)S(1)} %collective-permute-done.24.even, f32[384,128]{1,0:T(8,128)S(1)} %collective-permute-done.25.odd, f32[672,128]{1,0:T(8,128)S(1)} %collective-permute-done.26.on, ...), custom_call_target="tpu_custom_call" | custom-call | flops 16000000 | bytes 3973120 | tf_op jit(solution)/shard_map/pallas_call | solution.py:129
  (61 shorter events, 4.9 us)
Async XLA Ops:
  0.6 57.5 %copy-start.4 = (f32[8,8,128]{2,1,0:T(8,128)S(1)}, f32[8,8,128]{2,1,0:T(8,128)}, u32[]{:S(2)}) copy-start(f32[8,8,128]{2,1,0:T(8,128)} %sown.1) | copy-start | bytes 98308
  0.6 57.5 %copy-start = (f32[8,8,16,128]{3,2,1,0:T(8,128)S(1)}, f32[8,8,16,128]{3,2,1,0:T(8,128)}, u32[]{:S(2)}) copy-start(f32[8,8,16,128]{3,2,1,0:T(8,128)} %fown.1) | copy-start | bytes 1572868
  0.7 60.9 %copy-start.2 = (bf16[4,4,2,128,128]{4,3,2,1,0:T(8,128)(2,1)S(1)}, bf16[4,4,2,128,128]{4,3,2,1,0:T(8,128)(2,1)}, u32[]{:S(2)}) copy-start(bf16[4,4,2,128,128]{4,3,2,1,0:T(8,128)(2,1)} %blocks.2) | copy-start | bytes 3145732
  0.7 0.9 copy-start.8
  1.5 0.7 copy-start.12
  2.2 0.7 copy-start.13
  2.9 0.7 copy-start.15
  3.6 0.7 copy-start.16
  4.4 5.2 %collective-permute-start.2 = (f32[104,128]{1,0:T(8,128)S(1)}, f32[104,128]{1,0:T(8,128)S(1)}, u32[]{:S(2)}, u32[]{:S(2)}) collective-permute-start(f32[104,128]{1,0:T(8,128)S(1)} %shard_map.201), channel_id=1, source_target_pairs={{0,3},{1,2},{2,1},{3,0},{4,7},{5,6},{6,5},{7,4},{8,11},{9,10},{10,... | collective-permute-start | bytes 159752 | tf_op jit(solution)/shard_map/ppermute | solution.py:27
  8.1 4.6 %collective-permute-start.1 = (f32[104,128]{1,0:T(8,128)S(1)}, f32[104,128]{1,0:T(8,128)S(1)}, u32[]{:S(2)}, u32[]{:S(2)}) collective-permute-start(f32[104,128]{1,0:T(8,128)S(1)} %shard_map.201), channel_id=1, source_target_pairs={{0,2},{1,3},{2,0},{3,1},{4,6},{5,7},{6,4},{7,5},{8,10},{9,11},{10,... | collective-permute-start | bytes 159752 | tf_op jit(solution)/shard_map/ppermute | solution.py:27
  8.4 4.2 %collective-permute-start = (f32[104,128]{1,0:T(8,128)S(1)}, f32[104,128]{1,0:T(8,128)S(1)}, u32[]{:S(2)}, u32[]{:S(2)}) collective-permute-start(f32[104,128]{1,0:T(8,128)S(1)} %shard_map.201), channel_id=1, source_target_pairs={{0,1},{1,0},{2,3},{3,2},{4,5},{5,4},{6,7},{7,6},{8,9},{9,8},{10,11... | collective-permute-start | bytes 159752 | tf_op jit(solution)/shard_map/ppermute | solution.py:27
  12.7 3.2 %collective-permute-start.3 = (f32[4,104,128]{2,1,0:T(8,128)S(1)}, f32[4,104,128]{2,1,0:T(8,128)S(1)}, u32[]{:S(2)}, u32[]{:S(2)}) collective-permute-start(f32[4,104,128]{2,1,0:T(8,128)S(1)} %pad_maximum_fusion.3), channel_id=1, source_target_pairs={{0,4},{4,0},{8,12},{12,8},{16,20},{20,16},{24,28},{28,24},{32,36},... | collective-permute-start | bytes 638984 | tf_op jit(solution)/shard_map/ppermute | solution.py:27
  15.9 9.3 %collective-permute-start.5 = (f32[2,4,40,128]{3,2,1,0:T(8,128)S(1)}, f32[2,4,40,128]{3,2,1,0:T(8,128)S(1)}, u32[]{:S(2)}, u32[]{:S(2)}) collective-permute-start(f32[2,4,40,128]{3,2,1,0:T(8,128)S(1)} %pad_maximum_fusion.4.pair.spair), channel_id=1, source_target_pairs={{0,244},{4,16},{8,252},{12,24},{16,4},{20,32},{24,12},{28,40},{32,... | collective-permute-start | bytes 491528 | tf_op jit(solution)/shard_map/ppermute | solution.py:27
  19.2 10.8 %collective-permute-start.4 = (f32[2,4,40,128]{3,2,1,0:T(8,128)S(1)}, f32[2,4,40,128]{3,2,1,0:T(8,128)S(1)}, u32[]{:S(2)}, u32[]{:S(2)}) collective-permute-start(f32[2,4,40,128]{3,2,1,0:T(8,128)S(1)} %pad_maximum_fusion.4.pair.spair), channel_id=1, source_target_pairs={{0,252},{4,8},{8,4},{12,16},{16,12},{20,24},{24,20},{28,32},{32,28... | collective-permute-start | bytes 491528 | tf_op jit(solution)/shard_map/ppermute | solution.py:27
  25.2 8.2 %collective-permute-start.7 = (f32[2,4,40,128]{3,2,1,0:T(8,128)S(1)}, f32[2,4,40,128]{3,2,1,0:T(8,128)S(1)}, u32[]{:S(2)}, u32[]{:S(2)}) collective-permute-start(f32[2,4,40,128]{3,2,1,0:T(8,128)S(1)} %collective-permute-done.5.a3), channel_id=1, source_target_pairs={{0,4},{4,0},{8,12},{12,8},{16,20},{20,16},{24,28},{28,24},{32,36},... | collective-permute-start | bytes 491528 | tf_op jit(solution)/shard_map/ppermute | solution.py:27
  30.0 3.7 %collective-permute-start.6 = (f32[2,4,40,128]{3,2,1,0:T(8,128)S(1)}, f32[2,4,40,128]{3,2,1,0:T(8,128)S(1)}, u32[]{:S(2)}, u32[]{:S(2)}) collective-permute-start(f32[2,4,40,128]{3,2,1,0:T(8,128)S(1)} %collective-permute-done.4.a.sa), channel_id=1, source_target_pairs={{0,4},{4,0},{8,12},{12,8},{16,20},{20,16},{24,28},{28,24},{32,36},... | collective-permute-start | bytes 491528 | tf_op jit(solution)/shard_map/ppermute | solution.py:27
  33.7 0.9 copy-start.5
  34.6 0.8 copy-start.9
  35.4 48.5 %copy-start.11 = (s32[8,8,2]{1,2,0:T(2,128)S(1)}, s32[8,8,2]{1,2,0:T(2,128)}, u32[]{:S(2)}) copy-start(s32[8,8,2]{1,2,0:T(2,128)} %param.33) | copy-start | bytes 1540
  37.6 46.3 %copy-start.1 = (bf16[8,8,2,128,128]{4,3,2,1,0:T(8,128)(2,1)S(1)}, bf16[8,8,2,128,128]{4,3,2,1,0:T(8,128)(2,1)}, u32[]{:S(2)}) copy-start(bf16[8,8,2,128,128]{4,3,2,1,0:T(8,128)(2,1)} %blocks.3) | copy-start | bytes 12582916
  37.6 46.3 %copy-start.3 = (f32[8,8,16,128]{3,2,1,0:T(8,128)S(1)}, f32[8,8,16,128]{3,2,1,0:T(8,128)}, u32[]{:S(2)}) copy-start(f32[8,8,16,128]{3,2,1,0:T(8,128)} %guess.1) | copy-start | bytes 1572868
  37.6 4.1 %collective-permute-start.10 = (f32[64,128]{1,0:T(8,128)S(1)}, f32[64,128]{1,0:T(8,128)S(1)}, u32[]{:S(2)}, u32[]{:S(2)}) collective-permute-start(f32[64,128]{1,0:T(8,128)S(1)} %bitcast.29), channel_id=1, source_target_pairs={{0,3},{1,2},{2,1},{3,0},{4,7},{5,6},{6,5},{7,4},{8,11},{9,10},{10,... | collective-permute-start | bytes 98312 | tf_op jit(solution)/shard_map/ppermute | solution.py:27
  38.7 4.3 %collective-permute-start.9 = (f32[64,128]{1,0:T(8,128)S(1)}, f32[64,128]{1,0:T(8,128)S(1)}, u32[]{:S(2)}, u32[]{:S(2)}) collective-permute-start(f32[64,128]{1,0:T(8,128)S(1)} %bitcast.30), channel_id=1, source_target_pairs={{0,2},{1,3},{2,0},{3,1},{4,6},{5,7},{6,4},{7,5},{8,10},{9,11},{10,... | collective-permute-start | bytes 98312 | tf_op jit(solution)/shard_map/ppermute | solution.py:27
  39.5 3.5 %collective-permute-start.8 = (f32[64,128]{1,0:T(8,128)S(1)}, f32[64,128]{1,0:T(8,128)S(1)}, u32[]{:S(2)}, u32[]{:S(2)}) collective-permute-start(f32[64,128]{1,0:T(8,128)S(1)} %bitcast.31), channel_id=1, source_target_pairs={{0,1},{1,0},{2,3},{3,2},{4,5},{5,4},{6,7},{7,6},{8,9},{9,8},{10,11... | collective-permute-start | bytes 98312 | tf_op jit(solution)/shard_map/ppermute | solution.py:27
  43.0 3.1 %collective-permute-start.11 = (f32[4,64,128]{2,1,0:T(8,128)S(1)}, f32[4,64,128]{2,1,0:T(8,128)S(1)}, u32[]{:S(2)}, u32[]{:S(2)}) collective-permute-start(f32[4,64,128]{2,1,0:T(8,128)S(1)} %get-tuple-element.45), channel_id=1, source_target_pairs={{0,4},{4,0},{8,12},{12,8},{16,20},{20,16},{24,28},{28,24},{32,36},... | collective-permute-start | bytes 393224 | tf_op jit(solution)/shard_map/ppermute | solution.py:27
  45.2 6.2 %collective-permute-start.14 = (f32[2,4,64,128]{3,2,1,0:T(8,128)S(1)}, f32[2,4,64,128]{3,2,1,0:T(8,128)S(1)}, u32[]{:S(2)}, u32[]{:S(2)}) collective-permute-start(f32[2,4,64,128]{3,2,1,0:T(8,128)S(1)} %pad_maximum_fusion.2.fpair), channel_id=1, source_target_pairs={{0,252},{4,8},{8,4},{12,16},{16,12},{20,24},{24,20},{28,32},{32,28... | collective-permute-start | bytes 786440 | tf_op jit(solution)/shard_map/ppermute | solution.py:27
  46.2 8.3 %collective-permute-start.12 = (f32[2,4,64,128]{3,2,1,0:T(8,128)S(1)}, f32[2,4,64,128]{3,2,1,0:T(8,128)S(1)}, u32[]{:S(2)}, u32[]{:S(2)}) collective-permute-start(f32[2,4,64,128]{3,2,1,0:T(8,128)S(1)} %pad_maximum_fusion.1.pair), channel_id=1, source_target_pairs={{0,252},{4,8},{8,4},{12,16},{16,12},{20,24},{24,20},{28,32},{32,28... | collective-permute-start | bytes 786440 | tf_op jit(solution)/shard_map/ppermute | solution.py:27
  51.4 10.1 %collective-permute-start.15 = (f32[2,4,64,128]{3,2,1,0:T(8,128)S(1)}, f32[2,4,64,128]{3,2,1,0:T(8,128)S(1)}, u32[]{:S(2)}, u32[]{:S(2)}) collective-permute-start(f32[2,4,64,128]{3,2,1,0:T(8,128)S(1)} %collective-permute-done.14.fa), channel_id=1, source_target_pairs={{0,4},{4,0},{8,12},{12,8},{16,20},{20,16},{24,28},{28,24},{32,36},... | collective-permute-start | bytes 786440 | tf_op jit(solution)/shard_map/ppermute | solution.py:27
  54.4 7.1 %collective-permute-start.13 = (f32[2,4,64,128]{3,2,1,0:T(8,128)S(1)}, f32[2,4,64,128]{3,2,1,0:T(8,128)S(1)}, u32[]{:S(2)}, u32[]{:S(2)}) collective-permute-start(f32[2,4,64,128]{3,2,1,0:T(8,128)S(1)} %collective-permute-done.12.a), channel_id=1, source_target_pairs={{0,4},{4,0},{8,12},{12,8},{16,20},{20,16},{24,28},{28,24},{32,36},... | collective-permute-start | bytes 786440 | tf_op jit(solution)/shard_map/ppermute | solution.py:27
  58.1 0.9 copy-start.7
  59.1 0.7 copy-start.10
  60.0 9.5 %collective-permute-start.21 = (f32[544,128]{1,0:T(8,128)S(1)}, f32[544,128]{1,0:T(8,128)S(1)}, u32[]{:S(2)}, u32[]{:S(2)}) collective-permute-start(f32[544,128]{1,0:T(8,128)S(1)} %get-tuple-element.31), channel_id=1, source_target_pairs={{0,3},{1,2},{2,1},{3,0},{4,7},{5,6},{6,5},{7,4},{8,11},{9,10},{10,... | collective-permute-start | bytes 835592 | tf_op jit(solution)/shard_map/ppermute | solution.py:27
  61.5 8.0 %collective-permute-start.20 = (f32[544,128]{1,0:T(8,128)S(1)}, f32[544,128]{1,0:T(8,128)S(1)}, u32[]{:S(2)}, u32[]{:S(2)}) collective-permute-start(f32[544,128]{1,0:T(8,128)S(1)} %get-tuple-element.29), channel_id=1, source_target_pairs={{0,1},{1,0},{2,3},{3,2},{4,5},{5,4},{6,7},{7,6},{8,9},{9,8},{10,11... | collective-permute-start | bytes 835592 | tf_op jit(solution)/shard_map/ppermute | solution.py:27
  61.5 0.9 copy-start.6
  62.4 0.7 copy-start.14
  66.4 6.2 %collective-permute-start.17 = (f32[256,128]{1,0:T(8,128)S(1)}, f32[256,128]{1,0:T(8,128)S(1)}, u32[]{:S(2)}, u32[]{:S(2)}) collective-permute-start(f32[256,128]{1,0:T(8,128)S(1)} %bitcast.24), channel_id=1, source_target_pairs={{0,3},{1,2},{2,1},{3,0},{4,7},{5,6},{6,5},{7,4},{8,11},{9,10},{10,... | collective-permute-start | bytes 393224 | tf_op jit(solution)/shard_map/ppermute | solution.py:27
  68.1 4.5 %collective-permute-start.16 = (f32[256,128]{1,0:T(8,128)S(1)}, f32[256,128]{1,0:T(8,128)S(1)}, u32[]{:S(2)}, u32[]{:S(2)}) collective-permute-start(f32[256,128]{1,0:T(8,128)S(1)} %bitcast.25), channel_id=1, source_target_pairs={{0,1},{1,0},{2,3},{3,2},{4,5},{5,4},{6,7},{7,6},{8,9},{9,8},{10,11... | collective-permute-start | bytes 393224 | tf_op jit(solution)/shard_map/ppermute | solution.py:27
  69.6 10.1 %collective-permute-start.23 = (f32[1224,128]{1,0:T(8,128)S(1)}, f32[1224,128]{1,0:T(8,128)S(1)}, u32[]{:S(2)}, u32[]{:S(2)}) collective-permute-start(f32[1224,128]{1,0:T(8,128)S(1)} %get-tuple-element.35), channel_id=1, source_target_pairs={{0,252},{4,8},{8,4},{12,16},{16,12},{20,24},{24,20},{28,32},{32,28... | collective-permute-start | bytes 1880072 | tf_op jit(solution)/shard_map/ppermute | solution.py:27
  69.7 10.0 %collective-permute-start.22 = (f32[1224,128]{1,0:T(8,128)S(1)}, f32[1224,128]{1,0:T(8,128)S(1)}, u32[]{:S(2)}, u32[]{:S(2)}) collective-permute-start(f32[1224,128]{1,0:T(8,128)S(1)} %get-tuple-element.33), channel_id=1, source_target_pairs={{0,4},{4,0},{8,12},{12,8},{16,20},{20,16},{24,28},{28,24},{32,36},... | collective-permute-start | bytes 1880072 | tf_op jit(solution)/shard_map/ppermute | solution.py:27
  72.6 11.3 %collective-permute-start.19 = (f32[768,128]{1,0:T(8,128)S(1)}, f32[768,128]{1,0:T(8,128)S(1)}, u32[]{:S(2)}, u32[]{:S(2)}) collective-permute-start(f32[768,128]{1,0:T(8,128)S(1)} %pad_maximum_fusion), channel_id=1, source_target_pairs={{0,252},{4,8},{8,4},{12,16},{16,12},{20,24},{24,20},{28,32},{32,28... | collective-permute-start | bytes 1179656 | tf_op jit(solution)/shard_map/ppermute | solution.py:27
  72.7 11.2 %collective-permute-start.18 = (f32[768,128]{1,0:T(8,128)S(1)}, f32[768,128]{1,0:T(8,128)S(1)}, u32[]{:S(2)}, u32[]{:S(2)}) collective-permute-start(f32[768,128]{1,0:T(8,128)S(1)} %pad_maximum_fusion), channel_id=1, source_target_pairs={{0,4},{4,0},{8,12},{12,8},{16,20},{20,16},{24,28},{28,24},{32,36},... | collective-permute-start | bytes 1179656 | tf_op jit(solution)/shard_map/ppermute | solution.py:27
  90.3 4.6 %collective-permute-start.24 = (f32[384,128]{1,0:T(8,128)S(1)}, f32[384,128]{1,0:T(8,128)S(1)}, u32[]{:S(2)}, u32[]{:S(2)}) collective-permute-start(f32[384,128]{1,0:T(8,128)S(1)} %get-tuple-element.37), channel_id=1, source_target_pairs={{0,1},{1,0},{2,3},{3,2},{4,5},{5,4},{6,7},{7,6},{8,9},{9,8},{10,11... | collective-permute-start | bytes 589832 | tf_op jit(solution)/shard_map/ppermute | solution.py:27
  90.6 5.7 %collective-permute-start.25 = (f32[384,128]{1,0:T(8,128)S(1)}, f32[384,128]{1,0:T(8,128)S(1)}, u32[]{:S(2)}, u32[]{:S(2)}) collective-permute-start(f32[384,128]{1,0:T(8,128)S(1)} %get-tuple-element.38), channel_id=1, source_target_pairs={{0,3},{1,2},{2,1},{3,0},{4,7},{5,6},{6,5},{7,4},{8,11},{9,10},{10,... | collective-permute-start | bytes 589832 | tf_op jit(solution)/shard_map/ppermute | solution.py:27
  96.3 6.8 %collective-permute-start.26 = (f32[672,128]{1,0:T(8,128)S(1)}, f32[672,128]{1,0:T(8,128)S(1)}, u32[]{:S(2)}, u32[]{:S(2)}) collective-permute-start(f32[672,128]{1,0:T(8,128)S(1)} %get-tuple-element.39), channel_id=1, source_target_pairs={{0,4},{4,0},{8,12},{12,8},{16,20},{20,16},{24,28},{28,24},{32,36},... | collective-permute-start | bytes 1032200 | tf_op jit(solution)/shard_map/ppermute | solution.py:27
  101.9 7.0 %collective-permute-start.27 = (f32[672,128]{1,0:T(8,128)S(1)}, f32[672,128]{1,0:T(8,128)S(1)}, u32[]{:S(2)}, u32[]{:S(2)}) collective-permute-start(f32[672,128]{1,0:T(8,128)S(1)} %get-tuple-element.40), channel_id=1, source_target_pairs={{0,252},{4,8},{8,4},{12,16},{16,12},{20,24},{24,20},{28,32},{32,28... | collective-permute-start | bytes 1032200 | tf_op jit(solution)/shard_map/ppermute | solution.py:27

commit v2 on v1

--- a/solution.py
+++ b/solution.py
@@ -126,6 +126,7 @@
 def call(kernel, inputs, outs, scratch, flops, vmem=16, hbm=()):
     nbytes = sum(x.size * x.dtype.itemsize for x in inputs)
     specs = [HBM if n in hbm else VMEM for n in range(len(inputs))]
+    inputs = [pltpu.with_memory_space_constraint(x, pltpu.HBM) if n in hbm else x for n, x in enumerate(inputs)]
     return pl.pallas_call(
         kernel,
         out_shape=outs,
@@ -162,97 +163,38 @@
         copy.wait()
 
 
-def fourth_kernel(pair, a, a3, b, b3, links_h, blocks_h, guess_h, out, start, u, f, s, res, d0, d1, lines, blocks, guess, links, sems):
-    copies = fetch(sems, (blocks_h, blocks), (guess_h, guess), (links_h, links))
-    gz, gy = lax.axis_index("gz"), lax.axis_index("gy")
-    core = lax.rem(gz, 2)
-
-    def place(ref, chip, first_bit):
-        for slot in range(2):
-            bit = first_bit if slot == 0 else 1 - first_bit
-            row = chip * 2 + bit
-            for k in range(4):
-                col = lax.bitwise_xor(gy, k)
-                f[row, col] = ref[slot, k, 0:16, :]
-                u[row, col] = ref[slot, k, 16:32, :]
-                s[row, col] = ref[slot, k, 32:33, :]
-
-    place(pair, 2, core)
-    place(a, 1 + 2 * core, 1 - core)
-    place(b, 3 - 2 * core, core)
-    place(a3, 4 * core, 1 - core)
-    place(b3, 4 - 4 * core, core)
-
-    def emit(i, j, value):
-        lines[i - 3 - core, j] = value.astype(BF16)
-        res[i, j] = value
-
-    smooth(u, f, s, res, d0, d1, emit, core, 3, 4, True)
-    out[0, 0] = res[4 + core, gy]
-
-    for copy in copies:
+THIRD = 1232
+
+
+def ahead_kernel(
+    source_first_h, shift_first_h, source_second_h, shift_second_h, blocks_third, guess_third_h, links_third,
+    third, own, even, odd, row_on, row_off,
+    source_first, shift_first, source_second, shift_second, guess_third, links, sems,
+):
+    pairs = [
+        (links_third, links), (guess_third_h, guess_third), (source_second_h, source_second), (shift_second_h, shift_second),
+        (shift_first_h, shift_first), (source_first_h, source_first),
+    ]
+    for c in range(8):
+        pairs.append((blocks_third.at[c // 4, c // 2 % 2, c % 2], third.at[c * L : (c + 1) * L]))
+    copies = fetch(sems, *pairs)
+    for copy in copies[:6]:
         copy.wait()
-
-    def index(i, j, k):
-        q = links[i, k, j]
-        return lax.rem(q // 4 - gz + 1 + NZ, NZ), lax.rem(q, 4)
-
     for i in range(2):
         for j in range(2):
-            start[i, j] = prolong_cell(lines, index, blocks, guess, i, j)
-
-
-def third_kernel(pair, a, b, fpair, fa, fb, spair, sa, sb, links_h, blocks, guess_h, out, start, u, f, s, res, d0, d1, lines, guess, links, sems):
-    copies = fetch(sems, (guess_h, guess), (links_h, links))
-    gz, gy = lax.axis_index("gz"), lax.axis_index("gy")
-    core = lax.rem(gz, 2)
-
-    def place(ref, fref, sref, chip, first_bit):
-        for slot in range(2):
-            bit = first_bit if slot == 0 else 1 - first_bit
-            for k in range(4):
-                col = lax.bitwise_xor(gy, k) * 2
-                for i in range(2):
-                    row = chip * 4 + bit * 2 + i
-                    for j in range(2):
-                        at = (i * 2 + j) * R
-                        u[row, col + j] = ref[slot, k, at : at + R, :]
-                        f[row, col + j] = fref[slot, k, at : at + R, :]
-                        s[row, col + j] = sref[slot, k, 33 + i * 2 + j : 34 + i * 2 + j, :]
-
-    place(pair, fpair, spair, 1, core)
-    place(a, fa, sa, 2 * core, 1 - core)
-    place(b, fb, sb, 2 - 2 * core, core)
-
-    def emit(i, j, value):
-        lines[i - 3 - 2 * core, j] = value.astype(BF16)
-        res[i, j] = value
-
-    smooth(u, f, s, res, d0, d1, emit, 2 * core, 4, 8, True)
-    for i in range(2):
-        for j in range(2):
-            out[i, j] = res[4 + 2 * core + i, 2 * gy + j]
-
-    for copy in copies:
-        copy.wait()
-
-    def index(i, j, k):
-        q = links[i, k, j]
-        return lax.rem(q // 8 - 2 * gz + 1 + 2 * NZ, 2 * NZ), lax.rem(q, 8)
-
-    for i in range(4):
-        for j in range(4):
-            start[i, j] = prolong_cell(lines, index, blocks, guess, i, j)
-
-
-ALONG_Y, ALONG_Z = 544, 1224
-
-
-def along_y_kernel(source_first, shift_first, source_second_h, shift_second_h, own, even, odd, source_second, shift_second, sems):
-    copies = fetch(sems, (source_second_h, source_second), (shift_second_h, shift_second))
-    side = lax.rem(lax.axis_index("gy"), 2)
-    for copy in copies:
-        copy.wait()
+            rest = guess_third[i, j]
+            for n in range(3):
+                term = rest.astype(BF16)
+                at = 1024 + n * 64 + (i * 2 + j) * R
+                third[at : at + R, :] = term
+                rest = rest - term.astype(F32)
+    names = lax.broadcasted_iota(jnp.int32, (16, L), 0)
+    rows = jnp.zeros((16, L), jnp.int32)
+    for c in range(8):
+        rows = jnp.where(names == c, links[c // 4, c // 2 % 2, c % 2], rows)
+    third[1216:1232, :] = rows.astype(F32).astype(BF16)
+
+    side, core = lax.rem(lax.axis_index("gy"), 2), lax.rem(lax.axis_index("gz"), 2)
     for i in range(4):
         for j in range(4):
             at = (i * 4 + j) * R
@@ -265,20 +207,124 @@
                 at = 272 + (i * 2 + j) * R
                 ref[at : at + R, :] = source_first[i, first + j]
             ref[528 + i * 2 : 530 + i * 2, :] = jnp.where(first == 0, shift_first[i, 0:2, :], shift_first[i, 6:8, :])
-
-
-def along_z_kernel(source_first, shift_first, own, even, odd, on, off):
+    for ref, first in ((row_on, 6 - 6 * core), (row_off, 6 * core)):
+        for i in range(2):
+            for j in range(8):
+                at = (i * 8 + j) * R
+                ref[at : at + R, :] = source_first[first + i, j]
+            ref[256 + i * 8 : 264 + i * 8, :] = shift_first[first + i]
+    for copy in copies[6:]:
+        copy.wait()
+
+
+def fourth_kernel(pair, a, a3, b, b3, third0, third1, third2, third3, out, start, u, f, s, res, d0, d1, lines):
+    gz, gy = lax.axis_index("gz"), lax.axis_index("gy")
+    core = lax.rem(gz, 2)
+
+    def place(ref, chip, first_bit):
+        for slot in range(2):
+            bit = first_bit if slot == 0 else 1 - first_bit
+            row = chip * 2 + bit
+            for k in range(4):
+                col = lax.bitwise_xor(gy, k)
+                f[row, col] = ref[slot, k, 0:16, :]
+                u[row, col] = ref[slot, k, 16:32, :]
+                s[row, col] = ref[slot, k, 32:33, :]
+
+    place(pair, 2, core)
+    place(a, 1 + 2 * core, 1 - core)
+    place(b, 3 - 2 * core, core)
+    place(a3, 4 * core, 1 - core)
+    place(b3, 4 - 4 * core, core)
+
+    def emit(i, j, value):
+        lines[i - 3 - core, j] = value.astype(BF16).astype(F32)
+        res[i, j] = value
+
+    smooth(u, f, s, res, d0, d1, emit, core, 3, 4, True)
+    out[0, 0] = res[4 + core, gy]
+
+    for n, ref in enumerate((third0, third1, third2, third3)):
+        col = lax.bitwise_xor(gy, n) * 2
+        for c in range(4):
+            i, j = c // 2, c % 2
+            at = 1024 + c * R
+            total = (ref[at : at + R, :].astype(F32) + ref[at + 64 : at + 64 + R, :].astype(F32)) + ref[at + 128 : at + 128 + R, :].astype(F32)
+            names = ref[1216:1232, :].astype(F32)
+            for k in range(2):
+                name = names[c * 2 + k : c * 2 + k + 1, :]
+                line = jnp.zeros((R, L), F32)
+                for row in range(3):
+                    base = (lax.rem(gz + row - 1 + NZ, NZ) * 4).astype(F32)
+                    for x in range(4):
+                        line = jnp.where(jnp.broadcast_to(name == base + x, (R, L)), lines[row, x], line)
+                at = (c * 2 + k) * L
+                total = total + lax.dot_general(
+                    line.astype(BF16), ref[at : at + L, :], (((1,), (1,)), ((), ())), preferred_element_type=F32
+                )
+            start[pl.ds(pl.multiple_of((i * 8 + col + j) * R, R), R), :] = total
+
+
+def third_kernel(pair, a, b, fpair, fa, fb, spair, sa, sb, links_h, blocks, guess_h, out, start, u, f, s, res, d0, d1, lines, guess, links, sems):
+    copies = fetch(sems, (guess_h, guess), (links_h, links))
+    gz, gy = lax.axis_index("gz"), lax.axis_index("gy")
+    core = lax.rem(gz, 2)
+
+    def place(ref, fref, sref, chip, first_bit):
+        for slot in range(2):
+            bit = first_bit if slot == 0 else 1 - first_bit
+            for k in range(4):
+                col = lax.bitwise_xor(gy, k) * 2
+                for i in range(2):
+                    row = chip * 4 + bit * 2 + i
+                    for j in range(2):
+                        at = (i * 2 + j) * R
+                        f[row, col + j] = fref[slot, k, at : at + R, :]
+                        s[row, col + j] = sref[slot, k, 33 + i * 2 + j : 34 + i * 2 + j, :]
+            for i in range(2):
+                for j in range(8):
+                    at = (i * 8 + j) * R
+                    u[chip * 4 + bit * 2 + i, j] = ref[slot, at : at + R, :]
+
+    place(pair, fpair, spair, 1, core)
+    place(a, fa, sa, 2 * core, 1 - core)
+    place(b, fb, sb, 2 - 2 * core, core)
+
+    def emit(i, j, value):
+        lines[i - 3 - 2 * core, j] = value.astype(BF16)
+        res[i, j] = value
+
+    smooth(u, f, s, res, d0, d1, emit, 2 * core, 4, 8, True)
+    for i in range(2):
+        for j in range(2):
+            out[i, j] = res[4 + 2 * core + i, 2 * gy + j]
+
+    for copy in copies:
+        copy.wait()
+
+    def index(i, j, k):
+        q = links[i, k, j]
+        return lax.rem(q // 8 - 2 * gz + 1 + 2 * NZ, 2 * NZ), lax.rem(q, 8)
+
+    for i in range(4):
+        for j in range(4):
+            start[i, j] = prolong_cell(lines, index, blocks, guess, i, j)
+
+
+ALONG_Y, ALONG_Z = 544, 1224
+
+
+def along_z_kernel(own, even, odd, row_on, row_off, on, off):
     core = lax.rem(lax.axis_index("gz"), 2)
-    for ref, first in ((on, 6 - 6 * core), (off, 6 * core)):
+    for ref, rows, first in ((on, row_on, 6 - 6 * core), (off, row_off, 6 * core)):
         ref[0:272, :] = own[...]
         ref[272:544, :] = even[0:272, :]
         ref[544:816, :] = odd[0:272, :]
         for i in range(2):
             row = first + i
-            for j in range(8):
-                at = 816 + (i * 12 + j) * R
-                ref[at : at + R, :] = source_first[row, j]
-            ref[1200 + i * 12 : 1208 + i * 12, :] = shift_first[row]
+            at = 816 + i * 12 * R
+            ref[at : at + 8 * R, :] = rows[i * 8 * R : (i + 1) * 8 * R, :]
+            ref[1200 + i * 12 : 1208 + i * 12, :] = rows[256 + i * 8 : 264 + i * 8, :]
             for n, side_ref in enumerate((even, odd)):
                 at = 816 + (i * 12 + 8 + 2 * n) * R
                 ref[at : at + 2 * R, :] = side_ref[pl.ds(pl.multiple_of(272 + row * 2 * R, 8), 2 * R), :]
@@ -416,51 +462,62 @@
     blocks_first, blocks_second, blocks_third,
     links_first, links_second, links_third,
 ):
-    links_first, links_second, links_third = (x.transpose(0, 2, 1) for x in (links_first, links_second, links_third))
-
-    (pack,) = call(pack_kernel, (source_fourth, guess_fourth, shift_fourth, shift_third, source_third), (sds(104, L),), [pltpu.VMEM((1, 1, L), F32), pltpu.VMEM((2, 2, L), F32), pltpu.SemaphoreType.DMA((8,))], 1000, 2, range(5))
-    y1, y2, y3 = y_by(pack, 1), y_by(pack, 2), y_by(pack, 3)
+    links_first, links_second = links_first.transpose(0, 2, 1), links_second.transpose(0, 2, 1)
+
+    (pack,) = call(
+        pack_kernel,
+        (source_fourth, guess_fourth, shift_fourth, shift_third, source_third),
+        (sds(104, L),),
+        [pltpu.VMEM((1, 1, L), F32), pltpu.VMEM((2, 2, L), F32), pltpu.SemaphoreType.DMA((8,))],
+        1000, 2, range(5),
+    )
+    y1 = y_by(pack, 1)
+    y2 = y_by(pack, 2)
+    y3 = y_by(pack, 3)
     line = jnp.stack([pack, y1, y2, y3])
     line_on = z_on(line)
     pair = jnp.stack([line[:, :40], line_on[:, :40]])
     pair_f = jnp.stack([line[:, 40:], line_on[:, 40:]])
     near = z_off(pair)
     far = z_off3(pair)
-
-    mine, ahead_even, ahead_odd = call(
-        along_y_kernel,
-        (source_first, shift_first, source_second, shift_second),
-        (sds(272, L), sds(ALONG_Y, L), sds(ALONG_Y, L)),
-        fetched(source_second, shift_second), 10000, 4, (2, 3),
-    )
+    near_b = z_on(near)
+    far_b = z_on(far)
+    near_f = z_off(pair_f)
+    near_fb = z_on(near_f)
+
+    third, mine, ahead_even, ahead_odd, row_on, row_off = call(
+        ahead_kernel,
+        (source_first, shift_first, source_second, shift_second, blocks_third, guess_third, links_third),
+        (sds(THIRD, L, dtype=BF16), sds(272, L), sds(ALONG_Y, L), sds(ALONG_Y, L), sds(272, L), sds(272, L)),
+        [pltpu.VMEM(x.shape, x.dtype) for x in (source_first, shift_first, source_second, shift_second, guess_third)]
+        + [pltpu.SMEM(links_third.shape, jnp.int32), pltpu.SemaphoreType.DMA((16,))],
+        1000, 6, range(7),
+    )
+    third1 = y_by(third, 1)
+    third2 = y_by(third, 2)
+    third3 = y_by(third, 3)
     ahead_even, ahead_odd = y_even(after(ahead_even, y1, y2, y3)), y_odd(after(ahead_odd, y1, y2, y3))
     ahead_on, ahead_off = call(
         along_z_kernel,
-        (source_first, shift_first, mine, ahead_even, ahead_odd),
+        (mine, ahead_even, ahead_odd, row_on, row_off),
         (sds(ALONG_Z, L), sds(ALONG_Z, L)),
         [], 10000, 6,
     )
-
-    near_b, far_b = z_on(near), z_on(far)
-    near_f = z_off(after(pair_f, near, far))
-    near_fb = z_on(near_f)
-    ahead_on = z_on(after(ahead_on, near_b, far_b))
-    ahead_off = z_off(after(ahead_off, near_b, far_b))
+    ahead_on = z_on(ahead_on)
+    ahead_off = z_off(ahead_off)
 
     def smoothing_scratch(rows, cols):
         return [cells(rows, cols), cells(rows, cols), shifts(rows, cols)] + [cells(rows, cols)] * 3
 
     out_fourth, start_third = call(
         fourth_kernel,
-        (pair, near, far, near_b, far_b, links_third, blocks_third, guess_third),
-        (sds(1, 1, R, L), sds(2, 2, R, L)),
-        smoothing_scratch(10, 4) + [cells(3, 4, BF16)] + smem_last(blocks_third, guess_third, links_third),
-        4_000_000, 6, (5, 6, 7),
-    )
-
-    own = flat(start_third)
-    line3 = jnp.stack([own, y_by(own, 1), y_by(own, 2), y_by(own, 3)])
-    pair3 = jnp.stack([line3, z_on(line3)])
+        (pair, near, far, near_b, far_b, third, third1, third2, third3),
+        (sds(1, 1, R, L), sds(256, L)),
+        smoothing_scratch(10, 4) + [cells(3, 4)],
+        4_000_000, 6,
+    )
+
+    pair3 = jnp.stack([start_third, z_on(start_third)])
     near3 = z_off(pair3)
     near3_b = z_on(near3)
     out_third, start_second = call(

time: 114 us -> 111 us (0.974)
  waiting for transfers between devices: 33.9 us -> 45.8 us
  local copies, waits for them, and re-layouts: 9.32 us -> 0.06 us
  starting transfers between devices: 52.3 us -> 45 us
  Pallas kernels: 16.8 us -> 19 us
    ppermute x28, waiting for transfers between devices: 33.9 us -> 45.8 us  [swap(): lax.ppermute(x, axis, [(i, partner(i)) for i in range(lax.axis_size(axis))])]
    unnamed x35 -> x10, local copies, waits for them, and re-layouts: 9.29 us -> 0.03 us
    ppermute x28, starting transfers between devices: 52.3 us -> 45 us  [swap(): lax.ppermute(x, axis, [(i, partner(i)) for i in range(lax.axis_size(axis))])]
    pallas_call x8, Pallas kernels: 16.8 us -> 19 us  [call(): pl.pallas_call(kernel, out_shape=outs, in_specs=specs, out_specs=jax.tree...]
  transfers between devices with their start and end apart: 28 -> 28, of which waited for: 17 -> 15; matrix products, arithmetic and copies ran while one was open for 1% -> 0% of each run, Pallas kernels for 3% -> 4%
where the time goes in v2:
time: 111 us
  waiting for transfers between devices  45.8 us (41%)
  starting transfers between devices  45 us (41%)
  Pallas kernels  19 us (17%)
    ppermute x28, waiting for transfers between devices, swap(): lax.ppermute(x, axis, [(i, partner(i)) for i in range(lax.axis_size(axis))])  45.8 us
    ppermute x28, starting transfers between devices, swap(): lax.ppermute(x, axis, [(i, partner(i)) for i in range(lax.axis_size(axis))])  45 us
    pallas_call x8, Pallas kernels, call(): pl.pallas_call(kernel, out_shape=outs, in_specs=specs, out_specs=jax.tree...  19 us
  transfers between devices with their start and end apart: 28, of which 15 were waited for; matrix products, arithmetic and copies ran while one was open for 0% of the time, Pallas kernels for 4%

profile of v2, /device:TPU:1, one launch (start us, length us, event | category | flops | bytes accessed | tf_op | source)
XLA Modules:
  0.0 110.8 jit_solution(7678827841602814671)
XLA Ops:
  0.6 1.0 shard_map.201
  1.6 3.6 %collective-permute-start.2 = (f32[104,128]{1,0:T(8,128)S(1)}, f32[104,128]{1,0:T(8,128)S(1)}, u32[]{:S(2)}, u32[]{:S(2)}) collective-permute-start(f32[104,128]{1,0:T(8,128)S(1)} %shard_map.201), channel_id=1, source_target_pairs={{0,3},{1,2},{2,1},{3,0},{4,7},{5,6},{6,5},{7,4},{8,11},{9,10},{10,... | collective-permute-start | bytes 159752 | tf_op jit(solution)/shard_map/ppermute | solution.py:27
  5.3 0.3 collective-permute-start.1
  5.6 0.3 collective-permute-start
  5.9 0.8 collective-permute-done.2
  6.8 3.1 %collective-permute-done.1 = f32[104,128]{1,0:T(8,128)S(1)} collective-permute-done((f32[104,128]{1,0:T(8,128)S(1)}, f32[104,128]{1,0:T(8,128)S(1)}, u32[]{:S(2)}, u32[]{:S(2)}) %collective-permute-start.1) | collective-permute-done | bytes 53280 | tf_op jit(solution)/shard_map/ppermute | solution.py:27
  9.9 2.1 %collective-permute-start.3 = (f32[4,104,128]{2,1,0:T(8,128)S(1)}, f32[4,104,128]{2,1,0:T(8,128)S(1)}, u32[]{:S(2)}, u32[]{:S(2)}) collective-permute-start(f32[4,104,128]{2,1,0:T(8,128)S(1)} %pad_maximum_fusion.3), channel_id=1, source_target_pairs={{0,4},{4,0},{8,12},{12,8},{16,20},{20,16},{24,28},{28,24},{32,36},... | collective-permute-start | bytes 638984 | tf_op jit(solution)/shard_map/ppermute | solution.py:27
  12.0 1.1 collective-permute-done.3
  13.1 3.3 %collective-permute-start.5 = (f32[2,4,40,128]{3,2,1,0:T(8,128)S(1)}, f32[2,4,40,128]{3,2,1,0:T(8,128)S(1)}, u32[]{:S(2)}, u32[]{:S(2)}) collective-permute-start(f32[2,4,40,128]{3,2,1,0:T(8,128)S(1)} %pad_maximum_fusion.4.pair.spair), channel_id=1, source_target_pairs={{0,244},{4,16},{8,252},{12,24},{16,4},{20,32},{24,12},{28,40},{32,... | collective-permute-start | bytes 491528 | tf_op jit(solution)/shard_map/ppermute | solution.py:27
  16.4 6.0 %collective-permute-start.4 = (f32[2,4,40,128]{3,2,1,0:T(8,128)S(1)}, f32[2,4,40,128]{3,2,1,0:T(8,128)S(1)}, u32[]{:S(2)}, u32[]{:S(2)}) collective-permute-start(f32[2,4,40,128]{3,2,1,0:T(8,128)S(1)} %pad_maximum_fusion.4.pair.spair), channel_id=1, source_target_pairs={{0,252},{4,8},{8,4},{12,16},{16,12},{20,24},{24,20},{28,32},{32,28... | collective-permute-start | bytes 491528 | tf_op jit(solution)/shard_map/ppermute | solution.py:27
  22.4 1.4 %shard_map.202 = (bf16[1232,128]{1,0:T(8,128)(2,1)S(1)}, f32[272,128]{1,0:T(8,128)S(1)}, f32[544,128]{1,0:T(8,128)S(1)}, f32[544,128]{1,0:T(8,128)S(1)}, f32[272,128]{1,0:T(8,128)S(1)}, /*index=5*/f32[272,128]{1,0:T(8,128)S(1)}) custom-call(f32[8,8,16,128]{3,2,1,0:T(8,128)} %fown.1, f32[8,8,128]{2,1,0:T(8,128)} %sown.1, f32[4,4,16,128]{3,2,1,0:T(8,128)} %source_second_h.1, ...), custom_call_target="tpu_custom_call" | custom-call | flops 1000 | bytes 991264 | tf_op jit(solution)/shard_map/pallas_call | solution.py:130
  23.8 1.1 %collective-permute-start.10 = (bf16[1232,128]{1,0:T(8,128)(2,1)S(1)}, bf16[1232,128]{1,0:T(8,128)(2,1)S(1)}, u32[]{:S(2)}, u32[]{:S(2)}) collective-permute-start(bf16[1232,128]{1,0:T(8,128)(2,1)S(1)} %get-tuple-element.24.third0), channel_id=1, source_target_pairs={{0,3},{1,2},{2,1},{3,0},{4,7},{5,6},{6,5},{7,4},{8,11},{9,10},{10,... | collective-permute-start | bytes 946184 | tf_op jit(solution)/shard_map/ppermute | solution.py:27
  24.9 0.8 collective-permute-start.9
  25.7 1.4 %collective-permute-start.8 = (bf16[1232,128]{1,0:T(8,128)(2,1)S(1)}, bf16[1232,128]{1,0:T(8,128)(2,1)S(1)}, u32[]{:S(2)}, u32[]{:S(2)}) collective-permute-start(bf16[1232,128]{1,0:T(8,128)(2,1)S(1)} %get-tuple-element.24.third0), channel_id=1, source_target_pairs={{0,1},{1,0},{2,3},{3,2},{4,5},{5,4},{6,7},{7,6},{8,9},{9,8},{10,11... | collective-permute-start | bytes 946184 | tf_op jit(solution)/shard_map/ppermute | solution.py:27
  27.1 0.2 collective-permute-start.7
  27.4 2.5 %collective-permute-start.6 = (f32[2,4,40,128]{3,2,1,0:T(8,128)S(1)}, f32[2,4,40,128]{3,2,1,0:T(8,128)S(1)}, u32[]{:S(2)}, u32[]{:S(2)}) collective-permute-start(f32[2,4,40,128]{3,2,1,0:T(8,128)S(1)} %collective-permute-done.4.a.sa), channel_id=1, source_target_pairs={{0,4},{4,0},{8,12},{12,8},{16,20},{20,16},{24,28},{28,24},{32,36},... | collective-permute-start | bytes 491528 | tf_op jit(solution)/shard_map/ppermute | solution.py:27
  29.9 11.1 %collective-permute-done.10.third3 = bf16[1232,128]{1,0:T(8,128)(2,1)S(1)} collective-permute-done((bf16[1232,128]{1,0:T(8,128)(2,1)S(1)}, bf16[1232,128]{1,0:T(8,128)(2,1)S(1)}, u32[]{:S(2)}, u32[]{:S(2)}) %collective-permute-start.10) | collective-permute-done | bytes 315424 | tf_op jit(solution)/shard_map/ppermute | solution.py:27
  41.0 0.8 collective-permute-done.8.third1
  41.8 2.6 %shard_map.203 = (f32[1,1,16,128]{3,2,1,0:T(8,128)}, f32[256,128]{1,0:T(8,128)S(1)}) custom-call(f32[2,4,40,128]{3,2,1,0:T(8,128)S(1)} %pad_maximum_fusion.4.pair.spair, f32[2,4,40,128]{3,2,1,0:T(8,128)S(1)} %collective-permute-done.4.a.sa, f32[2,4,40,128]{3,2,1,0:T(8,128)S(1)} %collective-permute-done.5.a3, ...), custom_call_target="tpu_custom_call" | custom-call | flops 4000000 | bytes 2080768 | tf_op jit(solution)/shard_map/pallas_call | solution.py:130
  44.4 0.5 collective-permute-start.11
  45.0 0.1 collective-permute-start.14
  45.1 0.8 collective-permute-done.11
  45.9 1.0 collective-permute-start.12
  46.9 4.2 %collective-permute-done.14.fa = f32[2,4,64,128]{3,2,1,0:T(8,128)S(1)} collective-permute-done((f32[2,4,64,128]{3,2,1,0:T(8,128)S(1)}, f32[2,4,64,128]{3,2,1,0:T(8,128)S(1)}, u32[]{:S(2)}, u32[]{:S(2)}) %collective-permute-start.14) | collective-permute-done | bytes 262176 | tf_op jit(solution)/shard_map/ppermute | solution.py:27
  51.1 3.0 %collective-permute-start.15 = (f32[2,4,64,128]{3,2,1,0:T(8,128)S(1)}, f32[2,4,64,128]{3,2,1,0:T(8,128)S(1)}, u32[]{:S(2)}, u32[]{:S(2)}) collective-permute-start(f32[2,4,64,128]{3,2,1,0:T(8,128)S(1)} %collective-permute-done.14.fa), channel_id=1, source_target_pairs={{0,4},{4,0},{8,12},{12,8},{16,20},{20,16},{24,28},{28,24},{32,36},... | collective-permute-start | bytes 786440 | tf_op jit(solution)/shard_map/ppermute | solution.py:27
  54.2 2.8 %collective-permute-start.13 = (f32[2,256,128]{2,1,0:T(8,128)S(1)}, f32[2,256,128]{2,1,0:T(8,128)S(1)}, u32[]{:S(2)}, u32[]{:S(2)}) collective-permute-start(f32[2,256,128]{2,1,0:T(8,128)S(1)} %collective-permute-done.12.a), channel_id=1, source_target_pairs={{0,4},{4,0},{8,12},{12,8},{16,20},{20,16},{24,28},{28,24},{32,36},... | collective-permute-start | bytes 786440 | tf_op jit(solution)/shard_map/ppermute | solution.py:27
  57.0 1.0 collective-permute-start.21
  58.0 0.4 collective-permute-start.20
  58.4 3.1 %shard_map.204 = (f32[2,2,16,128]{3,2,1,0:T(8,128)}, f32[4,4,16,128]{3,2,1,0:T(8,128)S(1)}) custom-call(f32[2,256,128]{2,1,0:T(8,128)S(1)} %pad_maximum_fusion.1.pair, f32[2,256,128]{2,1,0:T(8,128)S(1)} %collective-permute-done.12.a, f32[2,256,128]{2,1,0:T(8,128)S(1)} %collective-permute-done.13.b, f32[2,4,64,128]{3,2,1,0:T(8,128)S(1)} %pad_maximum_fusion.2.fpair, ...), custom_call_target="tpu_custom_call" | custom-call | flops 8000000 | bytes 3244160 | tf_op jit(solution)/shard_map/pallas_call | solution.py:130
  61.5 1.5 %collective-permute-start.17 = (f32[256,128]{1,0:T(8,128)S(1)}, f32[256,128]{1,0:T(8,128)S(1)}, u32[]{:S(2)}, u32[]{:S(2)}) collective-permute-start(f32[256,128]{1,0:T(8,128)S(1)} %bitcast.17), channel_id=1, source_target_pairs={{0,3},{1,2},{2,1},{3,0},{4,7},{5,6},{6,5},{7,4},{8,11},{9,10},{10,... | collective-permute-start | bytes 393224 | tf_op jit(solution)/shard_map/ppermute | solution.py:27
  63.0 0.9 collective-permute-start.16
  63.9 2.5 %collective-permute-done.21.odd.fodd = f32[544,128]{1,0:T(8,128)S(1)} collective-permute-done((f32[544,128]{1,0:T(8,128)S(1)}, f32[544,128]{1,0:T(8,128)S(1)}, u32[]{:S(2)}, u32[]{:S(2)}) %collective-permute-start.21) | collective-permute-done | bytes 278560 | tf_op jit(solution)/shard_map/ppermute | solution.py:27
  66.4 0.1 shard_map.205
  66.5 1.5 %collective-permute-start.22 = (f32[1224,128]{1,0:T(8,128)S(1)}, f32[1224,128]{1,0:T(8,128)S(1)}, u32[]{:S(2)}, u32[]{:S(2)}) collective-permute-start(f32[1224,128]{1,0:T(8,128)S(1)} %get-tuple-element.34), channel_id=1, source_target_pairs={{0,4},{4,0},{8,12},{12,8},{16,20},{20,16},{24,28},{28,24},{32,36},... | collective-permute-start | bytes 1880072 | tf_op jit(solution)/shard_map/ppermute | solution.py:27
  68.0 1.2 %collective-permute-done.17.own_odd = f32[256,128]{1,0:T(8,128)S(1)} collective-permute-done((f32[256,128]{1,0:T(8,128)S(1)}, f32[256,128]{1,0:T(8,128)S(1)}, u32[]{:S(2)}, u32[]{:S(2)}) %collective-permute-start.17) | collective-permute-done | bytes 131104 | tf_op jit(solution)/shard_map/ppermute | solution.py:27
  69.2 0.6 collective-permute-start.19
  69.9 3.4 %collective-permute-start.18 = (f32[768,128]{1,0:T(8,128)S(1)}, f32[768,128]{1,0:T(8,128)S(1)}, u32[]{:S(2)}, u32[]{:S(2)}) collective-permute-start(f32[768,128]{1,0:T(8,128)S(1)} %pad_maximum_fusion), channel_id=1, source_target_pairs={{0,4},{4,0},{8,12},{12,8},{16,20},{20,16},{24,28},{28,24},{32,36},... | collective-permute-start | bytes 1179656 | tf_op jit(solution)/shard_map/ppermute | solution.py:27
  73.3 4.7 %collective-permute-done.23.foff = f32[1224,128]{1,0:T(8,128)S(1)} collective-permute-done((f32[1224,128]{1,0:T(8,128)S(1)}, f32[1224,128]{1,0:T(8,128)S(1)}, u32[]{:S(2)}, u32[]{:S(2)}) %collective-permute-start.23) | collective-permute-done | bytes 626720 | tf_op jit(solution)/shard_map/ppermute | solution.py:27
  78.0 4.2 %collective-permute-done.19.off = f32[768,128]{1,0:T(8,128)S(1)} collective-permute-done((f32[768,128]{1,0:T(8,128)S(1)}, f32[768,128]{1,0:T(8,128)S(1)}, u32[]{:S(2)}, u32[]{:S(2)}) %collective-permute-start.19) | collective-permute-done | bytes 393248 | tf_op jit(solution)/shard_map/ppermute | solution.py:27
  82.2 6.4 %shard_map.206 = (f32[4,4,16,128]{3,2,1,0:T(8,128)}, f32[8,8,16,128]{3,2,1,0:T(8,128)S(1)}, f32[384,128]{1,0:T(8,128)S(1)}, f32[384,128]{1,0:T(8,128)S(1)}) custom-call(f32[256,128]{1,0:T(8,128)S(1)} %bitcast.20, f32[256,128]{1,0:T(8,128)S(1)} %collective-permute-done.16.own_even, f32[256,128]{1,0:T(8,128)S(1)} %collective-permute-done.17.own_odd, ...), custom_call_target="tpu_custom_call" | custom-call | flops 16000000 | bytes 7848448 | tf_op jit(solution)/shard_map/pallas_call | solution.py:130
  88.7 0.2 collective-permute-start.24
  88.9 1.6 %collective-permute-start.25 = (f32[384,128]{1,0:T(8,128)S(1)}, f32[384,128]{1,0:T(8,128)S(1)}, u32[]{:S(2)}, u32[]{:S(2)}) collective-permute-start(f32[384,128]{1,0:T(8,128)S(1)} %get-tuple-element.38), channel_id=1, source_target_pairs={{0,3},{1,2},{2,1},{3,0},{4,7},{5,6},{6,5},{7,4},{8,11},{9,10},{10,... | collective-permute-start | bytes 589832 | tf_op jit(solution)/shard_map/ppermute | solution.py:27
  90.5 2.8 %collective-permute-done.24.even = f32[384,128]{1,0:T(8,128)S(1)} collective-permute-done((f32[384,128]{1,0:T(8,128)S(1)}, f32[384,128]{1,0:T(8,128)S(1)}, u32[]{:S(2)}, u32[]{:S(2)}) %collective-permute-start.24) | collective-permute-done | bytes 196640 | tf_op jit(solution)/shard_map/ppermute | solution.py:27
  93.3 1.3 %collective-permute-done.25.odd = f32[384,128]{1,0:T(8,128)S(1)} collective-permute-done((f32[384,128]{1,0:T(8,128)S(1)}, f32[384,128]{1,0:T(8,128)S(1)}, u32[]{:S(2)}, u32[]{:S(2)}) %collective-permute-start.25) | collective-permute-done | bytes 196640 | tf_op jit(solution)/shard_map/ppermute | solution.py:27
  94.7 4.6 %collective-permute-start.26 = (f32[672,128]{1,0:T(8,128)S(1)}, f32[672,128]{1,0:T(8,128)S(1)}, u32[]{:S(2)}, u32[]{:S(2)}) collective-permute-start(f32[672,128]{1,0:T(8,128)S(1)} %get-tuple-element.39), channel_id=1, source_target_pairs={{0,4},{4,0},{8,12},{12,8},{16,20},{20,16},{24,28},{28,24},{32,36},... | collective-permute-start | bytes 1032200 | tf_op jit(solution)/shard_map/ppermute | solution.py:27
  99.3 1.3 %collective-permute-done.26.on = f32[672,128]{1,0:T(8,128)S(1)} collective-permute-done((f32[672,128]{1,0:T(8,128)S(1)}, f32[672,128]{1,0:T(8,128)S(1)}, u32[]{:S(2)}, u32[]{:S(2)}) %collective-permute-start.26) | collective-permute-done | bytes 344096 | tf_op jit(solution)/shard_map/ppermute | solution.py:27
  100.6 5.7 %collective-permute-done.27.off = f32[672,128]{1,0:T(8,128)S(1)} collective-permute-done((f32[672,128]{1,0:T(8,128)S(1)}, f32[672,128]{1,0:T(8,128)S(1)}, u32[]{:S(2)}, u32[]{:S(2)}) %collective-permute-start.27) | collective-permute-done | bytes 344096 | tf_op jit(solution)/shard_map/ppermute | solution.py:27
  106.3 4.5 %shard_map.208 = f32[8,8,16,128]{3,2,1,0:T(8,128)} custom-call(f32[8,8,16,128]{3,2,1,0:T(8,128)S(1)} %get-tuple-element.36.start.own, f32[384,128]{1,0:T(8,128)S(1)} %collective-permute-done.24.even, f32[384,128]{1,0:T(8,128)S(1)} %collective-permute-done.25.odd, f32[672,128]{1,0:T(8,128)S(1)} %collective-permute-done.26.on, ...), custom_call_target="tpu_custom_call" | custom-call | flops 16000000 | bytes 3973120 | tf_op jit(solution)/shard_map/pallas_call | solution.py:130
  (35 shorter events, 0.2 us)
Async XLA Ops:
  0.6 57.8 %copy-start.2 = (bf16[4,4,2,128,128]{4,3,2,1,0:T(8,128)(2,1)S(1)}, bf16[4,4,2,128,128]{4,3,2,1,0:T(8,128)(2,1)}, u32[]{:S(2)}) copy-start(bf16[4,4,2,128,128]{4,3,2,1,0:T(8,128)(2,1)} %blocks.2) | copy-start | bytes 3145732
  1.6 5.2 %collective-permute-start.2 = (f32[104,128]{1,0:T(8,128)S(1)}, f32[104,128]{1,0:T(8,128)S(1)}, u32[]{:S(2)}, u32[]{:S(2)}) collective-permute-start(f32[104,128]{1,0:T(8,128)S(1)} %shard_map.201), channel_id=1, source_target_pairs={{0,3},{1,2},{2,1},{3,0},{4,7},{5,6},{6,5},{7,4},{8,11},{9,10},{10,... | collective-permute-start | bytes 159752 | tf_op jit(solution)/shard_map/ppermute | solution.py:27
  5.3 4.6 %collective-permute-start.1 = (f32[104,128]{1,0:T(8,128)S(1)}, f32[104,128]{1,0:T(8,128)S(1)}, u32[]{:S(2)}, u32[]{:S(2)}) collective-permute-start(f32[104,128]{1,0:T(8,128)S(1)} %shard_map.201), channel_id=1, source_target_pairs={{0,2},{1,3},{2,0},{3,1},{4,6},{5,7},{6,4},{7,5},{8,10},{9,11},{10,... | collective-permute-start | bytes 159752 | tf_op jit(solution)/shard_map/ppermute | solution.py:27
  5.6 4.2 %collective-permute-start = (f32[104,128]{1,0:T(8,128)S(1)}, f32[104,128]{1,0:T(8,128)S(1)}, u32[]{:S(2)}, u32[]{:S(2)}) collective-permute-start(f32[104,128]{1,0:T(8,128)S(1)} %shard_map.201), channel_id=1, source_target_pairs={{0,1},{1,0},{2,3},{3,2},{4,5},{5,4},{6,7},{7,6},{8,9},{9,8},{10,11... | collective-permute-start | bytes 159752 | tf_op jit(solution)/shard_map/ppermute | solution.py:27
  9.9 3.2 %collective-permute-start.3 = (f32[4,104,128]{2,1,0:T(8,128)S(1)}, f32[4,104,128]{2,1,0:T(8,128)S(1)}, u32[]{:S(2)}, u32[]{:S(2)}) collective-permute-start(f32[4,104,128]{2,1,0:T(8,128)S(1)} %pad_maximum_fusion.3), channel_id=1, source_target_pairs={{0,4},{4,0},{8,12},{12,8},{16,20},{20,16},{24,28},{28,24},{32,36},... | collective-permute-start | bytes 638984 | tf_op jit(solution)/shard_map/ppermute | solution.py:27
  13.1 14.1 %collective-permute-start.5 = (f32[2,4,40,128]{3,2,1,0:T(8,128)S(1)}, f32[2,4,40,128]{3,2,1,0:T(8,128)S(1)}, u32[]{:S(2)}, u32[]{:S(2)}) collective-permute-start(f32[2,4,40,128]{3,2,1,0:T(8,128)S(1)} %pad_maximum_fusion.4.pair.spair), channel_id=1, source_target_pairs={{0,244},{4,16},{8,252},{12,24},{16,4},{20,32},{24,12},{28,40},{32,... | collective-permute-start | bytes 491528 | tf_op jit(solution)/shard_map/ppermute | solution.py:27
  16.4 11.0 %collective-permute-start.4 = (f32[2,4,40,128]{3,2,1,0:T(8,128)S(1)}, f32[2,4,40,128]{3,2,1,0:T(8,128)S(1)}, u32[]{:S(2)}, u32[]{:S(2)}) collective-permute-start(f32[2,4,40,128]{3,2,1,0:T(8,128)S(1)} %pad_maximum_fusion.4.pair.spair), channel_id=1, source_target_pairs={{0,252},{4,8},{8,4},{12,16},{16,12},{20,24},{24,20},{28,32},{32,28... | collective-permute-start | bytes 491528 | tf_op jit(solution)/shard_map/ppermute | solution.py:27
  23.8 17.2 %collective-permute-start.10 = (bf16[1232,128]{1,0:T(8,128)(2,1)S(1)}, bf16[1232,128]{1,0:T(8,128)(2,1)S(1)}, u32[]{:S(2)}, u32[]{:S(2)}) collective-permute-start(bf16[1232,128]{1,0:T(8,128)(2,1)S(1)} %get-tuple-element.24.third0), channel_id=1, source_target_pairs={{0,3},{1,2},{2,1},{3,0},{4,7},{5,6},{6,5},{7,4},{8,11},{9,10},{10,... | collective-permute-start | bytes 946184 | tf_op jit(solution)/shard_map/ppermute | solution.py:27
  24.9 16.1 %collective-permute-start.9 = (bf16[1232,128]{1,0:T(8,128)(2,1)S(1)}, bf16[1232,128]{1,0:T(8,128)(2,1)S(1)}, u32[]{:S(2)}, u32[]{:S(2)}) collective-permute-start(bf16[1232,128]{1,0:T(8,128)(2,1)S(1)} %get-tuple-element.24.third0), channel_id=1, source_target_pairs={{0,2},{1,3},{2,0},{3,1},{4,6},{5,7},{6,4},{7,5},{8,10},{9,11},{10,... | collective-permute-start | bytes 946184 | tf_op jit(solution)/shard_map/ppermute | solution.py:27
  25.7 16.1 %collective-permute-start.8 = (bf16[1232,128]{1,0:T(8,128)(2,1)S(1)}, bf16[1232,128]{1,0:T(8,128)(2,1)S(1)}, u32[]{:S(2)}, u32[]{:S(2)}) collective-permute-start(bf16[1232,128]{1,0:T(8,128)(2,1)S(1)} %get-tuple-element.24.third0), channel_id=1, source_target_pairs={{0,1},{1,0},{2,3},{3,2},{4,5},{5,4},{6,7},{7,6},{8,9},{9,8},{10,11... | collective-permute-start | bytes 946184 | tf_op jit(solution)/shard_map/ppermute | solution.py:27
  27.1 14.7 %collective-permute-start.7 = (f32[2,4,40,128]{3,2,1,0:T(8,128)S(1)}, f32[2,4,40,128]{3,2,1,0:T(8,128)S(1)}, u32[]{:S(2)}, u32[]{:S(2)}) collective-permute-start(f32[2,4,40,128]{3,2,1,0:T(8,128)S(1)} %collective-permute-done.5.a3), channel_id=1, source_target_pairs={{0,4},{4,0},{8,12},{12,8},{16,20},{20,16},{24,28},{28,24},{32,36},... | collective-permute-start | bytes 491528 | tf_op jit(solution)/shard_map/ppermute | solution.py:27
  27.4 14.5 %collective-permute-start.6 = (f32[2,4,40,128]{3,2,1,0:T(8,128)S(1)}, f32[2,4,40,128]{3,2,1,0:T(8,128)S(1)}, u32[]{:S(2)}, u32[]{:S(2)}) collective-permute-start(f32[2,4,40,128]{3,2,1,0:T(8,128)S(1)} %collective-permute-done.4.a.sa), channel_id=1, source_target_pairs={{0,4},{4,0},{8,12},{12,8},{16,20},{20,16},{24,28},{28,24},{32,36},... | collective-permute-start | bytes 491528 | tf_op jit(solution)/shard_map/ppermute | solution.py:27
  29.9 52.4 %copy-start = (bf16[8,8,2,128,128]{4,3,2,1,0:T(8,128)(2,1)S(1)}, bf16[8,8,2,128,128]{4,3,2,1,0:T(8,128)(2,1)}, u32[]{:S(2)}) copy-start(bf16[8,8,2,128,128]{4,3,2,1,0:T(8,128)(2,1)} %blocks.3) | copy-start | bytes 12582916
  29.9 52.3 %copy-start.3 = (f32[8,8,16,128]{3,2,1,0:T(8,128)S(1)}, f32[8,8,16,128]{3,2,1,0:T(8,128)}, u32[]{:S(2)}) copy-start(f32[8,8,16,128]{3,2,1,0:T(8,128)} %guess.1) | copy-start | bytes 1572868
  44.4 1.5 %collective-permute-start.11 = (f32[256,128]{1,0:T(8,128)S(1)}, f32[256,128]{1,0:T(8,128)S(1)}, u32[]{:S(2)}, u32[]{:S(2)}) collective-permute-start(f32[256,128]{1,0:T(8,128)S(1)} %get-tuple-element.25), channel_id=1, source_target_pairs={{0,4},{4,0},{8,12},{12,8},{16,20},{20,16},{24,28},{28,24},{32,36},... | collective-permute-start | bytes 393224 | tf_op jit(solution)/shard_map/ppermute | solution.py:27
  45.0 6.2 %collective-permute-start.14 = (f32[2,4,64,128]{3,2,1,0:T(8,128)S(1)}, f32[2,4,64,128]{3,2,1,0:T(8,128)S(1)}, u32[]{:S(2)}, u32[]{:S(2)}) collective-permute-start(f32[2,4,64,128]{3,2,1,0:T(8,128)S(1)} %pad_maximum_fusion.2.fpair), channel_id=1, source_target_pairs={{0,252},{4,8},{8,4},{12,16},{16,12},{20,24},{24,20},{28,32},{32,28... | collective-permute-start | bytes 786440 | tf_op jit(solution)/shard_map/ppermute | solution.py:27
  45.9 8.2 %collective-permute-start.12 = (f32[2,256,128]{2,1,0:T(8,128)S(1)}, f32[2,256,128]{2,1,0:T(8,128)S(1)}, u32[]{:S(2)}, u32[]{:S(2)}) collective-permute-start(f32[2,256,128]{2,1,0:T(8,128)S(1)} %pad_maximum_fusion.1.pair), channel_id=1, source_target_pairs={{0,252},{4,8},{8,4},{12,16},{16,12},{20,24},{24,20},{28,32},{32,28... | collective-permute-start | bytes 786440 | tf_op jit(solution)/shard_map/ppermute | solution.py:27
  51.1 7.3 %collective-permute-start.15 = (f32[2,4,64,128]{3,2,1,0:T(8,128)S(1)}, f32[2,4,64,128]{3,2,1,0:T(8,128)S(1)}, u32[]{:S(2)}, u32[]{:S(2)}) collective-permute-start(f32[2,4,64,128]{3,2,1,0:T(8,128)S(1)} %collective-permute-done.14.fa), channel_id=1, source_target_pairs={{0,4},{4,0},{8,12},{12,8},{16,20},{20,16},{24,28},{28,24},{32,36},... | collective-permute-start | bytes 786440 | tf_op jit(solution)/shard_map/ppermute | solution.py:27
  54.2 4.2 %collective-permute-start.13 = (f32[2,256,128]{2,1,0:T(8,128)S(1)}, f32[2,256,128]{2,1,0:T(8,128)S(1)}, u32[]{:S(2)}, u32[]{:S(2)}) collective-permute-start(f32[2,256,128]{2,1,0:T(8,128)S(1)} %collective-permute-done.12.a), channel_id=1, source_target_pairs={{0,4},{4,0},{8,12},{12,8},{16,20},{20,16},{24,28},{28,24},{32,36},... | collective-permute-start | bytes 786440 | tf_op jit(solution)/shard_map/ppermute | solution.py:27
  57.0 9.4 %collective-permute-start.21 = (f32[544,128]{1,0:T(8,128)S(1)}, f32[544,128]{1,0:T(8,128)S(1)}, u32[]{:S(2)}, u32[]{:S(2)}) collective-permute-start(f32[544,128]{1,0:T(8,128)S(1)} %get-tuple-element.31), channel_id=1, source_target_pairs={{0,3},{1,2},{2,1},{3,0},{4,7},{5,6},{6,5},{7,4},{8,11},{9,10},{10,... | collective-permute-start | bytes 835592 | tf_op jit(solution)/shard_map/ppermute | solution.py:27
  58.0 8.4 %collective-permute-start.20 = (f32[544,128]{1,0:T(8,128)S(1)}, f32[544,128]{1,0:T(8,128)S(1)}, u32[]{:S(2)}, u32[]{:S(2)}) collective-permute-start(f32[544,128]{1,0:T(8,128)S(1)} %get-tuple-element.29), channel_id=1, source_target_pairs={{0,1},{1,0},{2,3},{3,2},{4,5},{5,4},{6,7},{7,6},{8,9},{9,8},{10,11... | collective-permute-start | bytes 835592 | tf_op jit(solution)/shard_map/ppermute | solution.py:27
  61.5 7.7 %collective-permute-start.17 = (f32[256,128]{1,0:T(8,128)S(1)}, f32[256,128]{1,0:T(8,128)S(1)}, u32[]{:S(2)}, u32[]{:S(2)}) collective-permute-start(f32[256,128]{1,0:T(8,128)S(1)} %bitcast.17), channel_id=1, source_target_pairs={{0,3},{1,2},{2,1},{3,0},{4,7},{5,6},{6,5},{7,4},{8,11},{9,10},{10,... | collective-permute-start | bytes 393224 | tf_op jit(solution)/shard_map/ppermute | solution.py:27
  63.0 6.2 %collective-permute-start.16 = (f32[256,128]{1,0:T(8,128)S(1)}, f32[256,128]{1,0:T(8,128)S(1)}, u32[]{:S(2)}, u32[]{:S(2)}) collective-permute-start(f32[256,128]{1,0:T(8,128)S(1)} %bitcast.18), channel_id=1, source_target_pairs={{0,1},{1,0},{2,3},{3,2},{4,5},{5,4},{6,7},{7,6},{8,9},{9,8},{10,11... | collective-permute-start | bytes 393224 | tf_op jit(solution)/shard_map/ppermute | solution.py:27
  66.5 6.8 %collective-permute-start.22 = (f32[1224,128]{1,0:T(8,128)S(1)}, f32[1224,128]{1,0:T(8,128)S(1)}, u32[]{:S(2)}, u32[]{:S(2)}) collective-permute-start(f32[1224,128]{1,0:T(8,128)S(1)} %get-tuple-element.34), channel_id=1, source_target_pairs={{0,4},{4,0},{8,12},{12,8},{16,20},{20,16},{24,28},{28,24},{32,36},... | collective-permute-start | bytes 1880072 | tf_op jit(solution)/shard_map/ppermute | solution.py:27
  68.0 10.0 %collective-permute-start.23 = (f32[1224,128]{1,0:T(8,128)S(1)}, f32[1224,128]{1,0:T(8,128)S(1)}, u32[]{:S(2)}, u32[]{:S(2)}) collective-permute-start(f32[1224,128]{1,0:T(8,128)S(1)} %get-tuple-element.35), channel_id=1, source_target_pairs={{0,252},{4,8},{8,4},{12,16},{16,12},{20,24},{24,20},{28,32},{32,28... | collective-permute-start | bytes 1880072 | tf_op jit(solution)/shard_map/ppermute | solution.py:27
  69.2 13.0 %collective-permute-start.19 = (f32[768,128]{1,0:T(8,128)S(1)}, f32[768,128]{1,0:T(8,128)S(1)}, u32[]{:S(2)}, u32[]{:S(2)}) collective-permute-start(f32[768,128]{1,0:T(8,128)S(1)} %pad_maximum_fusion), channel_id=1, source_target_pairs={{0,252},{4,8},{8,4},{12,16},{16,12},{20,24},{24,20},{28,32},{32,28... | collective-permute-start | bytes 1179656 | tf_op jit(solution)/shard_map/ppermute | solution.py:27
  69.9 12.3 %collective-permute-start.18 = (f32[768,128]{1,0:T(8,128)S(1)}, f32[768,128]{1,0:T(8,128)S(1)}, u32[]{:S(2)}, u32[]{:S(2)}) collective-permute-start(f32[768,128]{1,0:T(8,128)S(1)} %pad_maximum_fusion), channel_id=1, source_target_pairs={{0,4},{4,0},{8,12},{12,8},{16,20},{20,16},{24,28},{28,24},{32,36},... | collective-permute-start | bytes 1179656 | tf_op jit(solution)/shard_map/ppermute | solution.py:27
  82.2 24.1 %copy-start.1 = (f32[8,8,16,128]{3,2,1,0:T(8,128)S(1)}, f32[8,8,16,128]{3,2,1,0:T(8,128)}, u32[]{:S(2)}) copy-start(f32[8,8,16,128]{3,2,1,0:T(8,128)} %fown.1) | copy-start | bytes 1572868
  82.2 24.1 %copy-start.4 = (f32[8,8,128]{2,1,0:T(8,128)S(1)}, f32[8,8,128]{2,1,0:T(8,128)}, u32[]{:S(2)}) copy-start(f32[8,8,128]{2,1,0:T(8,128)} %sown.1) | copy-start | bytes 98308
  88.7 4.6 %collective-permute-start.24 = (f32[384,128]{1,0:T(8,128)S(1)}, f32[384,128]{1,0:T(8,128)S(1)}, u32[]{:S(2)}, u32[]{:S(2)}) collective-permute-start(f32[384,128]{1,0:T(8,128)S(1)} %get-tuple-element.37), channel_id=1, source_target_pairs={{0,1},{1,0},{2,3},{3,2},{4,5},{5,4},{6,7},{7,6},{8,9},{9,8},{10,11... | collective-permute-start | bytes 589832 | tf_op jit(solution)/shard_map/ppermute | solution.py:27
  88.9 5.7 %collective-permute-start.25 = (f32[384,128]{1,0:T(8,128)S(1)}, f32[384,128]{1,0:T(8,128)S(1)}, u32[]{:S(2)}, u32[]{:S(2)}) collective-permute-start(f32[384,128]{1,0:T(8,128)S(1)} %get-tuple-element.38), channel_id=1, source_target_pairs={{0,3},{1,2},{2,1},{3,0},{4,7},{5,6},{6,5},{7,4},{8,11},{9,10},{10,... | collective-permute-start | bytes 589832 | tf_op jit(solution)/shard_map/ppermute | solution.py:27
  94.7 5.9 %collective-permute-start.26 = (f32[672,128]{1,0:T(8,128)S(1)}, f32[672,128]{1,0:T(8,128)S(1)}, u32[]{:S(2)}, u32[]{:S(2)}) collective-permute-start(f32[672,128]{1,0:T(8,128)S(1)} %get-tuple-element.39), channel_id=1, source_target_pairs={{0,4},{4,0},{8,12},{12,8},{16,20},{20,16},{24,28},{28,24},{32,36},... | collective-permute-start | bytes 1032200 | tf_op jit(solution)/shard_map/ppermute | solution.py:27
  99.3 7.0 %collective-permute-start.27 = (f32[672,128]{1,0:T(8,128)S(1)}, f32[672,128]{1,0:T(8,128)S(1)}, u32[]{:S(2)}, u32[]{:S(2)}) collective-permute-start(f32[672,128]{1,0:T(8,128)S(1)} %get-tuple-element.40), channel_id=1, source_target_pairs={{0,252},{4,8},{8,4},{12,16},{16,12},{20,24},{24,20},{28,32},{32,28... | collective-permute-start | bytes 1032200 | tf_op jit(solution)/shard_map/ppermute | solution.py:27

commit v3 on v2

--- a/solution.py
+++ b/solution.py
@@ -217,7 +217,12 @@
         copy.wait()
 
 
-def fourth_kernel(pair, a, a3, b, b3, third0, third1, third2, third3, out, start, u, f, s, res, d0, d1, lines):
+def relay_kernel(near, far, out):
+    out[0] = near[...]
+    out[1] = far[...]
+
+
+def fourth_kernel(pair, a, a3, both, third0, third1, third2, third3, out, start, u, f, s, res, d0, d1, lines):
     gz, gy = lax.axis_index("gz"), lax.axis_index("gy")
     core = lax.rem(gz, 2)
 
@@ -233,9 +238,9 @@
 
     place(pair, 2, core)
     place(a, 1 + 2 * core, 1 - core)
-    place(b, 3 - 2 * core, core)
+    place(both.at[0], 3 - 2 * core, core)
     place(a3, 4 * core, 1 - core)
-    place(b3, 4 - 4 * core, core)
+    place(both.at[1], 4 - 4 * core, core)
 
     def emit(i, j, value):
         lines[i - 3 - core, j] = value.astype(BF16).astype(F32)
@@ -288,7 +293,7 @@
 
     place(pair, fpair, spair, 1, core)
     place(a, fa, sa, 2 * core, 1 - core)
-    place(b, fb, sb, 2 - 2 * core, core)
+    place(b, fb, sb.at[0], 2 - 2 * core, core)
 
     def emit(i, j, value):
         lines[i - 3 - 2 * core, j] = value.astype(BF16)
@@ -333,27 +338,64 @@
                 ref[1208 + i * 12 + 2 * n : 1210 + i * 12 + 2 * n, :] = jnp.where(first == 0, low, high)
 
 
+SIDE4 = tuple((r, n) for r in range(4) for n in range(4 - r))
+BLOCK = (16 + 2 * len(SIDE4)) * R
+
+
+def at_cell(ref, cell):
+    return ref[pl.ds(pl.multiple_of(cell * R, R), R), :]
+
+
+def block_kernel(own, even, odd, on, off):
+    core, side = lax.rem(lax.axis_index("gz"), 2), lax.rem(lax.axis_index("gy"), 2)
+    for ref, right in ((on, 1 - core), (off, core)):
+        for r in range(4):
+            row = r + right * (3 - 2 * r)
+            for j in range(4):
+                at = (r * 4 + j) * R
+                ref[at : at + R, :] = at_cell(own, row * 4 + j)
+        for m, (r, n) in enumerate(SIDE4):
+            row = r + right * (3 - 2 * r)
+            for k, (beside, left) in enumerate(((even, side), (odd, 1 - side))):
+                at = (16 + k * len(SIDE4) + m) * R
+                ref[at : at + R, :] = at_cell(beside, row * 4 + n + left * (3 - 2 * n))
+
+
 def second_kernel(own, own_even, own_odd, on, off, fown, feven, fodd, fon, foff, links_h, blocks, guess, out, start, even, odd, u, f, s, res, d0, d1, lines, links, sems):
     copies = fetch(sems, (links_h, links))
     gz, gy = lax.axis_index("gz"), lax.axis_index("gy")
     core, side = lax.rem(gz, 2), lax.rem(gy, 2)
     starts = (4, 8 - 8 * side, 8 * side)
 
-    def place(refs, frefs, row0):
+    def place(frefs, row0):
         for k in range(3):
-            ref, base = refs[k]
             fref, fbase = frefs[k]
             for i in range(4):
                 for j in range(4):
                     c = i * 4 + j
                     row, col = row0 + i, starts[k] + j
-                    u[row, col] = ref[base + c * R : base + (c + 1) * R, :]
                     f[row, col] = fref[fbase + c * R : fbase + (c + 1) * R, :]
                     s[row, col] = fref[fbase + 256 + c : fbase + 257 + c, :]
 
-    place(((own, 0), (own_even, 0), (own_odd, 0)), ((fown, 0), (feven, 0), (fodd, 0)), 4)
-    for ref, fref, row0 in ((on, fon, 8 - 8 * core), (off, foff, 8 * core)):
-        place([(ref, 256 * k) for k in range(3)], [(fref, 272 * k) for k in range(3)], row0)
+    place(((fown, 0), (feven, 0), (fodd, 0)), 4)
+    for fref, row0 in ((fon, 8 - 8 * core), (foff, 8 * core)):
+        place([(fref, 272 * k) for k in range(3)], row0)
+    for i in range(4):
+        for j in range(4):
+            at = (i * 4 + j) * R
+            for k, ref in enumerate((own, own_even, own_odd)):
+                u[4 + i, starts[k] + j] = ref[at : at + R, :]
+    for ref, left in ((on, core), (off, 1 - core)):
+        for r in range(4):
+            row = 8 + r - left * (5 + 2 * r)
+            for j in range(4):
+                at = (r * 4 + j) * R
+                u[row, 4 + j] = ref[at : at + R, :]
+        for m, (r, n) in enumerate(SIDE4):
+            row = 8 + r - left * (5 + 2 * r)
+            for k, across in enumerate((side, 1 - side)):
+                at = (16 + k * len(SIDE4) + m) * R
+                u[row, 8 + n - across * (5 + 2 * n)] = ref[at : at + R, :]
 
     def emit(i, j, value):
         lines[i - 3, j - 3] = value.astype(BF16)
@@ -385,16 +427,23 @@
             odd[at : at + R, :] = start[i, 5 * side + j]
 
 
+SIDE3 = ((0, 0), (0, 1), (1, 0))
+ROWS = (24 + 2 * len(SIDE3)) * R
+
+
 def rows_kernel(start, even, odd, on, off):
-    core = lax.rem(lax.axis_index("gz"), 2)
-    for ref, first in ((on, 5 - 5 * core), (off, 5 * core)):
-        for i in range(3):
+    core, side = lax.rem(lax.axis_index("gz"), 2), lax.rem(lax.axis_index("gy"), 2)
+    for ref, right in ((on, 1 - core), (off, core)):
+        for r in range(3):
+            row = r + right * (7 - 2 * r)
             for j in range(8):
-                at = (i * 14 + j) * R
-                ref[at : at + R, :] = start[first + i, j]
-            for n, side_ref in enumerate((even, odd)):
-                at = (i * 14 + 8 + 3 * n) * R
-                ref[at : at + 3 * R, :] = side_ref[pl.ds(pl.multiple_of((first + i) * 3 * R, 8), 3 * R), :]
+                at = (r * 8 + j) * R
+                ref[at : at + R, :] = start[row, j]
+        for m, (r, n) in enumerate(SIDE3):
+            row = r + right * (7 - 2 * r)
+            for k, (beside, left) in enumerate(((even, side), (odd, 1 - side))):
+                at = (24 + k * len(SIDE3) + m) * R
+                ref[at : at + R, :] = at_cell(beside, row * 3 + n + left * (2 - 2 * n))
 
 
 def first_kernel(own, even, odd, on, off, fown, sown, feven, fodd, fon, foff, out, u, f, s, res, d0, d1):
@@ -420,12 +469,15 @@
             s[3 + i, even_f + j] = feven[528 + c : 529 + c, :]
             s[3 + i, odd_f + j] = fodd[528 + c : 529 + c, :]
 
-    def place(ref, fref, row_u, row_f):
-        for i in range(3):
-            for j in range(14):
-                col = 3 + j if j < 8 else even_u + j - 8 if j < 11 else odd_u + j - 11
-                at = (i * 14 + j) * R
-                u[row_u + i, col] = ref[at : at + R, :]
+    def place(ref, fref, left, row_f):
+        for r in range(3):
+            for j in range(8):
+                at = (r * 8 + j) * R
+                u[11 + r - left * (9 + 2 * r), 3 + j] = ref[at : at + R, :]
+        for m, (r, n) in enumerate(SIDE3):
+            for k, across in enumerate((side, 1 - side)):
+                at = (24 + k * len(SIDE3) + m) * R
+                u[11 + r - left * (9 + 2 * r), 11 + n - across * (9 + 2 * n)] = ref[at : at + R, :]
         for i in range(2):
             for j in range(12):
                 col = 3 + j if j < 8 else even_f + j - 8 if j < 10 else odd_f + j - 10
@@ -434,8 +486,8 @@
                 f[row_f + i, col] = fref[at : at + R, :]
                 s[row_f + i, col] = fref[1200 + c : 1201 + c, :]
 
-    place(on, fon, 11 - 11 * core, 11 - 10 * core)
-    place(off, foff, 11 * core, 1 + 10 * core)
+    place(on, fon, core, 11 - 10 * core)
+    place(off, foff, 1 - core, 1 + 10 * core)
 
     def emit(i, j, value):
         out[i - 3, j - 3] = value
@@ -445,10 +497,6 @@
 
 def sds(*shape, dtype=F32):
     return jax.ShapeDtypeStruct(shape, dtype)
-
-
-def after(x, *done):
-    return lax.optimization_barrier((x, *done))[0]
 
 
 def flat(x):
@@ -480,8 +528,8 @@
     pair_f = jnp.stack([line[:, 40:], line_on[:, 40:]])
     near = z_off(pair)
     far = z_off3(pair)
-    near_b = z_on(near)
-    far_b = z_on(far)
+    (both,) = call(relay_kernel, (near, far), (sds(2, 2, 4, 40, L),), [], 1000, 2)
+    both = z_on(both)
     near_f = z_off(pair_f)
     near_fb = z_on(near_f)
 
@@ -496,7 +544,8 @@
     third1 = y_by(third, 1)
     third2 = y_by(third, 2)
     third3 = y_by(third, 3)
-    ahead_even, ahead_odd = y_even(after(ahead_even, y1, y2, y3)), y_odd(after(ahead_odd, y1, y2, y3))
+    ahead_even = y_even(ahead_even)
+    ahead_odd = y_odd(ahead_odd)
     ahead_on, ahead_off = call(
         along_z_kernel,
         (mine, ahead_even, ahead_odd, row_on, row_off),
@@ -511,18 +560,19 @@
 
     out_fourth, start_third = call(
         fourth_kernel,
-        (pair, near, far, near_b, far_b, third, third1, third2, third3),
+        (pair, near, far, both, third, third1, third2, third3),
         (sds(1, 1, R, L), sds(256, L)),
         smoothing_scratch(10, 4) + [cells(3, 4)],
         4_000_000, 6,
     )
 
-    pair3 = jnp.stack([start_third, z_on(start_third)])
+    start_on = z_on(start_third)
+    pair3 = jnp.stack([start_third, start_on])
     near3 = z_off(pair3)
     near3_b = z_on(near3)
     out_third, start_second = call(
         third_kernel,
-        (pair3, near3, near3_b, pair_f, near_f, near_fb, pair, near, near_b, links_second, blocks_second, guess_second),
+        (pair3, near3, near3_b, pair_f, near_f, near_fb, pair, near, both, links_second, blocks_second, guess_second),
         (sds(2, 2, R, L), sds(4, 4, R, L)),
         smoothing_scratch(12, 8) + [cells(4, 8, BF16)] + smem_last(guess_second, links_second),
         8_000_000, 12, (9, 11),
@@ -530,17 +580,17 @@
 
     own = flat(start_second)
     own_even, own_odd = y_even(own), y_odd(own)
-    block = jnp.concatenate([own, own_even, own_odd])
+    block_on, block_off = call(block_kernel, (own, own_even, own_odd), (sds(BLOCK, L), sds(BLOCK, L)), [], 10000, 4)
     out_second, start_first, strip_even, strip_odd = call(
         second_kernel,
-        (own, own_even, own_odd, z_on(block), z_off(block), mine, ahead_even, ahead_odd, ahead_on, ahead_off, links_first, blocks_first, guess_first),
+        (own, own_even, own_odd, z_on(block_on), z_off(block_off), mine, ahead_even, ahead_odd, ahead_on, ahead_off, links_first, blocks_first, guess_first),
         (sds(4, 4, R, L), sds(8, 8, R, L), sds(24 * R, L), sds(24 * R, L)),
         smoothing_scratch(12, 12) + [cells(6, 6, BF16)] + smem_last(links_first),
         16_000_000, 20, (10,),
     )
 
     u_even, u_odd = y_even(strip_even), y_odd(strip_odd)
-    u_on, u_off = call(rows_kernel, (start_first, u_even, u_odd), (sds(42 * R, L), sds(42 * R, L)), [], 10000, 4)
+    u_on, u_off = call(rows_kernel, (start_first, u_even, u_odd), (sds(ROWS, L), sds(ROWS, L)), [], 10000, 4)
     (out_first,) = call(
         first_kernel,
         (start_first, u_even, u_odd, z_on(u_on), z_off(u_off), source_first, shift_first, ahead_even, ahead_odd, ahead_on, ahead_off),

time: 111 us -> 114 us (1.027)
  waiting for transfers between devices: 45.8 us -> 48.3 us
    ppermute x28 -> x27, waiting for transfers between devices: 45.8 us -> 48.3 us  [swap(): lax.ppermute(x, axis, [(i, partner(i)) for i in range(lax.axis_size(axis))])]
    ppermute x28 -> x27, starting transfers between devices: 45 us -> 44.2 us  [swap(): lax.ppermute(x, axis, [(i, partner(i)) for i in range(lax.axis_size(axis))])]
    pallas_call x8 -> x10, Pallas kernels: 19 us -> 19.3 us  [call(): pl.pallas_call(kernel, out_shape=outs, in_specs=specs, out_specs=jax.tree...]
  transfers between devices with their start and end apart: 28 -> 27, of which waited for: 15 -> 17; matrix products, arithmetic and copies ran while one was open for 0% -> 0% of each run, Pallas kernels for 4% -> 4%
where the time goes in v3:
time: 114 us; the launch traced here: 113 us
  waiting for transfers between devices  48.3 us (42%)
  starting transfers between devices  44.2 us (39%)
  Pallas kernels  19.3 us (17%)
    ppermute x27, waiting for transfers between devices, swap(): lax.ppermute(x, axis, [(i, partner(i)) for i in range(lax.axis_size(axis))])  48.3 us
    ppermute x27, starting transfers between devices, swap(): lax.ppermute(x, axis, [(i, partner(i)) for i in range(lax.axis_size(axis))])  44.2 us
    pallas_call x10, Pallas kernels, call(): pl.pallas_call(kernel, out_shape=outs, in_specs=specs, out_specs=jax.tree...  19.3 us
  transfers between devices with their start and end apart: 27, of which 17 were waited for; matrix products, arithmetic and copies ran while one was open for 0% of the time, Pallas kernels for 4%

profile of v3, /device:TPU:1, one launch (start us, length us, event | category | flops | bytes accessed | tf_op | source)
XLA Modules:
  0.0 112.7 jit_solution(9726566971565707045)
XLA Ops:
  0.6 1.0 shard_map.201
  1.6 3.6 %collective-permute-start.2 = (f32[104,128]{1,0:T(8,128)S(1)}, f32[104,128]{1,0:T(8,128)S(1)}, u32[]{:S(2)}, u32[]{:S(2)}) collective-permute-start(f32[104,128]{1,0:T(8,128)S(1)} %shard_map.201), channel_id=1, source_target_pairs={{0,3},{1,2},{2,1},{3,0},{4,7},{5,6},{6,5},{7,4},{8,11},{9,10},{10,... | collective-permute-start | bytes 159752 | tf_op jit(solution)/shard_map/ppermute | solution.py:27
  5.3 0.3 collective-permute-start.1
  5.6 0.3 collective-permute-start
  5.9 0.8 collective-permute-done.2
  6.8 3.1 %collective-permute-done.1 = f32[104,128]{1,0:T(8,128)S(1)} collective-permute-done((f32[104,128]{1,0:T(8,128)S(1)}, f32[104,128]{1,0:T(8,128)S(1)}, u32[]{:S(2)}, u32[]{:S(2)}) %collective-permute-start.1) | collective-permute-done | bytes 53280 | tf_op jit(solution)/shard_map/ppermute | solution.py:27
  9.9 2.1 %collective-permute-start.3 = (f32[4,104,128]{2,1,0:T(8,128)S(1)}, f32[4,104,128]{2,1,0:T(8,128)S(1)}, u32[]{:S(2)}, u32[]{:S(2)}) collective-permute-start(f32[4,104,128]{2,1,0:T(8,128)S(1)} %pad_maximum_fusion.2), channel_id=1, source_target_pairs={{0,4},{4,0},{8,12},{12,8},{16,20},{20,16},{24,28},{28,24},{32,36},... | collective-permute-start | bytes 638984 | tf_op jit(solution)/shard_map/ppermute | solution.py:27
  12.0 1.1 collective-permute-done.3
  13.1 3.3 %collective-permute-start.5 = (f32[2,4,40,128]{3,2,1,0:T(8,128)S(1)}, f32[2,4,40,128]{3,2,1,0:T(8,128)S(1)}, u32[]{:S(2)}, u32[]{:S(2)}) collective-permute-start(f32[2,4,40,128]{3,2,1,0:T(8,128)S(1)} %pad_maximum_fusion.3.pair.spair), channel_id=1, source_target_pairs={{0,244},{4,16},{8,252},{12,24},{16,4},{20,32},{24,12},{28,40},{32,... | collective-permute-start | bytes 491528 | tf_op jit(solution)/shard_map/ppermute | solution.py:27
  16.4 6.0 %collective-permute-start.4 = (f32[2,4,40,128]{3,2,1,0:T(8,128)S(1)}, f32[2,4,40,128]{3,2,1,0:T(8,128)S(1)}, u32[]{:S(2)}, u32[]{:S(2)}) collective-permute-start(f32[2,4,40,128]{3,2,1,0:T(8,128)S(1)} %pad_maximum_fusion.3.pair.spair), channel_id=1, source_target_pairs={{0,252},{4,8},{8,4},{12,16},{16,12},{20,24},{24,20},{28,32},{32,28... | collective-permute-start | bytes 491528 | tf_op jit(solution)/shard_map/ppermute | solution.py:27
  22.4 4.8 %collective-permute-done.4.near.a.sa = f32[2,4,40,128]{3,2,1,0:T(8,128)S(1)} collective-permute-done((f32[2,4,40,128]{3,2,1,0:T(8,128)S(1)}, f32[2,4,40,128]{3,2,1,0:T(8,128)S(1)}, u32[]{:S(2)}, u32[]{:S(2)}) %collective-permute-start.4) | collective-permute-done | bytes 163872 | tf_op jit(solution)/shard_map/ppermute | solution.py:27
  27.2 2.7 %collective-permute-start.6 = (f32[2,2,4,40,128]{4,3,2,1,0:T(8,128)S(1)}, f32[2,2,4,40,128]{4,3,2,1,0:T(8,128)S(1)}, u32[]{:S(2)}, u32[]{:S(2)}) collective-permute-start(f32[2,2,4,40,128]{4,3,2,1,0:T(8,128)S(1)} %shard_map.202), channel_id=1, source_target_pairs={{0,4},{4,0},{8,12},{12,8},{16,20},{20,16},{24,28},{28,24},{32,36},... | collective-permute-start | bytes 983048 | tf_op jit(solution)/shard_map/ppermute | solution.py:27
  30.0 1.4 %shard_map.203 = (bf16[1232,128]{1,0:T(8,128)(2,1)S(1)}, f32[272,128]{1,0:T(8,128)S(1)}, f32[544,128]{1,0:T(8,128)S(1)}, f32[544,128]{1,0:T(8,128)S(1)}, f32[272,128]{1,0:T(8,128)S(1)}, /*index=5*/f32[272,128]{1,0:T(8,128)S(1)}) custom-call(f32[8,8,16,128]{3,2,1,0:T(8,128)} %fown.1, f32[8,8,128]{2,1,0:T(8,128)} %sown.1, f32[4,4,16,128]{3,2,1,0:T(8,128)} %source_second_h.1, ...), custom_call_target="tpu_custom_call" | custom-call | flops 1000 | bytes 991264 | tf_op jit(solution)/shard_map/pallas_call | solution.py:130
  31.4 0.0 copy-start
  31.4 1.1 collective-permute-start.9
  32.5 0.8 collective-permute-start.8
  33.3 1.4 %collective-permute-start.7 = (bf16[1232,128]{1,0:T(8,128)(2,1)S(1)}, bf16[1232,128]{1,0:T(8,128)(2,1)S(1)}, u32[]{:S(2)}, u32[]{:S(2)}) collective-permute-start(bf16[1232,128]{1,0:T(8,128)(2,1)S(1)} %get-tuple-element.24.third0), channel_id=1, source_target_pairs={{0,1},{1,0},{2,3},{3,2},{4,5},{5,4},{6,7},{7,6},{8,9},{9,8},{10,11... | collective-permute-start | bytes 946184 | tf_op jit(solution)/shard_map/ppermute | solution.py:27
  34.7 13.7 %collective-permute-done.9.third3 = bf16[1232,128]{1,0:T(8,128)(2,1)S(1)} collective-permute-done((bf16[1232,128]{1,0:T(8,128)(2,1)S(1)}, bf16[1232,128]{1,0:T(8,128)(2,1)S(1)}, u32[]{:S(2)}, u32[]{:S(2)}) %collective-permute-start.9) | collective-permute-done | bytes 315424 | tf_op jit(solution)/shard_map/ppermute | solution.py:27
  48.4 0.3 collective-permute-done.7.third1
  48.8 2.6 %shard_map.204 = (f32[1,1,16,128]{3,2,1,0:T(8,128)}, f32[256,128]{1,0:T(8,128)S(1)}) custom-call(f32[2,4,40,128]{3,2,1,0:T(8,128)S(1)} %pad_maximum_fusion.3.pair.spair, f32[2,4,40,128]{3,2,1,0:T(8,128)S(1)} %collective-permute-done.4.near.a.sa, f32[2,4,40,128]{3,2,1,0:T(8,128)S(1)} %collective-permute-done.5.far.a3, ...), custom_call_target="tpu_custom_call" | custom-call | flops 4000000 | bytes 2080768 | tf_op jit(solution)/shard_map/pallas_call | solution.py:130
  51.3 1.2 %collective-permute-start.10 = (f32[256,128]{1,0:T(8,128)S(1)}, f32[256,128]{1,0:T(8,128)S(1)}, u32[]{:S(2)}, u32[]{:S(2)}) collective-permute-start(f32[256,128]{1,0:T(8,128)S(1)} %get-tuple-element.25), channel_id=1, source_target_pairs={{0,4},{4,0},{8,12},{12,8},{16,20},{20,16},{24,28},{28,24},{32,36},... | collective-permute-start | bytes 393224 | tf_op jit(solution)/shard_map/ppermute | solution.py:27
  52.5 0.1 collective-permute-start.13
  52.6 0.8 collective-permute-done.10
  53.5 1.0 collective-permute-start.11
  54.5 0.1 collective-permute-start.19
  54.5 2.0 %collective-permute-start.20 = (f32[544,128]{1,0:T(8,128)S(1)}, f32[544,128]{1,0:T(8,128)S(1)}, u32[]{:S(2)}, u32[]{:S(2)}) collective-permute-start(f32[544,128]{1,0:T(8,128)S(1)} %get-tuple-element.31), channel_id=1, source_target_pairs={{0,3},{1,2},{2,1},{3,0},{4,7},{5,6},{6,5},{7,4},{8,11},{9,10},{10,... | collective-permute-start | bytes 835592 | tf_op jit(solution)/shard_map/ppermute | solution.py:27
  56.5 2.2 %collective-permute-done.13.fa = f32[2,4,64,128]{3,2,1,0:T(8,128)S(1)} collective-permute-done((f32[2,4,64,128]{3,2,1,0:T(8,128)S(1)}, f32[2,4,64,128]{3,2,1,0:T(8,128)S(1)}, u32[]{:S(2)}, u32[]{:S(2)}) %collective-permute-start.13) | collective-permute-done | bytes 262176 | tf_op jit(solution)/shard_map/ppermute | solution.py:27
  58.7 3.0 %collective-permute-start.14 = (f32[2,4,64,128]{3,2,1,0:T(8,128)S(1)}, f32[2,4,64,128]{3,2,1,0:T(8,128)S(1)}, u32[]{:S(2)}, u32[]{:S(2)}) collective-permute-start(f32[2,4,64,128]{3,2,1,0:T(8,128)S(1)} %collective-permute-done.13.fa), channel_id=1, source_target_pairs={{0,4},{4,0},{8,12},{12,8},{16,20},{20,16},{24,28},{28,24},{32,36},... | collective-permute-start | bytes 786440 | tf_op jit(solution)/shard_map/ppermute | solution.py:27
  61.7 3.6 %collective-permute-start.12 = (f32[2,256,128]{2,1,0:T(8,128)S(1)}, f32[2,256,128]{2,1,0:T(8,128)S(1)}, u32[]{:S(2)}, u32[]{:S(2)}) collective-permute-start(f32[2,256,128]{2,1,0:T(8,128)S(1)} %collective-permute-done.11.a), channel_id=1, source_target_pairs={{0,4},{4,0},{8,12},{12,8},{16,20},{20,16},{24,28},{28,24},{32,36},... | collective-permute-start | bytes 786440 | tf_op jit(solution)/shard_map/ppermute | solution.py:27
  65.4 0.1 shard_map.207
  65.5 0.6 collective-permute-start.21
  66.1 0.5 collective-permute-done.12.b
  66.5 3.3 %shard_map.205 = (f32[2,2,16,128]{3,2,1,0:T(8,128)}, f32[4,4,16,128]{3,2,1,0:T(8,128)S(1)}) custom-call(f32[2,256,128]{2,1,0:T(8,128)S(1)} %pad_maximum_fusion.pair, f32[2,256,128]{2,1,0:T(8,128)S(1)} %collective-permute-done.11.a, f32[2,256,128]{2,1,0:T(8,128)S(1)} %collective-permute-done.12.b, f32[2,4,64,128]{3,2,1,0:T(8,128)S(1)} %pad_maximum_fusion.1.fpair, ...), custom_call_target="tpu_custom_call" | custom-call | flops 8000000 | bytes 3408000 | tf_op jit(solution)/shard_map/pallas_call | solution.py:130
  69.8 1.6 %collective-permute-start.16 = (f32[256,128]{1,0:T(8,128)S(1)}, f32[256,128]{1,0:T(8,128)S(1)}, u32[]{:S(2)}, u32[]{:S(2)}) collective-permute-start(f32[256,128]{1,0:T(8,128)S(1)} %bitcast.17), channel_id=1, source_target_pairs={{0,3},{1,2},{2,1},{3,0},{4,7},{5,6},{6,5},{7,4},{8,11},{9,10},{10,... | collective-permute-start | bytes 393224 | tf_op jit(solution)/shard_map/ppermute | solution.py:27
  71.4 3.8 %collective-permute-done.16.odd.own_odd = f32[256,128]{1,0:T(8,128)S(1)} collective-permute-done((f32[256,128]{1,0:T(8,128)S(1)}, f32[256,128]{1,0:T(8,128)S(1)}, u32[]{:S(2)}, u32[]{:S(2)}) %collective-permute-start.16) | collective-permute-done | bytes 131104 | tf_op jit(solution)/shard_map/ppermute | solution.py:27
  75.2 0.3 collective-permute-done.15.even.own_even
  75.6 3.8 %collective-permute-start.17 = (f32[576,128]{1,0:T(8,128)S(1)}, f32[576,128]{1,0:T(8,128)S(1)}, u32[]{:S(2)}, u32[]{:S(2)}) collective-permute-start(f32[576,128]{1,0:T(8,128)S(1)} %get-tuple-element.27), channel_id=1, source_target_pairs={{0,4},{4,0},{8,12},{12,8},{16,20},{20,16},{24,28},{28,24},{32,36},... | collective-permute-start | bytes 884744 | tf_op jit(solution)/shard_map/ppermute | solution.py:27
  79.4 1.2 %collective-permute-done.17.on = f32[576,128]{1,0:T(8,128)S(1)} collective-permute-done((f32[576,128]{1,0:T(8,128)S(1)}, f32[576,128]{1,0:T(8,128)S(1)}, u32[]{:S(2)}, u32[]{:S(2)}) %collective-permute-start.17) | collective-permute-done | bytes 294944 | tf_op jit(solution)/shard_map/ppermute | solution.py:27
  80.6 5.2 %collective-permute-done.18.off = f32[576,128]{1,0:T(8,128)S(1)} collective-permute-done((f32[576,128]{1,0:T(8,128)S(1)}, f32[576,128]{1,0:T(8,128)S(1)}, u32[]{:S(2)}, u32[]{:S(2)}) %collective-permute-start.18) | collective-permute-done | bytes 294944 | tf_op jit(solution)/shard_map/ppermute | solution.py:27
  85.9 6.4 %shard_map.208 = (f32[4,4,16,128]{3,2,1,0:T(8,128)}, f32[8,8,16,128]{3,2,1,0:T(8,128)S(1)}, f32[384,128]{1,0:T(8,128)S(1)}, f32[384,128]{1,0:T(8,128)S(1)}) custom-call(f32[256,128]{1,0:T(8,128)S(1)} %bitcast.20, f32[256,128]{1,0:T(8,128)S(1)} %collective-permute-done.15.even.own_even, f32[256,128]{1,0:T(8,128)S(1)} %collective-permute-done.16.odd.own_odd, ...), custom_call_target="tpu_custom_call" | custom-call | flops 16000000 | bytes 7651840 | tf_op jit(solution)/shard_map/pallas_call | solution.py:130
  92.3 0.1 collective-permute-start.23
  92.4 1.0 collective-permute-start.24
  93.4 3.5 %collective-permute-done.23.even = f32[384,128]{1,0:T(8,128)S(1)} collective-permute-done((f32[384,128]{1,0:T(8,128)S(1)}, f32[384,128]{1,0:T(8,128)S(1)}, u32[]{:S(2)}, u32[]{:S(2)}) %collective-permute-start.23) | collective-permute-done | bytes 196640 | tf_op jit(solution)/shard_map/ppermute | solution.py:27
  96.9 1.3 %collective-permute-done.24.odd = f32[384,128]{1,0:T(8,128)S(1)} collective-permute-done((f32[384,128]{1,0:T(8,128)S(1)}, f32[384,128]{1,0:T(8,128)S(1)}, u32[]{:S(2)}, u32[]{:S(2)}) %collective-permute-start.24) | collective-permute-done | bytes 196640 | tf_op jit(solution)/shard_map/ppermute | solution.py:27
  98.3 4.4 %collective-permute-start.25 = (f32[480,128]{1,0:T(8,128)S(1)}, f32[480,128]{1,0:T(8,128)S(1)}, u32[]{:S(2)}, u32[]{:S(2)}) collective-permute-start(f32[480,128]{1,0:T(8,128)S(1)} %get-tuple-element.39), channel_id=1, source_target_pairs={{0,4},{4,0},{8,12},{12,8},{16,20},{20,16},{24,28},{28,24},{32,36},... | collective-permute-start | bytes 737288 | tf_op jit(solution)/shard_map/ppermute | solution.py:27
  102.6 1.1 %collective-permute-done.25.on = f32[480,128]{1,0:T(8,128)S(1)} collective-permute-done((f32[480,128]{1,0:T(8,128)S(1)}, f32[480,128]{1,0:T(8,128)S(1)}, u32[]{:S(2)}, u32[]{:S(2)}) %collective-permute-start.25) | collective-permute-done | bytes 245792 | tf_op jit(solution)/shard_map/ppermute | solution.py:27
  103.8 4.5 %collective-permute-done.26.off = f32[480,128]{1,0:T(8,128)S(1)} collective-permute-done((f32[480,128]{1,0:T(8,128)S(1)}, f32[480,128]{1,0:T(8,128)S(1)}, u32[]{:S(2)}, u32[]{:S(2)}) %collective-permute-start.26) | collective-permute-done | bytes 245792 | tf_op jit(solution)/shard_map/ppermute | solution.py:27
  108.2 4.5 %shard_map.210 = f32[8,8,16,128]{3,2,1,0:T(8,128)} custom-call(f32[8,8,16,128]{3,2,1,0:T(8,128)S(1)} %get-tuple-element.36.start.own, f32[384,128]{1,0:T(8,128)S(1)} %collective-permute-done.23.even, f32[384,128]{1,0:T(8,128)S(1)} %collective-permute-done.24.odd, f32[480,128]{1,0:T(8,128)S(1)} %collective-permute-done.25.on, ...), custom_call_target="tpu_custom_call" | custom-call | flops 16000000 | bytes 3776512 | tf_op jit(solution)/shard_map/pallas_call | solution.py:130
  (34 shorter events, 0.2 us)
Async XLA Ops:
  0.6 65.9 %copy-start.2 = (bf16[4,4,2,128,128]{4,3,2,1,0:T(8,128)(2,1)S(1)}, bf16[4,4,2,128,128]{4,3,2,1,0:T(8,128)(2,1)}, u32[]{:S(2)}) copy-start(bf16[4,4,2,128,128]{4,3,2,1,0:T(8,128)(2,1)} %blocks.2) | copy-start | bytes 3145732
  1.6 5.2 %collective-permute-start.2 = (f32[104,128]{1,0:T(8,128)S(1)}, f32[104,128]{1,0:T(8,128)S(1)}, u32[]{:S(2)}, u32[]{:S(2)}) collective-permute-start(f32[104,128]{1,0:T(8,128)S(1)} %shard_map.201), channel_id=1, source_target_pairs={{0,3},{1,2},{2,1},{3,0},{4,7},{5,6},{6,5},{7,4},{8,11},{9,10},{10,... | collective-permute-start | bytes 159752 | tf_op jit(solution)/shard_map/ppermute | solution.py:27
  5.3 4.6 %collective-permute-start.1 = (f32[104,128]{1,0:T(8,128)S(1)}, f32[104,128]{1,0:T(8,128)S(1)}, u32[]{:S(2)}, u32[]{:S(2)}) collective-permute-start(f32[104,128]{1,0:T(8,128)S(1)} %shard_map.201), channel_id=1, source_target_pairs={{0,2},{1,3},{2,0},{3,1},{4,6},{5,7},{6,4},{7,5},{8,10},{9,11},{10,... | collective-permute-start | bytes 159752 | tf_op jit(solution)/shard_map/ppermute | solution.py:27
  5.6 4.2 %collective-permute-start = (f32[104,128]{1,0:T(8,128)S(1)}, f32[104,128]{1,0:T(8,128)S(1)}, u32[]{:S(2)}, u32[]{:S(2)}) collective-permute-start(f32[104,128]{1,0:T(8,128)S(1)} %shard_map.201), channel_id=1, source_target_pairs={{0,1},{1,0},{2,3},{3,2},{4,5},{5,4},{6,7},{7,6},{8,9},{9,8},{10,11... | collective-permute-start | bytes 159752 | tf_op jit(solution)/shard_map/ppermute | solution.py:27
  9.9 3.2 %collective-permute-start.3 = (f32[4,104,128]{2,1,0:T(8,128)S(1)}, f32[4,104,128]{2,1,0:T(8,128)S(1)}, u32[]{:S(2)}, u32[]{:S(2)}) collective-permute-start(f32[4,104,128]{2,1,0:T(8,128)S(1)} %pad_maximum_fusion.2), channel_id=1, source_target_pairs={{0,4},{4,0},{8,12},{12,8},{16,20},{20,16},{24,28},{28,24},{32,36},... | collective-permute-start | bytes 638984 | tf_op jit(solution)/shard_map/ppermute | solution.py:27
  13.1 9.3 %collective-permute-start.5 = (f32[2,4,40,128]{3,2,1,0:T(8,128)S(1)}, f32[2,4,40,128]{3,2,1,0:T(8,128)S(1)}, u32[]{:S(2)}, u32[]{:S(2)}) collective-permute-start(f32[2,4,40,128]{3,2,1,0:T(8,128)S(1)} %pad_maximum_fusion.3.pair.spair), channel_id=1, source_target_pairs={{0,244},{4,16},{8,252},{12,24},{16,4},{20,32},{24,12},{28,40},{32,... | collective-permute-start | bytes 491528 | tf_op jit(solution)/shard_map/ppermute | solution.py:27
  16.4 10.8 %collective-permute-start.4 = (f32[2,4,40,128]{3,2,1,0:T(8,128)S(1)}, f32[2,4,40,128]{3,2,1,0:T(8,128)S(1)}, u32[]{:S(2)}, u32[]{:S(2)}) collective-permute-start(f32[2,4,40,128]{3,2,1,0:T(8,128)S(1)} %pad_maximum_fusion.3.pair.spair), channel_id=1, source_target_pairs={{0,252},{4,8},{8,4},{12,16},{16,12},{20,24},{24,20},{28,32},{32,28... | collective-permute-start | bytes 491528 | tf_op jit(solution)/shard_map/ppermute | solution.py:27
  27.2 21.5 %collective-permute-start.6 = (f32[2,2,4,40,128]{4,3,2,1,0:T(8,128)S(1)}, f32[2,2,4,40,128]{4,3,2,1,0:T(8,128)S(1)}, u32[]{:S(2)}, u32[]{:S(2)}) collective-permute-start(f32[2,2,4,40,128]{4,3,2,1,0:T(8,128)S(1)} %shard_map.202), channel_id=1, source_target_pairs={{0,4},{4,0},{8,12},{12,8},{16,20},{20,16},{24,28},{28,24},{32,36},... | collective-permute-start | bytes 983048 | tf_op jit(solution)/shard_map/ppermute | solution.py:27
  31.4 54.5 %copy-start = (bf16[8,8,2,128,128]{4,3,2,1,0:T(8,128)(2,1)S(1)}, bf16[8,8,2,128,128]{4,3,2,1,0:T(8,128)(2,1)}, u32[]{:S(2)}) copy-start(bf16[8,8,2,128,128]{4,3,2,1,0:T(8,128)(2,1)} %blocks.3) | copy-start | bytes 12582916
  31.4 54.5 %copy-start.3 = (f32[8,8,16,128]{3,2,1,0:T(8,128)S(1)}, f32[8,8,16,128]{3,2,1,0:T(8,128)}, u32[]{:S(2)}) copy-start(f32[8,8,16,128]{3,2,1,0:T(8,128)} %guess.1) | copy-start | bytes 1572868
  31.4 17.0 %collective-permute-start.9 = (bf16[1232,128]{1,0:T(8,128)(2,1)S(1)}, bf16[1232,128]{1,0:T(8,128)(2,1)S(1)}, u32[]{:S(2)}, u32[]{:S(2)}) collective-permute-start(bf16[1232,128]{1,0:T(8,128)(2,1)S(1)} %get-tuple-element.24.third0), channel_id=1, source_target_pairs={{0,3},{1,2},{2,1},{3,0},{4,7},{5,6},{6,5},{7,4},{8,11},{9,10},{10,... | collective-permute-start | bytes 946184 | tf_op jit(solution)/shard_map/ppermute | solution.py:27
  32.5 15.9 %collective-permute-start.8 = (bf16[1232,128]{1,0:T(8,128)(2,1)S(1)}, bf16[1232,128]{1,0:T(8,128)(2,1)S(1)}, u32[]{:S(2)}, u32[]{:S(2)}) collective-permute-start(bf16[1232,128]{1,0:T(8,128)(2,1)S(1)} %get-tuple-element.24.third0), channel_id=1, source_target_pairs={{0,2},{1,3},{2,0},{3,1},{4,6},{5,7},{6,4},{7,5},{8,10},{9,11},{10,... | collective-permute-start | bytes 946184 | tf_op jit(solution)/shard_map/ppermute | solution.py:27
  33.3 15.5 %collective-permute-start.7 = (bf16[1232,128]{1,0:T(8,128)(2,1)S(1)}, bf16[1232,128]{1,0:T(8,128)(2,1)S(1)}, u32[]{:S(2)}, u32[]{:S(2)}) collective-permute-start(bf16[1232,128]{1,0:T(8,128)(2,1)S(1)} %get-tuple-element.24.third0), channel_id=1, source_target_pairs={{0,1},{1,0},{2,3},{3,2},{4,5},{5,4},{6,7},{7,6},{8,9},{9,8},{10,11... | collective-permute-start | bytes 946184 | tf_op jit(solution)/shard_map/ppermute | solution.py:27
  51.3 2.1 %collective-permute-start.10 = (f32[256,128]{1,0:T(8,128)S(1)}, f32[256,128]{1,0:T(8,128)S(1)}, u32[]{:S(2)}, u32[]{:S(2)}) collective-permute-start(f32[256,128]{1,0:T(8,128)S(1)} %get-tuple-element.25), channel_id=1, source_target_pairs={{0,4},{4,0},{8,12},{12,8},{16,20},{20,16},{24,28},{28,24},{32,36},... | collective-permute-start | bytes 393224 | tf_op jit(solution)/shard_map/ppermute | solution.py:27
  52.5 6.2 %collective-permute-start.13 = (f32[2,4,64,128]{3,2,1,0:T(8,128)S(1)}, f32[2,4,64,128]{3,2,1,0:T(8,128)S(1)}, u32[]{:S(2)}, u32[]{:S(2)}) collective-permute-start(f32[2,4,64,128]{3,2,1,0:T(8,128)S(1)} %pad_maximum_fusion.1.fpair), channel_id=1, source_target_pairs={{0,252},{4,8},{8,4},{12,16},{16,12},{20,24},{24,20},{28,32},{32,28... | collective-permute-start | bytes 786440 | tf_op jit(solution)/shard_map/ppermute | solution.py:27
  53.5 8.2 %collective-permute-start.11 = (f32[2,256,128]{2,1,0:T(8,128)S(1)}, f32[2,256,128]{2,1,0:T(8,128)S(1)}, u32[]{:S(2)}, u32[]{:S(2)}) collective-permute-start(f32[2,256,128]{2,1,0:T(8,128)S(1)} %pad_maximum_fusion.pair), channel_id=1, source_target_pairs={{0,252},{4,8},{8,4},{12,16},{16,12},{20,24},{24,20},{28,32},{32,28... | collective-permute-start | bytes 786440 | tf_op jit(solution)/shard_map/ppermute | solution.py:27
  54.5 10.9 %collective-permute-start.19 = (f32[544,128]{1,0:T(8,128)S(1)}, f32[544,128]{1,0:T(8,128)S(1)}, u32[]{:S(2)}, u32[]{:S(2)}) collective-permute-start(f32[544,128]{1,0:T(8,128)S(1)} %get-tuple-element.30), channel_id=1, source_target_pairs={{0,1},{1,0},{2,3},{3,2},{4,5},{5,4},{6,7},{7,6},{8,9},{9,8},{10,11... | collective-permute-start | bytes 835592 | tf_op jit(solution)/shard_map/ppermute | solution.py:27
  54.5 10.9 %collective-permute-start.20 = (f32[544,128]{1,0:T(8,128)S(1)}, f32[544,128]{1,0:T(8,128)S(1)}, u32[]{:S(2)}, u32[]{:S(2)}) collective-permute-start(f32[544,128]{1,0:T(8,128)S(1)} %get-tuple-element.31), channel_id=1, source_target_pairs={{0,3},{1,2},{2,1},{3,0},{4,7},{5,6},{6,5},{7,4},{8,11},{9,10},{10,... | collective-permute-start | bytes 835592 | tf_op jit(solution)/shard_map/ppermute | solution.py:27
  58.7 7.4 %collective-permute-start.14 = (f32[2,4,64,128]{3,2,1,0:T(8,128)S(1)}, f32[2,4,64,128]{3,2,1,0:T(8,128)S(1)}, u32[]{:S(2)}, u32[]{:S(2)}) collective-permute-start(f32[2,4,64,128]{3,2,1,0:T(8,128)S(1)} %collective-permute-done.13.fa), channel_id=1, source_target_pairs={{0,4},{4,0},{8,12},{12,8},{16,20},{20,16},{24,28},{28,24},{32,36},... | collective-permute-start | bytes 786440 | tf_op jit(solution)/shard_map/ppermute | solution.py:27
  61.7 4.8 %collective-permute-start.12 = (f32[2,256,128]{2,1,0:T(8,128)S(1)}, f32[2,256,128]{2,1,0:T(8,128)S(1)}, u32[]{:S(2)}, u32[]{:S(2)}) collective-permute-start(f32[2,256,128]{2,1,0:T(8,128)S(1)} %collective-permute-done.11.a), channel_id=1, source_target_pairs={{0,4},{4,0},{8,12},{12,8},{16,20},{20,16},{24,28},{28,24},{32,36},... | collective-permute-start | bytes 786440 | tf_op jit(solution)/shard_map/ppermute | solution.py:27
  65.5 13.9 %collective-permute-start.21 = (f32[1224,128]{1,0:T(8,128)S(1)}, f32[1224,128]{1,0:T(8,128)S(1)}, u32[]{:S(2)}, u32[]{:S(2)}) collective-permute-start(f32[1224,128]{1,0:T(8,128)S(1)} %get-tuple-element.34), channel_id=1, source_target_pairs={{0,4},{4,0},{8,12},{12,8},{16,20},{20,16},{24,28},{28,24},{32,36},... | collective-permute-start | bytes 1880072 | tf_op jit(solution)/shard_map/ppermute | solution.py:27
  66.1 13.3 %collective-permute-start.22 = (f32[1224,128]{1,0:T(8,128)S(1)}, f32[1224,128]{1,0:T(8,128)S(1)}, u32[]{:S(2)}, u32[]{:S(2)}) collective-permute-start(f32[1224,128]{1,0:T(8,128)S(1)} %get-tuple-element.35), channel_id=1, source_target_pairs={{0,252},{4,8},{8,4},{12,16},{16,12},{20,24},{24,20},{28,32},{32,28... | collective-permute-start | bytes 1880072 | tf_op jit(solution)/shard_map/ppermute | solution.py:27
  69.8 5.4 %collective-permute-start.16 = (f32[256,128]{1,0:T(8,128)S(1)}, f32[256,128]{1,0:T(8,128)S(1)}, u32[]{:S(2)}, u32[]{:S(2)}) collective-permute-start(f32[256,128]{1,0:T(8,128)S(1)} %bitcast.17), channel_id=1, source_target_pairs={{0,3},{1,2},{2,1},{3,0},{4,7},{5,6},{6,5},{7,4},{8,11},{9,10},{10,... | collective-permute-start | bytes 393224 | tf_op jit(solution)/shard_map/ppermute | solution.py:27
  71.4 4.1 %collective-permute-start.15 = (f32[256,128]{1,0:T(8,128)S(1)}, f32[256,128]{1,0:T(8,128)S(1)}, u32[]{:S(2)}, u32[]{:S(2)}) collective-permute-start(f32[256,128]{1,0:T(8,128)S(1)} %bitcast.18), channel_id=1, source_target_pairs={{0,1},{1,0},{2,3},{3,2},{4,5},{5,4},{6,7},{7,6},{8,9},{9,8},{10,11... | collective-permute-start | bytes 393224 | tf_op jit(solution)/shard_map/ppermute | solution.py:27
  75.6 5.0 %collective-permute-start.17 = (f32[576,128]{1,0:T(8,128)S(1)}, f32[576,128]{1,0:T(8,128)S(1)}, u32[]{:S(2)}, u32[]{:S(2)}) collective-permute-start(f32[576,128]{1,0:T(8,128)S(1)} %get-tuple-element.27), channel_id=1, source_target_pairs={{0,4},{4,0},{8,12},{12,8},{16,20},{20,16},{24,28},{28,24},{32,36},... | collective-permute-start | bytes 884744 | tf_op jit(solution)/shard_map/ppermute | solution.py:27
  79.4 6.4 %collective-permute-start.18 = (f32[576,128]{1,0:T(8,128)S(1)}, f32[576,128]{1,0:T(8,128)S(1)}, u32[]{:S(2)}, u32[]{:S(2)}) collective-permute-start(f32[576,128]{1,0:T(8,128)S(1)} %get-tuple-element.28), channel_id=1, source_target_pairs={{0,252},{4,8},{8,4},{12,16},{16,12},{20,24},{24,20},{28,32},{32,28... | collective-permute-start | bytes 884744 | tf_op jit(solution)/shard_map/ppermute | solution.py:27
  85.8 22.4 %copy-start.1 = (f32[8,8,16,128]{3,2,1,0:T(8,128)S(1)}, f32[8,8,16,128]{3,2,1,0:T(8,128)}, u32[]{:S(2)}) copy-start(f32[8,8,16,128]{3,2,1,0:T(8,128)} %fown.1) | copy-start | bytes 1572868
  85.8 22.4 %copy-start.4 = (f32[8,8,128]{2,1,0:T(8,128)S(1)}, f32[8,8,128]{2,1,0:T(8,128)}, u32[]{:S(2)}) copy-start(f32[8,8,128]{2,1,0:T(8,128)} %sown.1) | copy-start | bytes 98308
  92.3 4.6 %collective-permute-start.23 = (f32[384,128]{1,0:T(8,128)S(1)}, f32[384,128]{1,0:T(8,128)S(1)}, u32[]{:S(2)}, u32[]{:S(2)}) collective-permute-start(f32[384,128]{1,0:T(8,128)S(1)} %get-tuple-element.37), channel_id=1, source_target_pairs={{0,1},{1,0},{2,3},{3,2},{4,5},{5,4},{6,7},{7,6},{8,9},{9,8},{10,11... | collective-permute-start | bytes 589832 | tf_op jit(solution)/shard_map/ppermute | solution.py:27
  92.4 5.8 %collective-permute-start.24 = (f32[384,128]{1,0:T(8,128)S(1)}, f32[384,128]{1,0:T(8,128)S(1)}, u32[]{:S(2)}, u32[]{:S(2)}) collective-permute-start(f32[384,128]{1,0:T(8,128)S(1)} %get-tuple-element.38), channel_id=1, source_target_pairs={{0,3},{1,2},{2,1},{3,0},{4,7},{5,6},{6,5},{7,4},{8,11},{9,10},{10,... | collective-permute-start | bytes 589832 | tf_op jit(solution)/shard_map/ppermute | solution.py:27
  98.3 5.5 %collective-permute-start.25 = (f32[480,128]{1,0:T(8,128)S(1)}, f32[480,128]{1,0:T(8,128)S(1)}, u32[]{:S(2)}, u32[]{:S(2)}) collective-permute-start(f32[480,128]{1,0:T(8,128)S(1)} %get-tuple-element.39), channel_id=1, source_target_pairs={{0,4},{4,0},{8,12},{12,8},{16,20},{20,16},{24,28},{28,24},{32,36},... | collective-permute-start | bytes 737288 | tf_op jit(solution)/shard_map/ppermute | solution.py:27
  102.6 5.6 %collective-permute-start.26 = (f32[480,128]{1,0:T(8,128)S(1)}, f32[480,128]{1,0:T(8,128)S(1)}, u32[]{:S(2)}, u32[]{:S(2)}) collective-permute-start(f32[480,128]{1,0:T(8,128)S(1)} %get-tuple-element.40), channel_id=1, source_target_pairs={{0,252},{4,8},{8,4},{12,16},{16,12},{20,24},{24,20},{28,32},{32,28... | collective-permute-start | bytes 737288 | tf_op jit(solution)/shard_map/ppermute | solution.py:27

commit v4 on v3

--- a/solution.py
+++ b/solution.py
@@ -60,7 +60,7 @@
     return mid, beside
 
 
-def smooth(u, f, s, res, d0, d1, emit, low, rows, width, wrap):
+def smooth(u, f, s, res, d0, d1, emit, low, rows, width, wrap, row_done=lambda i: None):
     def columns(k):
         return range(width) if wrap else range(k, width - k)
 
@@ -86,6 +86,7 @@
             r = res[i, j] - ((6.0 + s[i, j]) * mid - beside)
             d2 = (FACTOR2 * FACTOR1) * mid + (2.0 * FACTOR2 / HALF) * r
             emit(i, j, u[i, j] + d0[i, j] + mid + d2)
+        row_done(i)
         return carry
 
     lax.fori_loop(low + 1, low + 5 + rows, first, 0)
@@ -94,13 +95,9 @@
 
 
 def prolong_cell(lines, index, blocks, guess, a, b):
-    total = guess[a, b]
-    for k in range(2):
-        ri, ci = index(a, b, k)
-        total = total + lax.dot_general(
-            lines[ri, ci], blocks[a, b, k], (((1,), (1,)), ((), ())), preferred_element_type=F32
-        )
-    return total
+    pair = jnp.concatenate([lines[index(a, b, k)] for k in range(2)], axis=1)
+    both = jnp.concatenate([blocks[a, b, k] for k in range(2)], axis=1)
+    return guess[a, b] + lax.dot_general(pair, both, (((1,), (1,)), ((), ())), preferred_element_type=F32)
 
 
 VMEM = pl.BlockSpec(memory_space=pltpu.VMEM)
@@ -123,7 +120,7 @@
     return [*first[:-1], pltpu.SMEM(arrays[-1].shape, arrays[-1].dtype), sems]
 
 
-def call(kernel, inputs, outs, scratch, flops, vmem=16, hbm=()):
+def call(kernel, inputs, outs, scratch, flops, vmem=16, hbm=(), out=None):
     nbytes = sum(x.size * x.dtype.itemsize for x in inputs)
     specs = [HBM if n in hbm else VMEM for n in range(len(inputs))]
     inputs = [pltpu.with_memory_space_constraint(x, pltpu.HBM) if n in hbm else x for n, x in enumerate(inputs)]
@@ -131,7 +128,7 @@
         kernel,
         out_shape=outs,
         in_specs=specs,
-        out_specs=jax.tree.map(lambda _: VMEM, outs),
+        out_specs=tuple(out or VMEM for _ in outs),
         scratch_shapes=scratch,
         compiler_params=pltpu.CompilerParams(vmem_limit_bytes=vmem << 20),
         cost_estimate=pl.CostEstimate(flops=flops, bytes_accessed=nbytes, transcendentals=0),
@@ -446,7 +443,7 @@
                 ref[at : at + R, :] = at_cell(beside, row * 3 + n + left * (2 - 2 * n))
 
 
-def first_kernel(own, even, odd, on, off, fown, sown, feven, fodd, fon, foff, out, u, f, s, res, d0, d1):
+def first_kernel(own, even, odd, on, off, fown, sown, feven, fodd, fon, foff, out, u, f, s, res, d0, d1, done, sems):
     gz, gy = lax.axis_index("gz"), lax.axis_index("gy")
     core, side = lax.rem(gz, 2), lax.rem(gy, 2)
     even_u, odd_u = 11 - 11 * side, 11 * side
@@ -490,9 +487,18 @@
     place(off, foff, 1 - core, 1 + 10 * core)
 
     def emit(i, j, value):
-        out[i - 3, j - 3] = value
-
-    smooth(u, f, s, res, d0, d1, emit, 0, 8, 14, False)
+        done[i - 3, j - 3] = value
+
+    def leave(i):
+        return pltpu.make_async_copy(done.at[i], out.at[i], sems.at[i])
+
+    smooth(u, f, s, res, d0, d1, emit, 0, 8, 14, False, lambda i: leave(i - 3).start())
+    for i in range(8):
+        leave(i).wait()
+
+
+def onchip(*shape):
+    return pltpu.VMEM(shape, F32)
 
 
 def sds(*shape, dtype=F32):
@@ -561,7 +567,7 @@
     out_fourth, start_third = call(
         fourth_kernel,
         (pair, near, far, both, third, third1, third2, third3),
-        (sds(1, 1, R, L), sds(256, L)),
+        (onchip(1, 1, R, L), sds(256, L)),
         smoothing_scratch(10, 4) + [cells(3, 4)],
         4_000_000, 6,
     )
@@ -573,7 +579,7 @@
     out_third, start_second = call(
         third_kernel,
         (pair3, near3, near3_b, pair_f, near_f, near_fb, pair, near, both, links_second, blocks_second, guess_second),
-        (sds(2, 2, R, L), sds(4, 4, R, L)),
+        (onchip(2, 2, R, L), sds(4, 4, R, L)),
         smoothing_scratch(12, 8) + [cells(4, 8, BF16)] + smem_last(guess_second, links_second),
         8_000_000, 12, (9, 11),
     )
@@ -584,7 +590,7 @@
     out_second, start_first, strip_even, strip_odd = call(
         second_kernel,
         (own, own_even, own_odd, z_on(block_on), z_off(block_off), mine, ahead_even, ahead_odd, ahead_on, ahead_off, links_first, blocks_first, guess_first),
-        (sds(4, 4, R, L), sds(8, 8, R, L), sds(24 * R, L), sds(24 * R, L)),
+        (onchip(4, 4, R, L), sds(8, 8, R, L), sds(24 * R, L), sds(24 * R, L)),
         smoothing_scratch(12, 12) + [cells(6, 6, BF16)] + smem_last(links_first),
         16_000_000, 20, (10,),
     )
@@ -595,8 +601,8 @@
         first_kernel,
         (start_first, u_even, u_odd, z_on(u_on), z_off(u_off), source_first, shift_first, ahead_even, ahead_odd, ahead_on, ahead_off),
         (sds(8, 8, R, L),),
-        smoothing_scratch(14, 14),
-        16_000_000, 20,
+        smoothing_scratch(14, 14) + [cells(8, 8), pltpu.SemaphoreType.DMA((8,))],
+        16_000_000, 20, (), HBM,
     )
     return out_first, out_second, out_third, out_fourth
 

time: 114 us -> 112 us (0.982)
  Pallas kernels: 19.3 us -> 16.7 us
  waiting for transfers between devices: 48.3 us -> 46.4 us
  local copies, waits for them, and re-layouts: 0.06 us -> 1.92 us
    pallas_call x10, Pallas kernels: 19.3 us -> 16.7 us  [call(): pl.pallas_call(kernel, out_shape=outs, in_specs=specs, out_specs=tuple((o...]
    ppermute x27, waiting for transfers between devices: 48.3 us -> 46.4 us  [swap(): lax.ppermute(x, axis, [(i, partner(i)) for i in range(lax.axis_size(axis))])]
    unnamed x10 -> x13, local copies, waits for them, and re-layouts: 0.02 us -> 1.89 us
  transfers between devices with their start and end apart: 27 -> 27, of which waited for: 17 -> 16; matrix products, arithmetic and copies ran while one was open for 0% -> 2% of each run, Pallas kernels for 4% -> 4%
where the time goes in v4:
time: 112 us; the launch traced here: 110 us
  waiting for transfers between devices  46.4 us (41%)
  starting transfers between devices  44.2 us (39%)
  Pallas kernels  16.7 us (15%)
  local copies, waits for them, and re-layouts  1.92 us (2%)
    ppermute x27, waiting for transfers between devices, swap(): lax.ppermute(x, axis, [(i, partner(i)) for i in range(lax.axis_size(axis))])  46.4 us
    ppermute x27, starting transfers between devices, swap(): lax.ppermute(x, axis, [(i, partner(i)) for i in range(lax.axis_size(axis))])  44.2 us
    pallas_call x10, Pallas kernels, call(): pl.pallas_call(kernel, out_shape=outs, in_specs=specs, out_specs=tuple((o...  16.7 us
  transfers between devices with their start and end apart: 27, of which 16 were waited for; matrix products, arithmetic and copies ran while one was open for 2% of the time, Pallas kernels for 4%

profile of v4, /device:TPU:1, one launch (start us, length us, event | category | flops | bytes accessed | tf_op | source)
XLA Modules:
  0.0 110.4 jit_solution(12688741486694503171)
XLA Ops:
  0.6 1.0 shard_map.201
  1.6 3.6 %collective-permute-start.2 = (f32[104,128]{1,0:T(8,128)S(1)}, f32[104,128]{1,0:T(8,128)S(1)}, u32[]{:S(2)}, u32[]{:S(2)}) collective-permute-start(f32[104,128]{1,0:T(8,128)S(1)} %shard_map.201), channel_id=1, source_target_pairs={{0,3},{1,2},{2,1},{3,0},{4,7},{5,6},{6,5},{7,4},{8,11},{9,10},{10,... | collective-permute-start | bytes 159752 | tf_op jit(solution)/shard_map/ppermute | solution.py:27
  5.3 0.3 collective-permute-start.1
  5.6 0.3 collective-permute-start
  5.9 0.8 collective-permute-done.2
  6.8 3.1 %collective-permute-done.1 = f32[104,128]{1,0:T(8,128)S(1)} collective-permute-done((f32[104,128]{1,0:T(8,128)S(1)}, f32[104,128]{1,0:T(8,128)S(1)}, u32[]{:S(2)}, u32[]{:S(2)}) %collective-permute-start.1) | collective-permute-done | bytes 53280 | tf_op jit(solution)/shard_map/ppermute | solution.py:27
  9.9 2.1 %collective-permute-start.3 = (f32[4,104,128]{2,1,0:T(8,128)S(1)}, f32[4,104,128]{2,1,0:T(8,128)S(1)}, u32[]{:S(2)}, u32[]{:S(2)}) collective-permute-start(f32[4,104,128]{2,1,0:T(8,128)S(1)} %pad_maximum_fusion.2), channel_id=1, source_target_pairs={{0,4},{4,0},{8,12},{12,8},{16,20},{20,16},{24,28},{28,24},{32,36},... | collective-permute-start | bytes 638984 | tf_op jit(solution)/shard_map/ppermute | solution.py:27
  12.0 1.1 collective-permute-done.3
  13.1 3.3 %collective-permute-start.5 = (f32[2,4,40,128]{3,2,1,0:T(8,128)S(1)}, f32[2,4,40,128]{3,2,1,0:T(8,128)S(1)}, u32[]{:S(2)}, u32[]{:S(2)}) collective-permute-start(f32[2,4,40,128]{3,2,1,0:T(8,128)S(1)} %pad_maximum_fusion.3.pair.spair), channel_id=1, source_target_pairs={{0,244},{4,16},{8,252},{12,24},{16,4},{20,32},{24,12},{28,40},{32,... | collective-permute-start | bytes 491528 | tf_op jit(solution)/shard_map/ppermute | solution.py:27
  16.4 6.0 %collective-permute-start.4 = (f32[2,4,40,128]{3,2,1,0:T(8,128)S(1)}, f32[2,4,40,128]{3,2,1,0:T(8,128)S(1)}, u32[]{:S(2)}, u32[]{:S(2)}) collective-permute-start(f32[2,4,40,128]{3,2,1,0:T(8,128)S(1)} %pad_maximum_fusion.3.pair.spair), channel_id=1, source_target_pairs={{0,252},{4,8},{8,4},{12,16},{16,12},{20,24},{24,20},{28,32},{32,28... | collective-permute-start | bytes 491528 | tf_op jit(solution)/shard_map/ppermute | solution.py:27
  22.4 4.8 %collective-permute-done.4.near.a.sa = f32[2,4,40,128]{3,2,1,0:T(8,128)S(1)} collective-permute-done((f32[2,4,40,128]{3,2,1,0:T(8,128)S(1)}, f32[2,4,40,128]{3,2,1,0:T(8,128)S(1)}, u32[]{:S(2)}, u32[]{:S(2)}) %collective-permute-start.4) | collective-permute-done | bytes 163872 | tf_op jit(solution)/shard_map/ppermute | solution.py:27
  27.2 2.7 %collective-permute-start.6 = (f32[2,2,4,40,128]{4,3,2,1,0:T(8,128)S(1)}, f32[2,2,4,40,128]{4,3,2,1,0:T(8,128)S(1)}, u32[]{:S(2)}, u32[]{:S(2)}) collective-permute-start(f32[2,2,4,40,128]{4,3,2,1,0:T(8,128)S(1)} %shard_map.202), channel_id=1, source_target_pairs={{0,4},{4,0},{8,12},{12,8},{16,20},{20,16},{24,28},{28,24},{32,36},... | collective-permute-start | bytes 983048 | tf_op jit(solution)/shard_map/ppermute | solution.py:27
  30.0 1.4 %shard_map.203 = (bf16[1232,128]{1,0:T(8,128)(2,1)S(1)}, f32[272,128]{1,0:T(8,128)S(1)}, f32[544,128]{1,0:T(8,128)S(1)}, f32[544,128]{1,0:T(8,128)S(1)}, f32[272,128]{1,0:T(8,128)S(1)}, /*index=5*/f32[272,128]{1,0:T(8,128)S(1)}) custom-call(f32[8,8,16,128]{3,2,1,0:T(8,128)} %fown.1, f32[8,8,128]{2,1,0:T(8,128)} %sown.1, f32[4,4,16,128]{3,2,1,0:T(8,128)} %source_second_h.1, ...), custom_call_target="tpu_custom_call" | custom-call | flops 1000 | bytes 991264 | tf_op jit(solution)/shard_map/pallas_call | solution.py:127
  31.4 1.1 %collective-permute-start.9 = (bf16[1232,128]{1,0:T(8,128)(2,1)S(1)}, bf16[1232,128]{1,0:T(8,128)(2,1)S(1)}, u32[]{:S(2)}, u32[]{:S(2)}) collective-permute-start(bf16[1232,128]{1,0:T(8,128)(2,1)S(1)} %get-tuple-element.24.third0), channel_id=1, source_target_pairs={{0,3},{1,2},{2,1},{3,0},{4,7},{5,6},{6,5},{7,4},{8,11},{9,10},{10,... | collective-permute-start | bytes 946184 | tf_op jit(solution)/shard_map/ppermute | solution.py:27
  32.5 0.8 collective-permute-start.8
  33.3 1.4 %collective-permute-start.7 = (bf16[1232,128]{1,0:T(8,128)(2,1)S(1)}, bf16[1232,128]{1,0:T(8,128)(2,1)S(1)}, u32[]{:S(2)}, u32[]{:S(2)}) collective-permute-start(bf16[1232,128]{1,0:T(8,128)(2,1)S(1)} %get-tuple-element.24.third0), channel_id=1, source_target_pairs={{0,1},{1,0},{2,3},{3,2},{4,5},{5,4},{6,7},{7,6},{8,9},{9,8},{10,11... | collective-permute-start | bytes 946184 | tf_op jit(solution)/shard_map/ppermute | solution.py:27
  34.7 13.7 %collective-permute-done.9.third3 = bf16[1232,128]{1,0:T(8,128)(2,1)S(1)} collective-permute-done((bf16[1232,128]{1,0:T(8,128)(2,1)S(1)}, bf16[1232,128]{1,0:T(8,128)(2,1)S(1)}, u32[]{:S(2)}, u32[]{:S(2)}) %collective-permute-start.9) | collective-permute-done | bytes 315424 | tf_op jit(solution)/shard_map/ppermute | solution.py:27
  48.4 0.3 collective-permute-done.7.third1
  48.8 2.1 %shard_map.204 = (f32[1,1,16,128]{3,2,1,0:T(8,128)S(1)}, f32[256,128]{1,0:T(8,128)S(1)}) custom-call(f32[2,4,40,128]{3,2,1,0:T(8,128)S(1)} %pad_maximum_fusion.3.pair.spair, f32[2,4,40,128]{3,2,1,0:T(8,128)S(1)} %collective-permute-done.4.near.a.sa, f32[2,4,40,128]{3,2,1,0:T(8,128)S(1)} %collective-permute-done.5.far.a3, ...), custom_call_target="tpu_custom_call" | custom-call | flops 4000000 | bytes 2080768 | tf_op jit(solution)/shard_map/pallas_call | solution.py:127
  50.8 1.2 %collective-permute-start.10 = (f32[256,128]{1,0:T(8,128)S(1)}, f32[256,128]{1,0:T(8,128)S(1)}, u32[]{:S(2)}, u32[]{:S(2)}) collective-permute-start(f32[256,128]{1,0:T(8,128)S(1)} %get-tuple-element.25), channel_id=1, source_target_pairs={{0,4},{4,0},{8,12},{12,8},{16,20},{20,16},{24,28},{28,24},{32,36},... | collective-permute-start | bytes 393224 | tf_op jit(solution)/shard_map/ppermute | solution.py:27
  52.1 0.1 collective-permute-start.13
  52.2 0.8 collective-permute-done.10
  53.0 1.0 collective-permute-start.11
  54.1 2.0 %collective-permute-start.20 = (f32[544,128]{1,0:T(8,128)S(1)}, f32[544,128]{1,0:T(8,128)S(1)}, u32[]{:S(2)}, u32[]{:S(2)}) collective-permute-start(f32[544,128]{1,0:T(8,128)S(1)} %get-tuple-element.31), channel_id=1, source_target_pairs={{0,3},{1,2},{2,1},{3,0},{4,7},{5,6},{6,5},{7,4},{8,11},{9,10},{10,... | collective-permute-start | bytes 835592 | tf_op jit(solution)/shard_map/ppermute | solution.py:27
  56.0 2.2 %collective-permute-done.13.fa = f32[2,4,64,128]{3,2,1,0:T(8,128)S(1)} collective-permute-done((f32[2,4,64,128]{3,2,1,0:T(8,128)S(1)}, f32[2,4,64,128]{3,2,1,0:T(8,128)S(1)}, u32[]{:S(2)}, u32[]{:S(2)}) %collective-permute-start.13) | collective-permute-done | bytes 262176 | tf_op jit(solution)/shard_map/ppermute | solution.py:27
  58.2 3.0 %collective-permute-start.14 = (f32[2,4,64,128]{3,2,1,0:T(8,128)S(1)}, f32[2,4,64,128]{3,2,1,0:T(8,128)S(1)}, u32[]{:S(2)}, u32[]{:S(2)}) collective-permute-start(f32[2,4,64,128]{3,2,1,0:T(8,128)S(1)} %collective-permute-done.13.fa), channel_id=1, source_target_pairs={{0,4},{4,0},{8,12},{12,8},{16,20},{20,16},{24,28},{28,24},{32,36},... | collective-permute-start | bytes 786440 | tf_op jit(solution)/shard_map/ppermute | solution.py:27
  61.3 3.6 %collective-permute-start.12 = (f32[2,256,128]{2,1,0:T(8,128)S(1)}, f32[2,256,128]{2,1,0:T(8,128)S(1)}, u32[]{:S(2)}, u32[]{:S(2)}) collective-permute-start(f32[2,256,128]{2,1,0:T(8,128)S(1)} %collective-permute-done.11.a), channel_id=1, source_target_pairs={{0,4},{4,0},{8,12},{12,8},{16,20},{20,16},{24,28},{28,24},{32,36},... | collective-permute-start | bytes 786440 | tf_op jit(solution)/shard_map/ppermute | solution.py:27
  64.9 0.1 shard_map.207
  65.0 0.6 collective-permute-start.21
  65.6 0.5 collective-permute-done.12.b
  66.1 2.7 %shard_map.205 = (f32[2,2,16,128]{3,2,1,0:T(8,128)S(1)}, f32[4,4,16,128]{3,2,1,0:T(8,128)S(1)}) custom-call(f32[2,256,128]{2,1,0:T(8,128)S(1)} %pad_maximum_fusion.pair, f32[2,256,128]{2,1,0:T(8,128)S(1)} %collective-permute-done.11.a, f32[2,256,128]{2,1,0:T(8,128)S(1)} %collective-permute-done.12.b, f32[2,4,64,128]{3,2,1,0:T(8,128)S(1)} %pad_maximum_fusion.1.fpair, ...), custom_call_target="tpu_custom_call" | custom-call | flops 8000000 | bytes 3408000 | tf_op jit(solution)/shard_map/pallas_call | solution.py:127
  68.7 1.6 %collective-permute-start.16 = (f32[256,128]{1,0:T(8,128)S(1)}, f32[256,128]{1,0:T(8,128)S(1)}, u32[]{:S(2)}, u32[]{:S(2)}) collective-permute-start(f32[256,128]{1,0:T(8,128)S(1)} %bitcast.17), channel_id=1, source_target_pairs={{0,3},{1,2},{2,1},{3,0},{4,7},{5,6},{6,5},{7,4},{8,11},{9,10},{10,... | collective-permute-start | bytes 393224 | tf_op jit(solution)/shard_map/ppermute | solution.py:27
  70.4 3.8 %collective-permute-done.16.odd.own_odd = f32[256,128]{1,0:T(8,128)S(1)} collective-permute-done((f32[256,128]{1,0:T(8,128)S(1)}, f32[256,128]{1,0:T(8,128)S(1)}, u32[]{:S(2)}, u32[]{:S(2)}) %collective-permute-start.16) | collective-permute-done | bytes 131104 | tf_op jit(solution)/shard_map/ppermute | solution.py:27
  74.2 0.3 collective-permute-done.15.even.own_even
  74.5 3.8 %collective-permute-start.17 = (f32[576,128]{1,0:T(8,128)S(1)}, f32[576,128]{1,0:T(8,128)S(1)}, u32[]{:S(2)}, u32[]{:S(2)}) collective-permute-start(f32[576,128]{1,0:T(8,128)S(1)} %get-tuple-element.27), channel_id=1, source_target_pairs={{0,4},{4,0},{8,12},{12,8},{16,20},{20,16},{24,28},{28,24},{32,36},... | collective-permute-start | bytes 884744 | tf_op jit(solution)/shard_map/ppermute | solution.py:27
  78.3 1.2 %collective-permute-done.17.on = f32[576,128]{1,0:T(8,128)S(1)} collective-permute-done((f32[576,128]{1,0:T(8,128)S(1)}, f32[576,128]{1,0:T(8,128)S(1)}, u32[]{:S(2)}, u32[]{:S(2)}) %collective-permute-start.17) | collective-permute-done | bytes 294944 | tf_op jit(solution)/shard_map/ppermute | solution.py:27
  79.5 5.2 %collective-permute-done.18.off = f32[576,128]{1,0:T(8,128)S(1)} collective-permute-done((f32[576,128]{1,0:T(8,128)S(1)}, f32[576,128]{1,0:T(8,128)S(1)}, u32[]{:S(2)}, u32[]{:S(2)}) %collective-permute-start.18) | collective-permute-done | bytes 294944 | tf_op jit(solution)/shard_map/ppermute | solution.py:27
  84.8 5.1 %shard_map.208 = (f32[4,4,16,128]{3,2,1,0:T(8,128)S(1)}, f32[8,8,16,128]{3,2,1,0:T(8,128)S(1)}, f32[384,128]{1,0:T(8,128)S(1)}, f32[384,128]{1,0:T(8,128)S(1)}) custom-call(f32[256,128]{1,0:T(8,128)S(1)} %bitcast.20, f32[256,128]{1,0:T(8,128)S(1)} %collective-permute-done.15.even.own_even, f32[256,128]{1,0:T(8,128)S(1)} %collective-permute-done.16.odd.own_odd, ...), custom_call_target="tpu_custom_call" | custom-call | flops 16000000 | bytes 7651840 | tf_op jit(solution)/shard_map/pallas_call | solution.py:127
  89.9 0.1 collective-permute-start.23
  90.0 1.0 collective-permute-start.24
  91.0 3.5 %collective-permute-done.23.even = f32[384,128]{1,0:T(8,128)S(1)} collective-permute-done((f32[384,128]{1,0:T(8,128)S(1)}, f32[384,128]{1,0:T(8,128)S(1)}, u32[]{:S(2)}, u32[]{:S(2)}) %collective-permute-start.23) | collective-permute-done | bytes 196640 | tf_op jit(solution)/shard_map/ppermute | solution.py:27
  94.5 1.3 %collective-permute-done.24.odd = f32[384,128]{1,0:T(8,128)S(1)} collective-permute-done((f32[384,128]{1,0:T(8,128)S(1)}, f32[384,128]{1,0:T(8,128)S(1)}, u32[]{:S(2)}, u32[]{:S(2)}) %collective-permute-start.24) | collective-permute-done | bytes 196640 | tf_op jit(solution)/shard_map/ppermute | solution.py:27
  95.8 4.4 %collective-permute-start.25 = (f32[480,128]{1,0:T(8,128)S(1)}, f32[480,128]{1,0:T(8,128)S(1)}, u32[]{:S(2)}, u32[]{:S(2)}) collective-permute-start(f32[480,128]{1,0:T(8,128)S(1)} %get-tuple-element.39), channel_id=1, source_target_pairs={{0,4},{4,0},{8,12},{12,8},{16,20},{20,16},{24,28},{28,24},{32,36},... | collective-permute-start | bytes 737288 | tf_op jit(solution)/shard_map/ppermute | solution.py:27
  100.2 0.6 copy.24
  100.8 0.6 copy.23
  101.4 0.7 copy.22
  102.1 3.7 %collective-permute-done.26.off = f32[480,128]{1,0:T(8,128)S(1)} collective-permute-done((f32[480,128]{1,0:T(8,128)S(1)}, f32[480,128]{1,0:T(8,128)S(1)}, u32[]{:S(2)}, u32[]{:S(2)}) %collective-permute-start.26) | collective-permute-done | bytes 245792 | tf_op jit(solution)/shard_map/ppermute | solution.py:27
  105.8 4.4 %shard_map.210 = f32[8,8,16,128]{3,2,1,0:T(8,128)} custom-call(f32[8,8,16,128]{3,2,1,0:T(8,128)S(1)} %get-tuple-element.36.start.own, f32[384,128]{1,0:T(8,128)S(1)} %collective-permute-done.23.even, f32[384,128]{1,0:T(8,128)S(1)} %collective-permute-done.24.odd, f32[480,128]{1,0:T(8,128)S(1)} %collective-permute-done.25.on, ...), custom_call_target="tpu_custom_call" | custom-call | flops 16000000 | bytes 3776512 | tf_op jit(solution)/shard_map/pallas_call | solution.py:127
  (37 shorter events, 0.3 us)
Async XLA Ops:
  0.6 65.4 %copy-start.2 = (bf16[4,4,2,128,128]{4,3,2,1,0:T(8,128)(2,1)S(1)}, bf16[4,4,2,128,128]{4,3,2,1,0:T(8,128)(2,1)}, u32[]{:S(2)}) copy-start(bf16[4,4,2,128,128]{4,3,2,1,0:T(8,128)(2,1)} %blocks.2) | copy-start | bytes 3145732
  1.6 5.2 %collective-permute-start.2 = (f32[104,128]{1,0:T(8,128)S(1)}, f32[104,128]{1,0:T(8,128)S(1)}, u32[]{:S(2)}, u32[]{:S(2)}) collective-permute-start(f32[104,128]{1,0:T(8,128)S(1)} %shard_map.201), channel_id=1, source_target_pairs={{0,3},{1,2},{2,1},{3,0},{4,7},{5,6},{6,5},{7,4},{8,11},{9,10},{10,... | collective-permute-start | bytes 159752 | tf_op jit(solution)/shard_map/ppermute | solution.py:27
  5.3 4.6 %collective-permute-start.1 = (f32[104,128]{1,0:T(8,128)S(1)}, f32[104,128]{1,0:T(8,128)S(1)}, u32[]{:S(2)}, u32[]{:S(2)}) collective-permute-start(f32[104,128]{1,0:T(8,128)S(1)} %shard_map.201), channel_id=1, source_target_pairs={{0,2},{1,3},{2,0},{3,1},{4,6},{5,7},{6,4},{7,5},{8,10},{9,11},{10,... | collective-permute-start | bytes 159752 | tf_op jit(solution)/shard_map/ppermute | solution.py:27
  5.6 4.2 %collective-permute-start = (f32[104,128]{1,0:T(8,128)S(1)}, f32[104,128]{1,0:T(8,128)S(1)}, u32[]{:S(2)}, u32[]{:S(2)}) collective-permute-start(f32[104,128]{1,0:T(8,128)S(1)} %shard_map.201), channel_id=1, source_target_pairs={{0,1},{1,0},{2,3},{3,2},{4,5},{5,4},{6,7},{7,6},{8,9},{9,8},{10,11... | collective-permute-start | bytes 159752 | tf_op jit(solution)/shard_map/ppermute | solution.py:27
  9.9 3.2 %collective-permute-start.3 = (f32[4,104,128]{2,1,0:T(8,128)S(1)}, f32[4,104,128]{2,1,0:T(8,128)S(1)}, u32[]{:S(2)}, u32[]{:S(2)}) collective-permute-start(f32[4,104,128]{2,1,0:T(8,128)S(1)} %pad_maximum_fusion.2), channel_id=1, source_target_pairs={{0,4},{4,0},{8,12},{12,8},{16,20},{20,16},{24,28},{28,24},{32,36},... | collective-permute-start | bytes 638984 | tf_op jit(solution)/shard_map/ppermute | solution.py:27
  13.1 9.3 %collective-permute-start.5 = (f32[2,4,40,128]{3,2,1,0:T(8,128)S(1)}, f32[2,4,40,128]{3,2,1,0:T(8,128)S(1)}, u32[]{:S(2)}, u32[]{:S(2)}) collective-permute-start(f32[2,4,40,128]{3,2,1,0:T(8,128)S(1)} %pad_maximum_fusion.3.pair.spair), channel_id=1, source_target_pairs={{0,244},{4,16},{8,252},{12,24},{16,4},{20,32},{24,12},{28,40},{32,... | collective-permute-start | bytes 491528 | tf_op jit(solution)/shard_map/ppermute | solution.py:27
  16.4 10.8 %collective-permute-start.4 = (f32[2,4,40,128]{3,2,1,0:T(8,128)S(1)}, f32[2,4,40,128]{3,2,1,0:T(8,128)S(1)}, u32[]{:S(2)}, u32[]{:S(2)}) collective-permute-start(f32[2,4,40,128]{3,2,1,0:T(8,128)S(1)} %pad_maximum_fusion.3.pair.spair), channel_id=1, source_target_pairs={{0,252},{4,8},{8,4},{12,16},{16,12},{20,24},{24,20},{28,32},{32,28... | collective-permute-start | bytes 491528 | tf_op jit(solution)/shard_map/ppermute | solution.py:27
  27.2 21.5 %collective-permute-start.6 = (f32[2,2,4,40,128]{4,3,2,1,0:T(8,128)S(1)}, f32[2,2,4,40,128]{4,3,2,1,0:T(8,128)S(1)}, u32[]{:S(2)}, u32[]{:S(2)}) collective-permute-start(f32[2,2,4,40,128]{4,3,2,1,0:T(8,128)S(1)} %shard_map.202), channel_id=1, source_target_pairs={{0,4},{4,0},{8,12},{12,8},{16,20},{20,16},{24,28},{28,24},{32,36},... | collective-permute-start | bytes 983048 | tf_op jit(solution)/shard_map/ppermute | solution.py:27
  31.4 53.4 %copy-start = (bf16[8,8,2,128,128]{4,3,2,1,0:T(8,128)(2,1)S(1)}, bf16[8,8,2,128,128]{4,3,2,1,0:T(8,128)(2,1)}, u32[]{:S(2)}) copy-start(bf16[8,8,2,128,128]{4,3,2,1,0:T(8,128)(2,1)} %blocks.3) | copy-start | bytes 12582916
  31.4 53.4 %copy-start.3 = (f32[8,8,16,128]{3,2,1,0:T(8,128)S(1)}, f32[8,8,16,128]{3,2,1,0:T(8,128)}, u32[]{:S(2)}) copy-start(f32[8,8,16,128]{3,2,1,0:T(8,128)} %guess.1) | copy-start | bytes 1572868
  31.4 17.0 %collective-permute-start.9 = (bf16[1232,128]{1,0:T(8,128)(2,1)S(1)}, bf16[1232,128]{1,0:T(8,128)(2,1)S(1)}, u32[]{:S(2)}, u32[]{:S(2)}) collective-permute-start(bf16[1232,128]{1,0:T(8,128)(2,1)S(1)} %get-tuple-element.24.third0), channel_id=1, source_target_pairs={{0,3},{1,2},{2,1},{3,0},{4,7},{5,6},{6,5},{7,4},{8,11},{9,10},{10,... | collective-permute-start | bytes 946184 | tf_op jit(solution)/shard_map/ppermute | solution.py:27
  32.5 15.9 %collective-permute-start.8 = (bf16[1232,128]{1,0:T(8,128)(2,1)S(1)}, bf16[1232,128]{1,0:T(8,128)(2,1)S(1)}, u32[]{:S(2)}, u32[]{:S(2)}) collective-permute-start(bf16[1232,128]{1,0:T(8,128)(2,1)S(1)} %get-tuple-element.24.third0), channel_id=1, source_target_pairs={{0,2},{1,3},{2,0},{3,1},{4,6},{5,7},{6,4},{7,5},{8,10},{9,11},{10,... | collective-permute-start | bytes 946184 | tf_op jit(solution)/shard_map/ppermute | solution.py:27
  33.3 15.5 %collective-permute-start.7 = (bf16[1232,128]{1,0:T(8,128)(2,1)S(1)}, bf16[1232,128]{1,0:T(8,128)(2,1)S(1)}, u32[]{:S(2)}, u32[]{:S(2)}) collective-permute-start(bf16[1232,128]{1,0:T(8,128)(2,1)S(1)} %get-tuple-element.24.third0), channel_id=1, source_target_pairs={{0,1},{1,0},{2,3},{3,2},{4,5},{5,4},{6,7},{7,6},{8,9},{9,8},{10,11... | collective-permute-start | bytes 946184 | tf_op jit(solution)/shard_map/ppermute | solution.py:27
  50.8 2.2 %collective-permute-start.10 = (f32[256,128]{1,0:T(8,128)S(1)}, f32[256,128]{1,0:T(8,128)S(1)}, u32[]{:S(2)}, u32[]{:S(2)}) collective-permute-start(f32[256,128]{1,0:T(8,128)S(1)} %get-tuple-element.25), channel_id=1, source_target_pairs={{0,4},{4,0},{8,12},{12,8},{16,20},{20,16},{24,28},{28,24},{32,36},... | collective-permute-start | bytes 393224 | tf_op jit(solution)/shard_map/ppermute | solution.py:27
  52.1 6.2 %collective-permute-start.13 = (f32[2,4,64,128]{3,2,1,0:T(8,128)S(1)}, f32[2,4,64,128]{3,2,1,0:T(8,128)S(1)}, u32[]{:S(2)}, u32[]{:S(2)}) collective-permute-start(f32[2,4,64,128]{3,2,1,0:T(8,128)S(1)} %pad_maximum_fusion.1.fpair), channel_id=1, source_target_pairs={{0,252},{4,8},{8,4},{12,16},{16,12},{20,24},{24,20},{28,32},{32,28... | collective-permute-start | bytes 786440 | tf_op jit(solution)/shard_map/ppermute | solution.py:27
  53.0 8.2 %collective-permute-start.11 = (f32[2,256,128]{2,1,0:T(8,128)S(1)}, f32[2,256,128]{2,1,0:T(8,128)S(1)}, u32[]{:S(2)}, u32[]{:S(2)}) collective-permute-start(f32[2,256,128]{2,1,0:T(8,128)S(1)} %pad_maximum_fusion.pair), channel_id=1, source_target_pairs={{0,252},{4,8},{8,4},{12,16},{16,12},{20,24},{24,20},{28,32},{32,28... | collective-permute-start | bytes 786440 | tf_op jit(solution)/shard_map/ppermute | solution.py:27
  54.0 10.9 %collective-permute-start.19 = (f32[544,128]{1,0:T(8,128)S(1)}, f32[544,128]{1,0:T(8,128)S(1)}, u32[]{:S(2)}, u32[]{:S(2)}) collective-permute-start(f32[544,128]{1,0:T(8,128)S(1)} %get-tuple-element.30), channel_id=1, source_target_pairs={{0,1},{1,0},{2,3},{3,2},{4,5},{5,4},{6,7},{7,6},{8,9},{9,8},{10,11... | collective-permute-start | bytes 835592 | tf_op jit(solution)/shard_map/ppermute | solution.py:27
  54.1 10.9 %collective-permute-start.20 = (f32[544,128]{1,0:T(8,128)S(1)}, f32[544,128]{1,0:T(8,128)S(1)}, u32[]{:S(2)}, u32[]{:S(2)}) collective-permute-start(f32[544,128]{1,0:T(8,128)S(1)} %get-tuple-element.31), channel_id=1, source_target_pairs={{0,3},{1,2},{2,1},{3,0},{4,7},{5,6},{6,5},{7,4},{8,11},{9,10},{10,... | collective-permute-start | bytes 835592 | tf_op jit(solution)/shard_map/ppermute | solution.py:27
  58.2 7.4 %collective-permute-start.14 = (f32[2,4,64,128]{3,2,1,0:T(8,128)S(1)}, f32[2,4,64,128]{3,2,1,0:T(8,128)S(1)}, u32[]{:S(2)}, u32[]{:S(2)}) collective-permute-start(f32[2,4,64,128]{3,2,1,0:T(8,128)S(1)} %collective-permute-done.13.fa), channel_id=1, source_target_pairs={{0,4},{4,0},{8,12},{12,8},{16,20},{20,16},{24,28},{28,24},{32,36},... | collective-permute-start | bytes 786440 | tf_op jit(solution)/shard_map/ppermute | solution.py:27
  61.3 4.8 %collective-permute-start.12 = (f32[2,256,128]{2,1,0:T(8,128)S(1)}, f32[2,256,128]{2,1,0:T(8,128)S(1)}, u32[]{:S(2)}, u32[]{:S(2)}) collective-permute-start(f32[2,256,128]{2,1,0:T(8,128)S(1)} %collective-permute-done.11.a), channel_id=1, source_target_pairs={{0,4},{4,0},{8,12},{12,8},{16,20},{20,16},{24,28},{28,24},{32,36},... | collective-permute-start | bytes 786440 | tf_op jit(solution)/shard_map/ppermute | solution.py:27
  65.0 13.3 %collective-permute-start.21 = (f32[1224,128]{1,0:T(8,128)S(1)}, f32[1224,128]{1,0:T(8,128)S(1)}, u32[]{:S(2)}, u32[]{:S(2)}) collective-permute-start(f32[1224,128]{1,0:T(8,128)S(1)} %get-tuple-element.34), channel_id=1, source_target_pairs={{0,4},{4,0},{8,12},{12,8},{16,20},{20,16},{24,28},{28,24},{32,36},... | collective-permute-start | bytes 1880072 | tf_op jit(solution)/shard_map/ppermute | solution.py:27
  65.6 12.7 %collective-permute-start.22 = (f32[1224,128]{1,0:T(8,128)S(1)}, f32[1224,128]{1,0:T(8,128)S(1)}, u32[]{:S(2)}, u32[]{:S(2)}) collective-permute-start(f32[1224,128]{1,0:T(8,128)S(1)} %get-tuple-element.35), channel_id=1, source_target_pairs={{0,252},{4,8},{8,4},{12,16},{16,12},{20,24},{24,20},{28,32},{32,28... | collective-permute-start | bytes 1880072 | tf_op jit(solution)/shard_map/ppermute | solution.py:27
  68.7 5.4 %collective-permute-start.16 = (f32[256,128]{1,0:T(8,128)S(1)}, f32[256,128]{1,0:T(8,128)S(1)}, u32[]{:S(2)}, u32[]{:S(2)}) collective-permute-start(f32[256,128]{1,0:T(8,128)S(1)} %bitcast.17), channel_id=1, source_target_pairs={{0,3},{1,2},{2,1},{3,0},{4,7},{5,6},{6,5},{7,4},{8,11},{9,10},{10,... | collective-permute-start | bytes 393224 | tf_op jit(solution)/shard_map/ppermute | solution.py:27
  70.4 4.1 %collective-permute-start.15 = (f32[256,128]{1,0:T(8,128)S(1)}, f32[256,128]{1,0:T(8,128)S(1)}, u32[]{:S(2)}, u32[]{:S(2)}) collective-permute-start(f32[256,128]{1,0:T(8,128)S(1)} %bitcast.18), channel_id=1, source_target_pairs={{0,1},{1,0},{2,3},{3,2},{4,5},{5,4},{6,7},{7,6},{8,9},{9,8},{10,11... | collective-permute-start | bytes 393224 | tf_op jit(solution)/shard_map/ppermute | solution.py:27
  74.5 5.0 %collective-permute-start.17 = (f32[576,128]{1,0:T(8,128)S(1)}, f32[576,128]{1,0:T(8,128)S(1)}, u32[]{:S(2)}, u32[]{:S(2)}) collective-permute-start(f32[576,128]{1,0:T(8,128)S(1)} %get-tuple-element.27), channel_id=1, source_target_pairs={{0,4},{4,0},{8,12},{12,8},{16,20},{20,16},{24,28},{28,24},{32,36},... | collective-permute-start | bytes 884744 | tf_op jit(solution)/shard_map/ppermute | solution.py:27
  78.3 6.4 %collective-permute-start.18 = (f32[576,128]{1,0:T(8,128)S(1)}, f32[576,128]{1,0:T(8,128)S(1)}, u32[]{:S(2)}, u32[]{:S(2)}) collective-permute-start(f32[576,128]{1,0:T(8,128)S(1)} %get-tuple-element.28), channel_id=1, source_target_pairs={{0,252},{4,8},{8,4},{12,16},{16,12},{20,24},{24,20},{28,32},{32,28... | collective-permute-start | bytes 884744 | tf_op jit(solution)/shard_map/ppermute | solution.py:27
  84.8 21.1 %copy-start.1 = (f32[8,8,16,128]{3,2,1,0:T(8,128)S(1)}, f32[8,8,16,128]{3,2,1,0:T(8,128)}, u32[]{:S(2)}) copy-start(f32[8,8,16,128]{3,2,1,0:T(8,128)} %fown.1) | copy-start | bytes 1572868
  84.8 21.1 %copy-start.4 = (f32[8,8,128]{2,1,0:T(8,128)S(1)}, f32[8,8,128]{2,1,0:T(8,128)}, u32[]{:S(2)}) copy-start(f32[8,8,128]{2,1,0:T(8,128)} %sown.1) | copy-start | bytes 98308
  89.9 4.6 %collective-permute-start.23 = (f32[384,128]{1,0:T(8,128)S(1)}, f32[384,128]{1,0:T(8,128)S(1)}, u32[]{:S(2)}, u32[]{:S(2)}) collective-permute-start(f32[384,128]{1,0:T(8,128)S(1)} %get-tuple-element.37), channel_id=1, source_target_pairs={{0,1},{1,0},{2,3},{3,2},{4,5},{5,4},{6,7},{7,6},{8,9},{9,8},{10,11... | collective-permute-start | bytes 589832 | tf_op jit(solution)/shard_map/ppermute | solution.py:27
  90.0 5.8 %collective-permute-start.24 = (f32[384,128]{1,0:T(8,128)S(1)}, f32[384,128]{1,0:T(8,128)S(1)}, u32[]{:S(2)}, u32[]{:S(2)}) collective-permute-start(f32[384,128]{1,0:T(8,128)S(1)} %get-tuple-element.38), channel_id=1, source_target_pairs={{0,3},{1,2},{2,1},{3,0},{4,7},{5,6},{6,5},{7,4},{8,11},{9,10},{10,... | collective-permute-start | bytes 589832 | tf_op jit(solution)/shard_map/ppermute | solution.py:27
  95.8 6.2 %collective-permute-start.25 = (f32[480,128]{1,0:T(8,128)S(1)}, f32[480,128]{1,0:T(8,128)S(1)}, u32[]{:S(2)}, u32[]{:S(2)}) collective-permute-start(f32[480,128]{1,0:T(8,128)S(1)} %get-tuple-element.39), channel_id=1, source_target_pairs={{0,4},{4,0},{8,12},{12,8},{16,20},{20,16},{24,28},{28,24},{32,36},... | collective-permute-start | bytes 737288 | tf_op jit(solution)/shard_map/ppermute | solution.py:27
  100.2 5.6 %collective-permute-start.26 = (f32[480,128]{1,0:T(8,128)S(1)}, f32[480,128]{1,0:T(8,128)S(1)}, u32[]{:S(2)}, u32[]{:S(2)}) collective-permute-start(f32[480,128]{1,0:T(8,128)S(1)} %get-tuple-element.40), channel_id=1, source_target_pairs={{0,252},{4,8},{8,4},{12,16},{16,12},{20,24},{24,20},{28,32},{32,28... | collective-permute-start | bytes 737288 | tf_op jit(solution)/shard_map/ppermute | solution.py:27

commit v5 on v4

--- a/solution.py
+++ b/solution.py
@@ -165,7 +165,7 @@
 
 def ahead_kernel(
     source_first_h, shift_first_h, source_second_h, shift_second_h, blocks_third, guess_third_h, links_third,
-    third, own, even, odd, row_on, row_off,
+    third, own, even, odd, row_low, row_high,
     source_first, shift_first, source_second, shift_second, guess_third, links, sems,
 ):
     pairs = [
@@ -191,7 +191,7 @@
         rows = jnp.where(names == c, links[c // 4, c // 2 % 2, c % 2], rows)
     third[1216:1232, :] = rows.astype(F32).astype(BF16)
 
-    side, core = lax.rem(lax.axis_index("gy"), 2), lax.rem(lax.axis_index("gz"), 2)
+    side = lax.rem(lax.axis_index("gy"), 2)
     for i in range(4):
         for j in range(4):
             at = (i * 4 + j) * R
@@ -204,7 +204,7 @@
                 at = 272 + (i * 2 + j) * R
                 ref[at : at + R, :] = source_first[i, first + j]
             ref[528 + i * 2 : 530 + i * 2, :] = jnp.where(first == 0, shift_first[i, 0:2, :], shift_first[i, 6:8, :])
-    for ref, first in ((row_on, 6 - 6 * core), (row_off, 6 * core)):
+    for ref, first in ((row_low, 0), (row_high, 6)):
         for i in range(2):
             for j in range(8):
                 at = (i * 8 + j) * R
@@ -214,30 +214,42 @@
         copy.wait()
 
 
+def pair_kernel(line, line_on, pair, short):
+    for slot, ref in enumerate((line, line_on)):
+        pair[slot] = ref[...]
+        short[slot] = ref[:, 0:40, :]
+
+
 def relay_kernel(near, far, out):
-    out[0] = near[...]
-    out[1] = far[...]
+    out[:, :, 0:104, :] = near[...]
+    out[:, :, 104:144, :] = far[...]
+
+
+def pick_kernel(low, high, on, off):
+    core = lax.rem(lax.axis_index("gz"), 2)
+    on[...] = jnp.where(core == 0, high[...], low[...])
+    off[...] = jnp.where(core == 0, low[...], high[...])
 
 
 def fourth_kernel(pair, a, a3, both, third0, third1, third2, third3, out, start, u, f, s, res, d0, d1, lines):
     gz, gy = lax.axis_index("gz"), lax.axis_index("gy")
     core = lax.rem(gz, 2)
 
-    def place(ref, chip, first_bit):
+    def place(ref, chip, first_bit, at=0):
         for slot in range(2):
             bit = first_bit if slot == 0 else 1 - first_bit
             row = chip * 2 + bit
             for k in range(4):
                 col = lax.bitwise_xor(gy, k)
-                f[row, col] = ref[slot, k, 0:16, :]
-                u[row, col] = ref[slot, k, 16:32, :]
-                s[row, col] = ref[slot, k, 32:33, :]
+                f[row, col] = ref[slot, k, at : at + 16, :]
+                u[row, col] = ref[slot, k, at + 16 : at + 32, :]
+                s[row, col] = ref[slot, k, at + 32 : at + 33, :]
 
     place(pair, 2, core)
     place(a, 1 + 2 * core, 1 - core)
-    place(both.at[0], 3 - 2 * core, core)
+    place(both, 3 - 2 * core, core)
     place(a3, 4 * core, 1 - core)
-    place(both.at[1], 4 - 4 * core, core)
+    place(both, 4 - 4 * core, core, 104)
 
     def emit(i, j, value):
         lines[i - 3 - core, j] = value.astype(BF16).astype(F32)
@@ -267,12 +279,12 @@
             start[pl.ds(pl.multiple_of((i * 8 + col + j) * R, R), R), :] = total
 
 
-def third_kernel(pair, a, b, fpair, fa, fb, spair, sa, sb, links_h, blocks, guess_h, out, start, u, f, s, res, d0, d1, lines, guess, links, sems):
+def third_kernel(pair, a, b, fpair, fa, fb, links_h, blocks, guess_h, out, start, u, f, s, res, d0, d1, lines, guess, links, sems):
     copies = fetch(sems, (guess_h, guess), (links_h, links))
     gz, gy = lax.axis_index("gz"), lax.axis_index("gy")
     core = lax.rem(gz, 2)
 
-    def place(ref, fref, sref, chip, first_bit):
+    def place(ref, fref, chip, first_bit):
         for slot in range(2):
             bit = first_bit if slot == 0 else 1 - first_bit
             for k in range(4):
@@ -281,16 +293,16 @@
                     row = chip * 4 + bit * 2 + i
                     for j in range(2):
                         at = (i * 2 + j) * R
-                        f[row, col + j] = fref[slot, k, at : at + R, :]
-                        s[row, col + j] = sref[slot, k, 33 + i * 2 + j : 34 + i * 2 + j, :]
+                        f[row, col + j] = fref[slot, k, 40 + at : 40 + at + R, :]
+                        s[row, col + j] = fref[slot, k, 33 + i * 2 + j : 34 + i * 2 + j, :]
             for i in range(2):
                 for j in range(8):
                     at = (i * 8 + j) * R
                     u[chip * 4 + bit * 2 + i, j] = ref[slot, at : at + R, :]
 
-    place(pair, fpair, spair, 1, core)
-    place(a, fa, sa, 2 * core, 1 - core)
-    place(b, fb, sb.at[0], 2 - 2 * core, core)
+    place(pair, fpair, 1, core)
+    place(a, fa, 2 * core, 1 - core)
+    place(b, fb, 2 - 2 * core, core)
 
     def emit(i, j, value):
         lines[i - 3 - 2 * core, j] = value.astype(BF16)
@@ -530,16 +542,13 @@
     y3 = y_by(pack, 3)
     line = jnp.stack([pack, y1, y2, y3])
     line_on = z_on(line)
-    pair = jnp.stack([line[:, :40], line_on[:, :40]])
-    pair_f = jnp.stack([line[:, 40:], line_on[:, 40:]])
+    pair, short = call(pair_kernel, (line, line_on), (sds(2, 4, 104, L), sds(2, 4, 40, L)), [], 1000, 2)
     near = z_off(pair)
-    far = z_off3(pair)
-    (both,) = call(relay_kernel, (near, far), (sds(2, 2, 4, 40, L),), [], 1000, 2)
+    far = z_off3(short)
+    (both,) = call(relay_kernel, (near, far), (sds(2, 4, 144, L),), [], 1000, 3)
     both = z_on(both)
-    near_f = z_off(pair_f)
-    near_fb = z_on(near_f)
-
-    third, mine, ahead_even, ahead_odd, row_on, row_off = call(
+
+    third, mine, ahead_even, ahead_odd, row_low, row_high = call(
         ahead_kernel,
         (source_first, shift_first, source_second, shift_second, blocks_third, guess_third, links_third),
         (sds(THIRD, L, dtype=BF16), sds(272, L), sds(ALONG_Y, L), sds(ALONG_Y, L), sds(272, L), sds(272, L)),
@@ -547,6 +556,7 @@
         + [pltpu.SMEM(links_third.shape, jnp.int32), pltpu.SemaphoreType.DMA((16,))],
         1000, 6, range(7),
     )
+    row_on, row_off = call(pick_kernel, (row_low, row_high), (sds(272, L), sds(272, L)), [], 1000, 2)
     third1 = y_by(third, 1)
     third2 = y_by(third, 2)
     third3 = y_by(third, 3)
@@ -578,10 +588,10 @@
     near3_b = z_on(near3)
     out_third, start_second = call(
         third_kernel,
-        (pair3, near3, near3_b, pair_f, near_f, near_fb, pair, near, both, links_second, blocks_second, guess_second),
+        (pair3, near3, near3_b, pair, near, both, links_second, blocks_second, guess_second),
         (onchip(2, 2, R, L), sds(4, 4, R, L)),
         smoothing_scratch(12, 8) + [cells(4, 8, BF16)] + smem_last(guess_second, links_second),
-        8_000_000, 12, (9, 11),
+        8_000_000, 12, (6, 8),
     )
 
     own = flat(start_second)

time: 112 us -> 113 us (level)
  waiting for transfers between devices: 46.4 us -> 52.3 us
  starting transfers between devices: 44.2 us -> 40.2 us
    ppermute x27 -> x25, waiting for transfers between devices: 46.4 us -> 52.3 us  [swap(): lax.ppermute(x, axis, [(i, partner(i)) for i in range(lax.axis_size(axis))])]
    ppermute x27 -> x25, starting transfers between devices: 44.2 us -> 40.2 us  [swap(): lax.ppermute(x, axis, [(i, partner(i)) for i in range(lax.axis_size(axis))])]
    pallas_call x10 -> x12, Pallas kernels: 16.7 us -> 16.7 us  [call(): pl.pallas_call(kernel, out_shape=outs, in_specs=specs, out_specs=tuple((o...]
  transfers between devices with their start and end apart: 27 -> 25, of which waited for: 16 -> 15; matrix products, arithmetic and copies ran while one was open for 2% -> 2% of each run, Pallas kernels for 4% -> 4%
where the time goes in v5:
time: 113 us; the launch traced here: 112 us
  waiting for transfers between devices  52.3 us (46%)
  starting transfers between devices  40.2 us (36%)
  Pallas kernels  16.7 us (15%)
  local copies, waits for them, and re-layouts  1.89 us (2%)
    ppermute x25, waiting for transfers between devices, swap(): lax.ppermute(x, axis, [(i, partner(i)) for i in range(lax.axis_size(axis))])  52.3 us
    ppermute x25, starting transfers between devices, swap(): lax.ppermute(x, axis, [(i, partner(i)) for i in range(lax.axis_size(axis))])  40.2 us
    pallas_call x12, Pallas kernels, call(): pl.pallas_call(kernel, out_shape=outs, in_specs=specs, out_specs=tuple((o...  16.7 us
  transfers between devices with their start and end apart: 25, of which 15 were waited for; matrix products, arithmetic and copies ran while one was open for 2% of the time, Pallas kernels for 4%

profile of v5, /device:TPU:1, one launch (start us, length us, event | category | flops | bytes accessed | tf_op | source)
XLA Modules:
  0.0 112.1 jit_solution(593397006881356546)
XLA Ops:
  0.6 1.0 shard_map.201
  1.6 3.6 %collective-permute-start.2 = (f32[104,128]{1,0:T(8,128)S(1)}, f32[104,128]{1,0:T(8,128)S(1)}, u32[]{:S(2)}, u32[]{:S(2)}) collective-permute-start(f32[104,128]{1,0:T(8,128)S(1)} %shard_map.201), channel_id=1, source_target_pairs={{0,3},{1,2},{2,1},{3,0},{4,7},{5,6},{6,5},{7,4},{8,11},{9,10},{10,... | collective-permute-start | bytes 159752 | tf_op jit(solution)/shard_map/ppermute | solution.py:27
  5.3 0.3 collective-permute-start.1
  5.6 0.3 collective-permute-start
  5.9 0.8 collective-permute-done.2
  6.8 3.1 %collective-permute-done.1 = f32[104,128]{1,0:T(8,128)S(1)} collective-permute-done((f32[104,128]{1,0:T(8,128)S(1)}, f32[104,128]{1,0:T(8,128)S(1)}, u32[]{:S(2)}, u32[]{:S(2)}) %collective-permute-start.1) | collective-permute-done | bytes 53280 | tf_op jit(solution)/shard_map/ppermute | solution.py:27
  9.9 2.1 %collective-permute-start.3 = (f32[4,104,128]{2,1,0:T(8,128)S(1)}, f32[4,104,128]{2,1,0:T(8,128)S(1)}, u32[]{:S(2)}, u32[]{:S(2)}) collective-permute-start(f32[4,104,128]{2,1,0:T(8,128)S(1)} %pad_maximum_fusion.1.line), channel_id=1, source_target_pairs={{0,4},{4,0},{8,12},{12,8},{16,20},{20,16},{24,28},{28,24},{32,36},... | collective-permute-start | bytes 638984 | tf_op jit(solution)/shard_map/ppermute | solution.py:27
  12.0 1.1 collective-permute-done.3.line_on
  13.1 2.0 %collective-permute-start.4 = (f32[2,4,104,128]{3,2,1,0:T(8,128)S(1)}, f32[2,4,104,128]{3,2,1,0:T(8,128)S(1)}, u32[]{:S(2)}, u32[]{:S(2)}) collective-permute-start(f32[2,4,104,128]{3,2,1,0:T(8,128)S(1)} %get-tuple-element.28.pair.fpair), channel_id=1, source_target_pairs={{0,252},{4,8},{8,4},{12,16},{16,12},{20,24},{24,20},{28,32},{32,28... | collective-permute-start | bytes 1277960 | tf_op jit(solution)/shard_map/ppermute | solution.py:27
  15.1 1.5 %collective-permute-start.5 = (f32[2,4,40,128]{3,2,1,0:T(8,128)S(1)}, f32[2,4,40,128]{3,2,1,0:T(8,128)S(1)}, u32[]{:S(2)}, u32[]{:S(2)}) collective-permute-start(f32[2,4,40,128]{3,2,1,0:T(8,128)S(1)} %get-tuple-element.29), channel_id=1, source_target_pairs={{0,244},{4,16},{8,252},{12,24},{16,4},{20,32},{24,12},{28,40},{32,... | collective-permute-start | bytes 491528 | tf_op jit(solution)/shard_map/ppermute | solution.py:27
  16.5 9.5 %collective-permute-done.5.far.a3 = f32[2,4,40,128]{3,2,1,0:T(8,128)S(1)} collective-permute-done((f32[2,4,40,128]{3,2,1,0:T(8,128)S(1)}, f32[2,4,40,128]{3,2,1,0:T(8,128)S(1)}, u32[]{:S(2)}, u32[]{:S(2)}) %collective-permute-start.5) | collective-permute-done | bytes 163872 | tf_op jit(solution)/shard_map/ppermute | solution.py:27
  26.1 4.9 %collective-permute-start.6 = (f32[2,4,144,128]{3,2,1,0:T(8,128)S(1)}, f32[2,4,144,128]{3,2,1,0:T(8,128)S(1)}, u32[]{:S(2)}, u32[]{:S(2)}) collective-permute-start(f32[2,4,144,128]{3,2,1,0:T(8,128)S(1)} %shard_map.203), channel_id=1, source_target_pairs={{0,4},{4,0},{8,12},{12,8},{16,20},{20,16},{24,28},{28,24},{32,36},... | collective-permute-start | bytes 1769480 | tf_op jit(solution)/shard_map/ppermute | solution.py:27
  31.0 1.4 %shard_map.204 = (bf16[1232,128]{1,0:T(8,128)(2,1)S(1)}, f32[272,128]{1,0:T(8,128)S(1)}, f32[544,128]{1,0:T(8,128)S(1)}, f32[544,128]{1,0:T(8,128)S(1)}, f32[272,128]{1,0:T(8,128)S(1)}, /*index=5*/f32[272,128]{1,0:T(8,128)S(1)}) custom-call(f32[8,8,16,128]{3,2,1,0:T(8,128)} %fown.1, f32[8,8,128]{2,1,0:T(8,128)} %sown.1, f32[4,4,16,128]{3,2,1,0:T(8,128)} %source_second_h.1, ...), custom_call_target="tpu_custom_call" | custom-call | flops 1000 | bytes 991264 | tf_op jit(solution)/shard_map/pallas_call | solution.py:127
  32.4 0.0 copy-start
  32.4 0.0 copy-start.3
  32.5 1.1 collective-permute-start.9
  33.6 0.8 collective-permute-start.8
  34.4 1.4 %collective-permute-start.7 = (bf16[1232,128]{1,0:T(8,128)(2,1)S(1)}, bf16[1232,128]{1,0:T(8,128)(2,1)S(1)}, u32[]{:S(2)}, u32[]{:S(2)}) collective-permute-start(bf16[1232,128]{1,0:T(8,128)(2,1)S(1)} %get-tuple-element.30.third0), channel_id=1, source_target_pairs={{0,1},{1,0},{2,3},{3,2},{4,5},{5,4},{6,7},{7,6},{8,9},{9,8},{10,11... | collective-permute-start | bytes 946184 | tf_op jit(solution)/shard_map/ppermute | solution.py:27
  35.8 13.7 %collective-permute-done.9.third3 = bf16[1232,128]{1,0:T(8,128)(2,1)S(1)} collective-permute-done((bf16[1232,128]{1,0:T(8,128)(2,1)S(1)}, bf16[1232,128]{1,0:T(8,128)(2,1)S(1)}, u32[]{:S(2)}, u32[]{:S(2)}) %collective-permute-start.9) | collective-permute-done | bytes 315424 | tf_op jit(solution)/shard_map/ppermute | solution.py:27
  49.5 0.3 collective-permute-done.7.third1
  49.8 2.1 %shard_map.205 = (f32[1,1,16,128]{3,2,1,0:T(8,128)S(1)}, f32[256,128]{1,0:T(8,128)S(1)}) custom-call(f32[2,4,104,128]{3,2,1,0:T(8,128)S(1)} %get-tuple-element.28.pair.fpair, f32[2,4,104,128]{3,2,1,0:T(8,128)S(1)} %collective-permute-done.4.near.a.fa, f32[2,4,40,128]{3,2,1,0:T(8,128)S(1)} %collective-permute-done.5.far.a3, ...), custom_call_target="tpu_custom_call" | custom-call | flops 4000000 | bytes 2867200 | tf_op jit(solution)/shard_map/pallas_call | solution.py:127
  51.9 1.2 %collective-permute-start.10 = (f32[256,128]{1,0:T(8,128)S(1)}, f32[256,128]{1,0:T(8,128)S(1)}, u32[]{:S(2)}, u32[]{:S(2)}) collective-permute-start(f32[256,128]{1,0:T(8,128)S(1)} %get-tuple-element.31), channel_id=1, source_target_pairs={{0,4},{4,0},{8,12},{12,8},{16,20},{20,16},{24,28},{28,24},{32,36},... | collective-permute-start | bytes 393224 | tf_op jit(solution)/shard_map/ppermute | solution.py:27
  53.1 1.0 collective-permute-done.10
  54.1 0.1 collective-permute-start.11
  54.2 0.1 collective-permute-start.17
  54.3 2.0 %collective-permute-start.18 = (f32[544,128]{1,0:T(8,128)S(1)}, f32[544,128]{1,0:T(8,128)S(1)}, u32[]{:S(2)}, u32[]{:S(2)}) collective-permute-start(f32[544,128]{1,0:T(8,128)S(1)} %get-tuple-element.37), channel_id=1, source_target_pairs={{0,3},{1,2},{2,1},{3,0},{4,7},{5,6},{6,5},{7,4},{8,11},{9,10},{10,... | collective-permute-start | bytes 835592 | tf_op jit(solution)/shard_map/ppermute | solution.py:27
  56.3 3.7 %collective-permute-done.11.a = f32[2,256,128]{2,1,0:T(8,128)S(1)} collective-permute-done((f32[2,256,128]{2,1,0:T(8,128)S(1)}, f32[2,256,128]{2,1,0:T(8,128)S(1)}, u32[]{:S(2)}, u32[]{:S(2)}) %collective-permute-start.11) | collective-permute-done | bytes 262176 | tf_op jit(solution)/shard_map/ppermute | solution.py:27
  60.0 3.7 %collective-permute-start.12 = (f32[2,256,128]{2,1,0:T(8,128)S(1)}, f32[2,256,128]{2,1,0:T(8,128)S(1)}, u32[]{:S(2)}, u32[]{:S(2)}) collective-permute-start(f32[2,256,128]{2,1,0:T(8,128)S(1)} %collective-permute-done.11.a), channel_id=1, source_target_pairs={{0,4},{4,0},{8,12},{12,8},{16,20},{20,16},{24,28},{28,24},{32,36},... | collective-permute-start | bytes 786440 | tf_op jit(solution)/shard_map/ppermute | solution.py:27
  63.7 0.1 shard_map.209
  63.8 1.7 %collective-permute-start.19 = (f32[1224,128]{1,0:T(8,128)S(1)}, f32[1224,128]{1,0:T(8,128)S(1)}, u32[]{:S(2)}, u32[]{:S(2)}) collective-permute-start(f32[1224,128]{1,0:T(8,128)S(1)} %get-tuple-element.42), channel_id=1, source_target_pairs={{0,4},{4,0},{8,12},{12,8},{16,20},{20,16},{24,28},{28,24},{32,36},... | collective-permute-start | bytes 1880072 | tf_op jit(solution)/shard_map/ppermute | solution.py:27
  65.6 2.5 %shard_map.206 = (f32[2,2,16,128]{3,2,1,0:T(8,128)S(1)}, f32[4,4,16,128]{3,2,1,0:T(8,128)S(1)}) custom-call(f32[2,256,128]{2,1,0:T(8,128)S(1)} %pad_maximum_fusion.pair, f32[2,256,128]{2,1,0:T(8,128)S(1)} %collective-permute-done.11.a, f32[2,256,128]{2,1,0:T(8,128)S(1)} %collective-permute-done.12.b, f32[2,4,104,128]{3,2,1,0:T(8,128)S(1)} %get-tuple-element.28.pair.fpair, ...), custom_call_target="tpu_custom_call" | custom-call | flops 8000000 | bytes 3408000 | tf_op jit(solution)/shard_map/pallas_call | solution.py:127
  68.1 2.1 %collective-permute-start.14 = (f32[256,128]{1,0:T(8,128)S(1)}, f32[256,128]{1,0:T(8,128)S(1)}, u32[]{:S(2)}, u32[]{:S(2)}) collective-permute-start(f32[256,128]{1,0:T(8,128)S(1)} %bitcast.9), channel_id=1, source_target_pairs={{0,3},{1,2},{2,1},{3,0},{4,7},{5,6},{6,5},{7,4},{8,11},{9,10},{10,... | collective-permute-start | bytes 393224 | tf_op jit(solution)/shard_map/ppermute | solution.py:27
  70.1 3.3 %collective-permute-done.14.odd.own_odd = f32[256,128]{1,0:T(8,128)S(1)} collective-permute-done((f32[256,128]{1,0:T(8,128)S(1)}, f32[256,128]{1,0:T(8,128)S(1)}, u32[]{:S(2)}, u32[]{:S(2)}) %collective-permute-start.14) | collective-permute-done | bytes 131104 | tf_op jit(solution)/shard_map/ppermute | solution.py:27
  73.5 0.8 collective-permute-done.13.even.own_even
  74.3 5.8 %collective-permute-start.15 = (f32[576,128]{1,0:T(8,128)S(1)}, f32[576,128]{1,0:T(8,128)S(1)}, u32[]{:S(2)}, u32[]{:S(2)}) collective-permute-start(f32[576,128]{1,0:T(8,128)S(1)} %get-tuple-element.33), channel_id=1, source_target_pairs={{0,4},{4,0},{8,12},{12,8},{16,20},{20,16},{24,28},{28,24},{32,36},... | collective-permute-start | bytes 884744 | tf_op jit(solution)/shard_map/ppermute | solution.py:27
  80.1 1.2 %collective-permute-done.15.on = f32[576,128]{1,0:T(8,128)S(1)} collective-permute-done((f32[576,128]{1,0:T(8,128)S(1)}, f32[576,128]{1,0:T(8,128)S(1)}, u32[]{:S(2)}, u32[]{:S(2)}) %collective-permute-start.15) | collective-permute-done | bytes 294944 | tf_op jit(solution)/shard_map/ppermute | solution.py:27
  81.3 5.2 %collective-permute-done.16.off = f32[576,128]{1,0:T(8,128)S(1)} collective-permute-done((f32[576,128]{1,0:T(8,128)S(1)}, f32[576,128]{1,0:T(8,128)S(1)}, u32[]{:S(2)}, u32[]{:S(2)}) %collective-permute-start.16) | collective-permute-done | bytes 294944 | tf_op jit(solution)/shard_map/ppermute | solution.py:27
  86.5 5.1 %shard_map.210 = (f32[4,4,16,128]{3,2,1,0:T(8,128)S(1)}, f32[8,8,16,128]{3,2,1,0:T(8,128)S(1)}, f32[384,128]{1,0:T(8,128)S(1)}, f32[384,128]{1,0:T(8,128)S(1)}) custom-call(f32[256,128]{1,0:T(8,128)S(1)} %bitcast.12, f32[256,128]{1,0:T(8,128)S(1)} %collective-permute-done.13.even.own_even, f32[256,128]{1,0:T(8,128)S(1)} %collective-permute-done.14.odd.own_odd, ...), custom_call_target="tpu_custom_call" | custom-call | flops 16000000 | bytes 7651840 | tf_op jit(solution)/shard_map/pallas_call | solution.py:127
  91.6 0.1 collective-permute-start.21
  91.7 1.0 collective-permute-start.22
  92.7 3.5 %collective-permute-done.21.even = f32[384,128]{1,0:T(8,128)S(1)} collective-permute-done((f32[384,128]{1,0:T(8,128)S(1)}, f32[384,128]{1,0:T(8,128)S(1)}, u32[]{:S(2)}, u32[]{:S(2)}) %collective-permute-start.21) | collective-permute-done | bytes 196640 | tf_op jit(solution)/shard_map/ppermute | solution.py:27
  96.2 1.3 %collective-permute-done.22.odd = f32[384,128]{1,0:T(8,128)S(1)} collective-permute-done((f32[384,128]{1,0:T(8,128)S(1)}, f32[384,128]{1,0:T(8,128)S(1)}, u32[]{:S(2)}, u32[]{:S(2)}) %collective-permute-start.22) | collective-permute-done | bytes 196640 | tf_op jit(solution)/shard_map/ppermute | solution.py:27
  97.6 4.4 %collective-permute-start.23 = (f32[480,128]{1,0:T(8,128)S(1)}, f32[480,128]{1,0:T(8,128)S(1)}, u32[]{:S(2)}, u32[]{:S(2)}) collective-permute-start(f32[480,128]{1,0:T(8,128)S(1)} %get-tuple-element.47), channel_id=1, source_target_pairs={{0,4},{4,0},{8,12},{12,8},{16,20},{20,16},{24,28},{28,24},{32,36},... | collective-permute-start | bytes 737288 | tf_op jit(solution)/shard_map/ppermute | solution.py:27
  101.9 0.6 copy.24
  102.5 0.6 copy.23
  103.2 0.7 copy.22
  103.8 3.7 %collective-permute-done.24.off = f32[480,128]{1,0:T(8,128)S(1)} collective-permute-done((f32[480,128]{1,0:T(8,128)S(1)}, f32[480,128]{1,0:T(8,128)S(1)}, u32[]{:S(2)}, u32[]{:S(2)}) %collective-permute-start.24) | collective-permute-done | bytes 245792 | tf_op jit(solution)/shard_map/ppermute | solution.py:27
  107.6 4.4 %shard_map.212 = f32[8,8,16,128]{3,2,1,0:T(8,128)} custom-call(f32[8,8,16,128]{3,2,1,0:T(8,128)S(1)} %get-tuple-element.44.start.own, f32[384,128]{1,0:T(8,128)S(1)} %collective-permute-done.21.even, f32[384,128]{1,0:T(8,128)S(1)} %collective-permute-done.22.odd, f32[480,128]{1,0:T(8,128)S(1)} %collective-permute-done.23.on, ...), custom_call_target="tpu_custom_call" | custom-call | flops 16000000 | bytes 3776512 | tf_op jit(solution)/shard_map/pallas_call | solution.py:127
  (29 shorter events, 0.3 us)
Async XLA Ops:
  0.6 64.9 %copy-start.2 = (bf16[4,4,2,128,128]{4,3,2,1,0:T(8,128)(2,1)S(1)}, bf16[4,4,2,128,128]{4,3,2,1,0:T(8,128)(2,1)}, u32[]{:S(2)}) copy-start(bf16[4,4,2,128,128]{4,3,2,1,0:T(8,128)(2,1)} %blocks.2) | copy-start | bytes 3145732
  1.6 5.2 %collective-permute-start.2 = (f32[104,128]{1,0:T(8,128)S(1)}, f32[104,128]{1,0:T(8,128)S(1)}, u32[]{:S(2)}, u32[]{:S(2)}) collective-permute-start(f32[104,128]{1,0:T(8,128)S(1)} %shard_map.201), channel_id=1, source_target_pairs={{0,3},{1,2},{2,1},{3,0},{4,7},{5,6},{6,5},{7,4},{8,11},{9,10},{10,... | collective-permute-start | bytes 159752 | tf_op jit(solution)/shard_map/ppermute | solution.py:27
  5.3 4.6 %collective-permute-start.1 = (f32[104,128]{1,0:T(8,128)S(1)}, f32[104,128]{1,0:T(8,128)S(1)}, u32[]{:S(2)}, u32[]{:S(2)}) collective-permute-start(f32[104,128]{1,0:T(8,128)S(1)} %shard_map.201), channel_id=1, source_target_pairs={{0,2},{1,3},{2,0},{3,1},{4,6},{5,7},{6,4},{7,5},{8,10},{9,11},{10,... | collective-permute-start | bytes 159752 | tf_op jit(solution)/shard_map/ppermute | solution.py:27
  5.6 4.2 %collective-permute-start = (f32[104,128]{1,0:T(8,128)S(1)}, f32[104,128]{1,0:T(8,128)S(1)}, u32[]{:S(2)}, u32[]{:S(2)}) collective-permute-start(f32[104,128]{1,0:T(8,128)S(1)} %shard_map.201), channel_id=1, source_target_pairs={{0,1},{1,0},{2,3},{3,2},{4,5},{5,4},{6,7},{7,6},{8,9},{9,8},{10,11... | collective-permute-start | bytes 159752 | tf_op jit(solution)/shard_map/ppermute | solution.py:27
  9.9 3.2 %collective-permute-start.3 = (f32[4,104,128]{2,1,0:T(8,128)S(1)}, f32[4,104,128]{2,1,0:T(8,128)S(1)}, u32[]{:S(2)}, u32[]{:S(2)}) collective-permute-start(f32[4,104,128]{2,1,0:T(8,128)S(1)} %pad_maximum_fusion.1.line), channel_id=1, source_target_pairs={{0,4},{4,0},{8,12},{12,8},{16,20},{20,16},{24,28},{28,24},{32,36},... | collective-permute-start | bytes 638984 | tf_op jit(solution)/shard_map/ppermute | solution.py:27
  13.1 13.0 %collective-permute-start.4 = (f32[2,4,104,128]{3,2,1,0:T(8,128)S(1)}, f32[2,4,104,128]{3,2,1,0:T(8,128)S(1)}, u32[]{:S(2)}, u32[]{:S(2)}) collective-permute-start(f32[2,4,104,128]{3,2,1,0:T(8,128)S(1)} %get-tuple-element.28.pair.fpair), channel_id=1, source_target_pairs={{0,252},{4,8},{8,4},{12,16},{16,12},{20,24},{24,20},{28,32},{32,28... | collective-permute-start | bytes 1277960 | tf_op jit(solution)/shard_map/ppermute | solution.py:27
  15.1 11.0 %collective-permute-start.5 = (f32[2,4,40,128]{3,2,1,0:T(8,128)S(1)}, f32[2,4,40,128]{3,2,1,0:T(8,128)S(1)}, u32[]{:S(2)}, u32[]{:S(2)}) collective-permute-start(f32[2,4,40,128]{3,2,1,0:T(8,128)S(1)} %get-tuple-element.29), channel_id=1, source_target_pairs={{0,244},{4,16},{8,252},{12,24},{16,4},{20,32},{24,12},{28,40},{32,... | collective-permute-start | bytes 491528 | tf_op jit(solution)/shard_map/ppermute | solution.py:27
  26.1 23.7 %collective-permute-start.6 = (f32[2,4,144,128]{3,2,1,0:T(8,128)S(1)}, f32[2,4,144,128]{3,2,1,0:T(8,128)S(1)}, u32[]{:S(2)}, u32[]{:S(2)}) collective-permute-start(f32[2,4,144,128]{3,2,1,0:T(8,128)S(1)} %shard_map.203), channel_id=1, source_target_pairs={{0,4},{4,0},{8,12},{12,8},{16,20},{20,16},{24,28},{28,24},{32,36},... | collective-permute-start | bytes 1769480 | tf_op jit(solution)/shard_map/ppermute | solution.py:27
  32.4 54.1 %copy-start = (bf16[8,8,2,128,128]{4,3,2,1,0:T(8,128)(2,1)S(1)}, bf16[8,8,2,128,128]{4,3,2,1,0:T(8,128)(2,1)}, u32[]{:S(2)}) copy-start(bf16[8,8,2,128,128]{4,3,2,1,0:T(8,128)(2,1)} %blocks.3) | copy-start | bytes 12582916
  32.4 54.1 %copy-start.3 = (f32[8,8,16,128]{3,2,1,0:T(8,128)S(1)}, f32[8,8,16,128]{3,2,1,0:T(8,128)}, u32[]{:S(2)}) copy-start(f32[8,8,16,128]{3,2,1,0:T(8,128)} %guess.1) | copy-start | bytes 1572868
  32.5 17.0 %collective-permute-start.9 = (bf16[1232,128]{1,0:T(8,128)(2,1)S(1)}, bf16[1232,128]{1,0:T(8,128)(2,1)S(1)}, u32[]{:S(2)}, u32[]{:S(2)}) collective-permute-start(bf16[1232,128]{1,0:T(8,128)(2,1)S(1)} %get-tuple-element.30.third0), channel_id=1, source_target_pairs={{0,3},{1,2},{2,1},{3,0},{4,7},{5,6},{6,5},{7,4},{8,11},{9,10},{10,... | collective-permute-start | bytes 946184 | tf_op jit(solution)/shard_map/ppermute | solution.py:27
  33.6 15.9 %collective-permute-start.8 = (bf16[1232,128]{1,0:T(8,128)(2,1)S(1)}, bf16[1232,128]{1,0:T(8,128)(2,1)S(1)}, u32[]{:S(2)}, u32[]{:S(2)}) collective-permute-start(bf16[1232,128]{1,0:T(8,128)(2,1)S(1)} %get-tuple-element.30.third0), channel_id=1, source_target_pairs={{0,2},{1,3},{2,0},{3,1},{4,6},{5,7},{6,4},{7,5},{8,10},{9,11},{10,... | collective-permute-start | bytes 946184 | tf_op jit(solution)/shard_map/ppermute | solution.py:27
  34.4 15.5 %collective-permute-start.7 = (bf16[1232,128]{1,0:T(8,128)(2,1)S(1)}, bf16[1232,128]{1,0:T(8,128)(2,1)S(1)}, u32[]{:S(2)}, u32[]{:S(2)}) collective-permute-start(bf16[1232,128]{1,0:T(8,128)(2,1)S(1)} %get-tuple-element.30.third0), channel_id=1, source_target_pairs={{0,1},{1,0},{2,3},{3,2},{4,5},{5,4},{6,7},{7,6},{8,9},{9,8},{10,11... | collective-permute-start | bytes 946184 | tf_op jit(solution)/shard_map/ppermute | solution.py:27
  51.9 2.2 %collective-permute-start.10 = (f32[256,128]{1,0:T(8,128)S(1)}, f32[256,128]{1,0:T(8,128)S(1)}, u32[]{:S(2)}, u32[]{:S(2)}) collective-permute-start(f32[256,128]{1,0:T(8,128)S(1)} %get-tuple-element.31), channel_id=1, source_target_pairs={{0,4},{4,0},{8,12},{12,8},{16,20},{20,16},{24,28},{28,24},{32,36},... | collective-permute-start | bytes 393224 | tf_op jit(solution)/shard_map/ppermute | solution.py:27
  54.1 5.9 %collective-permute-start.11 = (f32[2,256,128]{2,1,0:T(8,128)S(1)}, f32[2,256,128]{2,1,0:T(8,128)S(1)}, u32[]{:S(2)}, u32[]{:S(2)}) collective-permute-start(f32[2,256,128]{2,1,0:T(8,128)S(1)} %pad_maximum_fusion.pair), channel_id=1, source_target_pairs={{0,252},{4,8},{8,4},{12,16},{16,12},{20,24},{24,20},{28,32},{32,28... | collective-permute-start | bytes 786440 | tf_op jit(solution)/shard_map/ppermute | solution.py:27
  54.2 9.5 %collective-permute-start.17 = (f32[544,128]{1,0:T(8,128)S(1)}, f32[544,128]{1,0:T(8,128)S(1)}, u32[]{:S(2)}, u32[]{:S(2)}) collective-permute-start(f32[544,128]{1,0:T(8,128)S(1)} %get-tuple-element.36), channel_id=1, source_target_pairs={{0,1},{1,0},{2,3},{3,2},{4,5},{5,4},{6,7},{7,6},{8,9},{9,8},{10,11... | collective-permute-start | bytes 835592 | tf_op jit(solution)/shard_map/ppermute | solution.py:27
  54.3 9.4 %collective-permute-start.18 = (f32[544,128]{1,0:T(8,128)S(1)}, f32[544,128]{1,0:T(8,128)S(1)}, u32[]{:S(2)}, u32[]{:S(2)}) collective-permute-start(f32[544,128]{1,0:T(8,128)S(1)} %get-tuple-element.37), channel_id=1, source_target_pairs={{0,3},{1,2},{2,1},{3,0},{4,7},{5,6},{6,5},{7,4},{8,11},{9,10},{10,... | collective-permute-start | bytes 835592 | tf_op jit(solution)/shard_map/ppermute | solution.py:27
  60.0 5.6 %collective-permute-start.12 = (f32[2,256,128]{2,1,0:T(8,128)S(1)}, f32[2,256,128]{2,1,0:T(8,128)S(1)}, u32[]{:S(2)}, u32[]{:S(2)}) collective-permute-start(f32[2,256,128]{2,1,0:T(8,128)S(1)} %collective-permute-done.11.a), channel_id=1, source_target_pairs={{0,4},{4,0},{8,12},{12,8},{16,20},{20,16},{24,28},{28,24},{32,36},... | collective-permute-start | bytes 786440 | tf_op jit(solution)/shard_map/ppermute | solution.py:27
  63.8 16.2 %collective-permute-start.19 = (f32[1224,128]{1,0:T(8,128)S(1)}, f32[1224,128]{1,0:T(8,128)S(1)}, u32[]{:S(2)}, u32[]{:S(2)}) collective-permute-start(f32[1224,128]{1,0:T(8,128)S(1)} %get-tuple-element.42), channel_id=1, source_target_pairs={{0,4},{4,0},{8,12},{12,8},{16,20},{20,16},{24,28},{28,24},{32,36},... | collective-permute-start | bytes 1880072 | tf_op jit(solution)/shard_map/ppermute | solution.py:27
  65.6 14.5 %collective-permute-start.20 = (f32[1224,128]{1,0:T(8,128)S(1)}, f32[1224,128]{1,0:T(8,128)S(1)}, u32[]{:S(2)}, u32[]{:S(2)}) collective-permute-start(f32[1224,128]{1,0:T(8,128)S(1)} %get-tuple-element.43), channel_id=1, source_target_pairs={{0,252},{4,8},{8,4},{12,16},{16,12},{20,24},{24,20},{28,32},{32,28... | collective-permute-start | bytes 1880072 | tf_op jit(solution)/shard_map/ppermute | solution.py:27
  68.1 5.4 %collective-permute-start.14 = (f32[256,128]{1,0:T(8,128)S(1)}, f32[256,128]{1,0:T(8,128)S(1)}, u32[]{:S(2)}, u32[]{:S(2)}) collective-permute-start(f32[256,128]{1,0:T(8,128)S(1)} %bitcast.9), channel_id=1, source_target_pairs={{0,3},{1,2},{2,1},{3,0},{4,7},{5,6},{6,5},{7,4},{8,11},{9,10},{10,... | collective-permute-start | bytes 393224 | tf_op jit(solution)/shard_map/ppermute | solution.py:27
  70.1 4.1 %collective-permute-start.13 = (f32[256,128]{1,0:T(8,128)S(1)}, f32[256,128]{1,0:T(8,128)S(1)}, u32[]{:S(2)}, u32[]{:S(2)}) collective-permute-start(f32[256,128]{1,0:T(8,128)S(1)} %bitcast.10), channel_id=1, source_target_pairs={{0,1},{1,0},{2,3},{3,2},{4,5},{5,4},{6,7},{7,6},{8,9},{9,8},{10,11... | collective-permute-start | bytes 393224 | tf_op jit(solution)/shard_map/ppermute | solution.py:27
  74.3 7.0 %collective-permute-start.15 = (f32[576,128]{1,0:T(8,128)S(1)}, f32[576,128]{1,0:T(8,128)S(1)}, u32[]{:S(2)}, u32[]{:S(2)}) collective-permute-start(f32[576,128]{1,0:T(8,128)S(1)} %get-tuple-element.33), channel_id=1, source_target_pairs={{0,4},{4,0},{8,12},{12,8},{16,20},{20,16},{24,28},{28,24},{32,36},... | collective-permute-start | bytes 884744 | tf_op jit(solution)/shard_map/ppermute | solution.py:27
  80.1 6.4 %collective-permute-start.16 = (f32[576,128]{1,0:T(8,128)S(1)}, f32[576,128]{1,0:T(8,128)S(1)}, u32[]{:S(2)}, u32[]{:S(2)}) collective-permute-start(f32[576,128]{1,0:T(8,128)S(1)} %get-tuple-element.34), channel_id=1, source_target_pairs={{0,252},{4,8},{8,4},{12,16},{16,12},{20,24},{24,20},{28,32},{32,28... | collective-permute-start | bytes 884744 | tf_op jit(solution)/shard_map/ppermute | solution.py:27
  86.5 21.1 %copy-start.1 = (f32[8,8,16,128]{3,2,1,0:T(8,128)S(1)}, f32[8,8,16,128]{3,2,1,0:T(8,128)}, u32[]{:S(2)}) copy-start(f32[8,8,16,128]{3,2,1,0:T(8,128)} %fown.1) | copy-start | bytes 1572868
  86.5 21.1 %copy-start.4 = (f32[8,8,128]{2,1,0:T(8,128)S(1)}, f32[8,8,128]{2,1,0:T(8,128)}, u32[]{:S(2)}) copy-start(f32[8,8,128]{2,1,0:T(8,128)} %sown.1) | copy-start | bytes 98308
  91.6 4.6 %collective-permute-start.21 = (f32[384,128]{1,0:T(8,128)S(1)}, f32[384,128]{1,0:T(8,128)S(1)}, u32[]{:S(2)}, u32[]{:S(2)}) collective-permute-start(f32[384,128]{1,0:T(8,128)S(1)} %get-tuple-element.45), channel_id=1, source_target_pairs={{0,1},{1,0},{2,3},{3,2},{4,5},{5,4},{6,7},{7,6},{8,9},{9,8},{10,11... | collective-permute-start | bytes 589832 | tf_op jit(solution)/shard_map/ppermute | solution.py:27
  91.7 5.8 %collective-permute-start.22 = (f32[384,128]{1,0:T(8,128)S(1)}, f32[384,128]{1,0:T(8,128)S(1)}, u32[]{:S(2)}, u32[]{:S(2)}) collective-permute-start(f32[384,128]{1,0:T(8,128)S(1)} %get-tuple-element.46), channel_id=1, source_target_pairs={{0,3},{1,2},{2,1},{3,0},{4,7},{5,6},{6,5},{7,4},{8,11},{9,10},{10,... | collective-permute-start | bytes 589832 | tf_op jit(solution)/shard_map/ppermute | solution.py:27
  97.6 6.2 %collective-permute-start.23 = (f32[480,128]{1,0:T(8,128)S(1)}, f32[480,128]{1,0:T(8,128)S(1)}, u32[]{:S(2)}, u32[]{:S(2)}) collective-permute-start(f32[480,128]{1,0:T(8,128)S(1)} %get-tuple-element.47), channel_id=1, source_target_pairs={{0,4},{4,0},{8,12},{12,8},{16,20},{20,16},{24,28},{28,24},{32,36},... | collective-permute-start | bytes 737288 | tf_op jit(solution)/shard_map/ppermute | solution.py:27
  101.9 5.6 %collective-permute-start.24 = (f32[480,128]{1,0:T(8,128)S(1)}, f32[480,128]{1,0:T(8,128)S(1)}, u32[]{:S(2)}, u32[]{:S(2)}) collective-permute-start(f32[480,128]{1,0:T(8,128)S(1)} %get-tuple-element.48), channel_id=1, source_target_pairs={{0,252},{4,8},{8,4},{12,16},{16,12},{20,24},{24,20},{28,32},{32,28... | collective-permute-start | bytes 737288 | tf_op jit(solution)/shard_map/ppermute | solution.py:27
